TPU v7x, 32 devices: a whole 2x2x4 slice. The times are simulated.
32 devices in a mesh: dp: 8 (over z, core), tensor: 4 (over y, x).
Axes of the slice: x: 2, y: 2, z: 4, core: 2. Of those that a mesh axis runs over, the one named last changes fastest.
Arguments:
- block_input: bfloat16 [8192, 2048], P(('dp', 'tensor')), may hold values from -6 to 6
- attn_gain: float32 [2048], replicated, may hold values from 0.5 to 1.5
- w_query: bfloat16 [2048, 2048], P('dp', 'tensor'), may hold values from -6 to 6
- w_key: bfloat16 [2048, 512], P('dp', 'tensor'), may hold values from -0.125 to 0.125
- w_value: bfloat16 [2048, 512], P('dp', 'tensor'), may hold values from -0.125 to 0.125
- w_out: bfloat16 [2048, 2048], P('dp', 'tensor'), may hold values from -0.5 to 0.5
- mlp_gain: float32 [2048], replicated, may hold values from 0.5 to 1.5
- w_gate: bfloat16 [2048, 8192], P('dp', 'tensor'), may hold values from -0.125 to 0.125
- w_up: bfloat16 [2048, 8192], P('dp', 'tensor'), may hold values from -0.125 to 0.125
- w_down: bfloat16 [2048, 8192], P('dp', 'tensor'), may hold values from -0.0625 to 0.0625
- doc_ids: int32 [8192], P('dp'), may hold values from -1 to 3, as said below
- cotangent: bfloat16 [8192, 2048], P(('dp', 'tensor')), may hold values from -6 to 6
Outputs:
- block_output: bfloat16 [8192, 2048], P(('dp', 'tensor'))
- input_grad: bfloat16 [8192, 2048], P(('dp', 'tensor'))
- grad_query: float32 [2048, 2048], P('dp', 'tensor')
- grad_key: float32 [2048, 512], P('dp', 'tensor')
- grad_value: float32 [2048, 512], P('dp', 'tensor')
- grad_out: float32 [2048, 2048], P('dp', 'tensor')
- grad_gate: float32 [2048, 8192], P('dp', 'tensor')
- grad_up: float32 [2048, 8192], P('dp', 'tensor')
- grad_down: float32 [2048, 8192], P('dp', 'tensor')
- grad_attn_gain: float32 [2048], replicated
- grad_mlp_gain: float32 [2048], replicated
Inputs may be any that keep to these rules, and one draw needn't show every extreme that they name: `doc_ids`: within each aligned block of 512 positions the ids of live positions never fall; -1 marks padding, which only ends a block; a block whose first position is -1 is padding throughout; every block ends with padding; a live block has at least 256 live positions; some index of dp has all its 2 blocks live, others may have fewer.
All inputs are finite; a program needn't handle non-finite values.
Results may differ from a plain program's by a relative error of at most 0.014.
The roundings to bfloat16 on the way count: a program that leaves them out, or rounds other values in their place, can miss the bound.
Values may be sent and summed in bfloat16 or wider, within the bound.
A program may use at most 256 MiB of HBM per device.

v0:
```python
import jax
import jax.numpy as jnp
from jax import lax
from jax.sharding import PartitionSpec as P

HD = 64
SEQ = 512


EPSILON = 1e-05
ROPE_BASE = 500000.0
NEG_LARGE = -1e30


def rotary_tables(length, head_dim):
    half_dim = head_dim // 2
    frequency = ROPE_BASE ** (-(jnp.arange(half_dim, dtype=jnp.float32) * (2.0 / head_dim)))
    angles = jnp.arange(length, dtype=jnp.float32)[:, None] * frequency[None, :]
    angles = jnp.concatenate([angles, angles], axis=1)
    return (jnp.cos(angles), jnp.sin(angles))


def rotate_half(tensor_rows):
    half_dim = tensor_rows.shape[-1] // 2
    return jnp.concatenate([-tensor_rows[..., half_dim:], tensor_rows[..., :half_dim]], axis=-1)


def rotate_back(tensor_rows):
    half_dim = tensor_rows.shape[-1] // 2
    return jnp.concatenate([tensor_rows[..., half_dim:], -tensor_rows[..., :half_dim]], axis=-1)


def apply_rotary(tensor_rows, cosine_table, sine_table):
    return (
        tensor_rows * cosine_table[:, None, :] + rotate_half(tensor_rows) * sine_table[:, None, :]
    )


def undo_rotary(tensor_rows, cosine_table, sine_table):
    return tensor_rows * cosine_table[:, None, :] + rotate_back(
        tensor_rows * sine_table[:, None, :]
    )


def norm_scale(tensor_rows):
    return lax.rsqrt(jnp.mean(tensor_rows * tensor_rows, axis=1, keepdims=True) + EPSILON)


def norm_back(grad_normed, tensor_rows, row_scale, gain_row):
    weighted = grad_normed * gain_row[None, :]
    inner_mean = jnp.mean(weighted * tensor_rows, axis=1, keepdims=True)
    return row_scale * weighted - tensor_rows * (row_scale * row_scale * row_scale) * inner_mean


def slot_mask(doc_rows):
    positions = jnp.arange(doc_rows.shape[0])
    earlier = positions[None, :] <= positions[:, None]
    same_doc = (doc_rows[:, None] == doc_rows[None, :]) & (doc_rows[:, None] >= 0)
    return same_doc & earlier | (positions[None, :] == positions[:, None])


def contract_rows(left_side, right_side):
    return lax.dot_general(
        left_side, right_side, (((0,), (0,)), ((), ())), preferred_element_type=jnp.float32
    )


def contract_cols(left_side, right_side):
    return lax.dot_general(
        left_side, right_side, (((1,), (1,)), ((), ())), preferred_element_type=jnp.float32
    )


def slot_scores(query_rows, key_rows, allowed):
    seq_len, head_count, head_dim = query_rows.shape
    groups = key_rows.shape[1]
    grouped = query_rows.reshape(seq_len, groups, head_count // groups, head_dim)
    scores = jnp.einsum(
        "sgjd,tgd->gjst", grouped, key_rows, preferred_element_type=jnp.float32
    ) * head_dim ** (-0.5)
    return (grouped, jnp.where(allowed[None, None], scores, NEG_LARGE))


def attend(packed):
    query_rows, key_rows, value_rows, doc_rows = packed
    seq_len, head_count, head_dim = query_rows.shape
    allowed = slot_mask(doc_rows)
    live_rows = (doc_rows >= 0).astype(jnp.float32)
    grouped, scores = slot_scores(query_rows, key_rows, allowed)
    row_max = jnp.max(scores, axis=-1, keepdims=True)
    weights = jnp.exp(scores - row_max)
    row_total = jnp.sum(weights, axis=-1, keepdims=True)
    prob_bf = (weights / row_total).astype(jnp.bfloat16)
    mixed_rows = jnp.einsum(
        "gjst,tgd->sgjd", prob_bf, value_rows, preferred_element_type=jnp.float32
    )
    mixed_rows = mixed_rows.reshape(seq_len, head_count * head_dim) * live_rows[:, None]
    return (mixed_rows.astype(jnp.bfloat16), row_max + jnp.log(row_total))


def attend_back(packed):
    query_rows, key_rows, value_rows, doc_rows, log_total, grad_mixed = packed
    seq_len, head_count, head_dim = query_rows.shape
    groups = key_rows.shape[1]
    allowed = slot_mask(doc_rows)
    grouped, scores = slot_scores(query_rows, key_rows, allowed)
    prob_full = jnp.where(allowed[None, None], jnp.exp(scores - log_total), 0.0)
    grad_rows = grad_mixed.reshape(seq_len, groups, head_count // groups, head_dim)
    grad_prob = jnp.einsum(
        "sgjd,tgd->gjst", grad_rows, value_rows, preferred_element_type=jnp.float32
    )
    row_delta = jnp.sum(prob_full * grad_prob, axis=-1, keepdims=True)
    grad_scores = (prob_full * (grad_prob - row_delta)).astype(jnp.bfloat16)
    grad_values = jnp.einsum(
        "gjst,sgjd->tgd",
        prob_full.astype(jnp.bfloat16),
        grad_rows,
        preferred_element_type=jnp.float32,
    )
    grad_queries = jnp.einsum(
        "gjst,tgd->sgjd", grad_scores, key_rows, preferred_element_type=jnp.float32
    ) * head_dim ** (-0.5)
    grad_keys = jnp.einsum(
        "gjst,sgjd->tgd", grad_scores, grouped, preferred_element_type=jnp.float32
    ) * head_dim ** (-0.5)
    return (grad_queries.reshape(seq_len, head_count, head_dim), grad_keys, grad_values)


def per_device(
    block_input,
    attn_gain,
    w_query,
    w_key,
    w_value,
    w_out,
    mlp_gain,
    w_gate,
    w_up,
    w_down,
    doc_ids,
    cotangent,
):
    query_full, key_full, value_full, out_full, gate_full, up_full, down_full = (
        lax.all_gather(w_query, "dp", axis=0, tiled=True),
        lax.all_gather(w_key, "dp", axis=0, tiled=True),
        lax.all_gather(w_value, "dp", axis=0, tiled=True),
        lax.all_gather(w_out, "dp", axis=0, tiled=True),
        lax.all_gather(w_gate, "dp", axis=0, tiled=True),
        lax.all_gather(w_up, "dp", axis=0, tiled=True),
        lax.all_gather(w_down, "dp", axis=0, tiled=True),
    )
    total_rows = doc_ids.shape[0]
    slot_count = total_rows // SEQ
    local_heads = query_full.shape[1] // HD
    local_groups = key_full.shape[1] // HD
    cosine_table, sine_table = rotary_tables(SEQ, HD)
    live_all = (doc_ids >= 0).astype(jnp.float32)
    input_own = block_input.astype(jnp.float32)
    scale_one = norm_scale(input_own)
    normed_one = lax.all_gather(
        (input_own * scale_one * attn_gain[None, :]).astype(jnp.bfloat16),
        "tensor",
        axis=0,
        tiled=True,
    )
    query_pre = jnp.dot(normed_one, query_full, preferred_element_type=jnp.float32).reshape(
        slot_count, SEQ, local_heads, HD
    )
    key_pre = jnp.dot(normed_one, key_full, preferred_element_type=jnp.float32).reshape(
        slot_count, SEQ, local_groups, HD
    )
    query_rows = apply_rotary(query_pre, cosine_table, sine_table).astype(jnp.bfloat16)
    key_rows = apply_rotary(key_pre, cosine_table, sine_table).astype(jnp.bfloat16)
    value_rows = (
        jnp.dot(normed_one, value_full, preferred_element_type=jnp.float32)
        .astype(jnp.bfloat16)
        .reshape(slot_count, SEQ, local_groups, HD)
    )
    doc_slots = doc_ids.reshape(slot_count, SEQ)
    mixed_slots, log_total = lax.map(attend, (query_rows, key_rows, value_rows, doc_slots))
    mixed_all = mixed_slots.reshape(total_rows, local_heads * HD)
    residual_own = input_own + lax.psum_scatter(
        contract_cols(mixed_all, out_full), "tensor", scatter_dimension=0, tiled=True
    )
    scale_two_own = norm_scale(residual_own)
    normed_two = lax.all_gather(
        (residual_own * scale_two_own * mlp_gain[None, :]).astype(jnp.bfloat16),
        "tensor",
        axis=0,
        tiled=True,
    )
    gate_pre = jnp.dot(normed_two, gate_full, preferred_element_type=jnp.float32)
    up_pre = jnp.dot(normed_two, up_full, preferred_element_type=jnp.float32)
    sigmoid_gate = jax.nn.sigmoid(gate_pre)
    silu_gate = gate_pre * sigmoid_gate
    hidden = (silu_gate * up_pre).astype(jnp.bfloat16)
    block_output = (
        residual_own
        + lax.psum_scatter(
            contract_cols(hidden, down_full), "tensor", scatter_dimension=0, tiled=True
        )
    ).astype(jnp.bfloat16)
    grad_full = lax.all_gather(cotangent, "tensor", axis=0, tiled=True)
    grad_hidden = jnp.dot(grad_full, down_full, preferred_element_type=jnp.float32)
    grad_down = contract_rows(grad_full, hidden)
    grad_gate_pre = (
        grad_hidden * up_pre * sigmoid_gate * (1.0 + gate_pre * (1.0 - sigmoid_gate))
    ).astype(jnp.bfloat16)
    grad_up_pre = (grad_hidden * silu_gate).astype(jnp.bfloat16)
    grad_gate = contract_rows(normed_two, grad_gate_pre)
    grad_up = contract_rows(normed_two, grad_up_pre)
    grad_normed_own = lax.psum_scatter(
        contract_cols(grad_gate_pre, gate_full) + contract_cols(grad_up_pre, up_full),
        "tensor",
        scatter_dimension=0,
        tiled=True,
    )
    grad_mlp_gain = jnp.sum(grad_normed_own * residual_own * scale_two_own, axis=0)
    grad_residual_own = cotangent.astype(jnp.float32) + norm_back(
        grad_normed_own, residual_own, scale_two_own, mlp_gain
    )
    grad_residual_bf = lax.all_gather(
        grad_residual_own.astype(jnp.bfloat16), "tensor", axis=0, tiled=True
    )
    grad_out = contract_rows(grad_residual_bf, mixed_all)
    grad_mixed = (
        jnp.dot(grad_residual_bf, out_full, preferred_element_type=jnp.float32) * live_all[:, None]
    ).astype(jnp.bfloat16)
    grad_mixed_slots = grad_mixed.reshape(slot_count, SEQ, local_heads * HD)
    grad_queries, grad_keys, grad_values = lax.map(
        attend_back, (query_rows, key_rows, value_rows, doc_slots, log_total, grad_mixed_slots)
    )
    grad_query_rows = (
        undo_rotary(grad_queries, cosine_table, sine_table)
        .astype(jnp.bfloat16)
        .reshape(total_rows, local_heads * HD)
    )
    grad_key_rows = (
        undo_rotary(grad_keys, cosine_table, sine_table)
        .astype(jnp.bfloat16)
        .reshape(total_rows, local_groups * HD)
    )
    grad_value_rows = grad_values.astype(jnp.bfloat16).reshape(total_rows, local_groups * HD)
    grad_query = contract_rows(normed_one, grad_query_rows)
    grad_key = contract_rows(normed_one, grad_key_rows)
    grad_value = contract_rows(normed_one, grad_value_rows)
    grad_normed_one = lax.psum_scatter(
        contract_cols(grad_query_rows, query_full)
        + contract_cols(grad_key_rows, key_full)
        + contract_cols(grad_value_rows, value_full),
        "tensor",
        scatter_dimension=0,
        tiled=True,
    )
    grad_attn_gain = jnp.sum(grad_normed_one * input_own * scale_one, axis=0)
    input_grad = (
        grad_residual_own + norm_back(grad_normed_one, input_own, scale_one, attn_gain)
    ).astype(jnp.bfloat16)
    summed = (
        lax.psum_scatter(grad_query, "dp", scatter_dimension=0, tiled=True),
        lax.psum_scatter(grad_key, "dp", scatter_dimension=0, tiled=True),
        lax.psum_scatter(grad_value, "dp", scatter_dimension=0, tiled=True),
        lax.psum_scatter(grad_out, "dp", scatter_dimension=0, tiled=True),
        lax.psum_scatter(grad_gate, "dp", scatter_dimension=0, tiled=True),
        lax.psum_scatter(grad_up, "dp", scatter_dimension=0, tiled=True),
        lax.psum_scatter(grad_down, "dp", scatter_dimension=0, tiled=True),
    )
    gains = lax.psum((grad_attn_gain, grad_mlp_gain), ("dp", "tensor"))
    return (
        block_output,
        input_grad,
        summed[0],
        summed[1],
        summed[2],
        summed[3],
        summed[4],
        summed[5],
        summed[6],
        gains[0],
        gains[1],
    )


def solution(mesh):
    in_specs = (
        P(("dp", "tensor"), None),
        P(),
        P("dp", "tensor"),
        P("dp", "tensor"),
        P("dp", "tensor"),
        P("dp", "tensor"),
        P(),
        P("dp", "tensor"),
        P("dp", "tensor"),
        P("dp", "tensor"),
        P("dp"),
        P(("dp", "tensor"), None),
    )
    out_specs = (
        P(("dp", "tensor"), None),
        P(("dp", "tensor"), None),
        P("dp", "tensor"),
        P("dp", "tensor"),
        P("dp", "tensor"),
        P("dp", "tensor"),
        P("dp", "tensor"),
        P("dp", "tensor"),
        P("dp", "tensor"),
        P(),
        P(),
    )
    return jax.shard_map(
        per_device, mesh=mesh, in_specs=in_specs, out_specs=out_specs, check_vma=False
    )
```

profile of v0, /device:TPU:0, one launch (start us, length us, event | category | flops | bytes accessed | tf_op | source)
XLA Modules:
  0.0 1646.8 jit_solution(966707774895748177)
XLA Ops:
  13.8 18.7 %all_gather.35 = bf16[2048,128]{1,0:T(8,128)(2,1)S(1)} all-gather(bf16[256,128]{1,0:T(8,128)(2,1)S(1)} %copy-done.29), channel_id=1, replica_groups=mesh['dp'=8,'tensor'=4] {'dp'}, dimensions={0}, use_global_device_ids=true | all-gather | bytes 589824 | tf_op jit(solution)/shard_map/all_gather | solution.py:145
  32.5 17.6 %all_gather.34 = bf16[2048,128]{1,0:T(8,128)(2,1)S(1)} all-gather(bf16[256,128]{1,0:T(8,128)(2,1)S(1)} %copy-done.30), channel_id=1, replica_groups=mesh['dp'=8,'tensor'=4] {'dp'}, dimensions={0}, use_global_device_ids=true | all-gather | bytes 589824 | tf_op jit(solution)/shard_map/all_gather | solution.py:146
  50.1 52.1 %all-gather.10.cloned.1.call-done = bf16[1024,2048]{1,0:T(8,128)(2,1)} async-done(((bf16[256,2048]{1,0:T(8,128)(2,1)}), bf16[1024,2048]{1,0:T(8,128)(2,1)}) %all-gather.10.cloned.1.call-update) | async-done | bytes 4194320 | tf_op jit(solution)/shard_map/all_gather | solution.py:160
  121.7 14.8 while.26
  145.4 85.9 %reduce-scatter.12.cloned.1.call-done = f32[256,2048]{1,0:T(8,128)} async-done(((f32[1024,2048]{1,0:T(8,128)}), f32[256,2048]{1,0:T(8,128)}) %reduce-scatter.12.cloned.1.call-update) | async-done | bytes 2097168 | tf_op jit(solution)/shard_map/reduce_scatter | solution.py:182
  236.8 78.0 %all-gather.18.cloned.1.call-done = bf16[2048,2048]{1,0:T(8,128)(2,1)} async-done(((bf16[256,2048]{1,0:T(8,128)(2,1)}), bf16[2048,2048]{1,0:T(8,128)(2,1)}) %all-gather.18.cloned.1.call-update) | async-done | bytes 8388624 | tf_op jit(solution)/shard_map/all_gather | solution.py:148
  314.8 53.4 %all-gather.16.cloned.1.call-done = bf16[1024,2048]{1,0:T(8,128)(2,1)} async-done(((bf16[256,2048]{1,0:T(8,128)(2,1)}), bf16[1024,2048]{1,0:T(8,128)(2,1)}) %all-gather.16.cloned.1.call-update) | async-done | bytes 4194320 | tf_op jit(solution)/shard_map/all_gather | solution.py:186
  368.2 14.8 fusion.68
  383.0 68.9 %all-gather.20.cloned.1.call-done = bf16[2048,2048]{1,0:T(8,128)(2,1)} async-done(((bf16[256,2048]{1,0:T(8,128)(2,1)}), bf16[2048,2048]{1,0:T(8,128)(2,1)}) %all-gather.20.cloned.1.call-update) | async-done | bytes 8388624 | tf_op jit(solution)/shard_map/all_gather | solution.py:149
  451.9 14.4 fusion.69
  466.3 38.5 %all-gather.24.cloned.1.call-done = bf16[1024,2048]{1,0:T(8,128)(2,1)} async-done(((bf16[256,2048]{1,0:T(8,128)(2,1)}), bf16[1024,2048]{1,0:T(8,128)(2,1)}) %all-gather.24.cloned.1.call-update) | async-done | bytes 4194320 | tf_op jit(solution)/shard_map/all_gather | solution.py:203
  504.8 83.7 %all-gather.22.cloned.1.call-done = bf16[2048,2048]{1,0:T(8,128)(2,1)} async-done(((bf16[256,2048]{1,0:T(8,128)(2,1)}), bf16[2048,2048]{1,0:T(8,128)(2,1)}) %all-gather.22.cloned.1.call-update) | async-done | bytes 8388624 | tf_op jit(solution)/shard_map/all_gather | solution.py:150
  588.5 21.1 %multiply_convert_fusion.1 = (bf16[1024,2048]{1,0:T(8,128)(2,1)S(1)}, bf16[1024,2048]{1,0:T(8,128)(2,1)}, bf16[1024,2048]{1,0:T(8,128)(2,1)}) fusion(f32[1024,2048]{1,0:T(8,128)} %fusion.68, f32[1024,2048]{1,0:T(8,128)} %fusion.69, bf16[1024,2048]{1,0:T(8,128)(2,1)} %all-gather.24.cloned.1.call-done, bf16[2048,2048]{1,0:T(8,128)(2,1)} %all-gather.22.cloned.1.call-done), kind=kOutput, calls=%fused_computation.63 | convolution fusion | flops 8621391872 | bytes 41943040 | tf_op jit(solution)/shard_map/dot_general | solution.py:204
  609.6 16.2 fusion.71
  625.8 13.0 convolution_add_fusion
  638.9 14.5 fusion.70
  653.5 70.3 %reduce-scatter.16.cloned.1.call-done = f32[256,2048]{1,0:T(8,128)} async-done(((f32[1024,2048]{1,0:T(8,128)}), f32[256,2048]{1,0:T(8,128)}) %reduce-scatter.16.cloned.1.call-update) | async-done | bytes 2097168 | tf_op jit(solution)/shard_map/reduce_scatter | solution.py:212
  726.6 86.7 %reduce-scatter.14.cloned.1.call-done = f32[256,2048]{1,0:T(8,128)} async-done(((f32[1024,2048]{1,0:T(8,128)}), f32[256,2048]{1,0:T(8,128)}) %reduce-scatter.14.cloned.1.call-update) | async-done | bytes 2097168 | tf_op jit(solution)/shard_map/reduce_scatter | solution.py:199
  818.3 15.6 convolution_bitcast_fusion.1
  834.6 36.4 %all-gather.26.cloned.1.call-done = bf16[1024,2048]{1,0:T(8,128)(2,1)} async-done(((bf16[256,2048]{1,0:T(8,128)(2,1)}), bf16[1024,2048]{1,0:T(8,128)(2,1)}) %all-gather.26.cloned.1.call-update) | async-done | bytes 4194320 | tf_op jit(solution)/shard_map/all_gather | solution.py:222
  876.5 109.4 %while.27 = (s32[]{:T(128)}, f32[2,512,8,64]{1,0,3,2:T(2,128)}, f32[2,512,2,64]{1,0,3,2:T(2,128)}, bf16[2,512,2,64]{1,3,2,0:T(8,128)(2,1)}, bf16[2,512,2,64]{1,3...) while((s32[]{:T(128)}, f32[2,512,8,64]{1,0,3,2:T(2,128)}, ...), condition=%wide.region_12.13_spmd, body=%wide.region_10.12_spmd.sunk | while | flops 1365045760 | bytes 130509056 | solution.py:230
  899.4 19.7 %dynamic_update_slice.30 = f32[2,512,8,64]{1,0,3,2:T(2,128)} dynamic-update-slice(f32[2,512,8,64]{1,0,3,2:T(2,128)} %get-tuple-element.385, f32[1,512,8,64]{1,0,3,2:T(1,128)S(1)} %copy.94, s32[]{:T(128)} %get-tuple-element.384, s32[]{:T(128)} %constant.45.clone.1..sunk, s32[]{:T(128)} %constant.45.clone.1..sunk, s32[]{:T(128)} %constant.45.clone.1..sunk) | dynamic-update-slice | bytes 2097156 | tf_op jit(solution)/shard_map/while/body/jit(dynamic_update_index_in_dim)/dynamic_update_slice | solution.py:230
  954.0 19.7 %dynamic_update_slice.30 = f32[2,512,8,64]{1,0,3,2:T(2,128)} dynamic-update-slice(f32[2,512,8,64]{1,0,3,2:T(2,128)} %get-tuple-element.385, f32[1,512,8,64]{1,0,3,2:T(1,128)S(1)} %copy.94, s32[]{:T(128)} %get-tuple-element.384, s32[]{:T(128)} %constant.45.clone.1..sunk, s32[]{:T(128)} %constant.45.clone.1..sunk, s32[]{:T(128)} %constant.45.clone.1..sunk) | dynamic-update-slice | bytes 2097156 | tf_op jit(solution)/shard_map/while/body/jit(dynamic_update_index_in_dim)/dynamic_update_slice | solution.py:230
  1024.5 15.2 fusion.78
  1040.0 15.3 fusion.79
  1058.6 70.7 %reduce-scatter.18.cloned.1.call-done = f32[256,2048]{1,0:T(8,128)} async-done(((f32[1024,2048]{1,0:T(8,128)}), f32[256,2048]{1,0:T(8,128)}) %reduce-scatter.18.cloned.1.call-update) | async-done | bytes 2097168 | tf_op jit(solution)/shard_map/reduce_scatter | solution.py:247
  1131.6 39.7 %all-reduce = (f32[2048]{0:T(1024)}, f32[2048]{0:T(1024)}) all-reduce(f32[2048]{0:T(1024)S(1)} %get-tuple-element.166, f32[2048]{0:T(1024)S(1)} %copy-done.31), channel_id=1, replica_groups=mesh['dp'=8,'tensor'=4] {'dp','tensor'}, use_global_device_ids=true, to_apply=%region_23.24 | all-reduce | flops 4096 | bytes 32768 | tf_op jit(solution)/shard_map/psum | solution.py:268
  1174.5 23.9 %reduce-scatter.24.cloned.1.call-done = f32[256,128]{1,0:T(8,128)} async-done(((f32[2048,128]{1,0:T(8,128)}), f32[256,128]{1,0:T(8,128)}) %reduce-scatter.24.cloned.1.call-update) | async-done | bytes 131088 | tf_op jit(solution)/shard_map/reduce_scatter | solution.py:262
  1198.4 50.9 %reduce-scatter.26.cloned.1.call-done = f32[256,512]{1,0:T(8,128)} async-done(((f32[2048,512]{1,0:T(8,128)}), f32[256,512]{1,0:T(8,128)}) %reduce-scatter.26.cloned.1.call-update) | async-done | bytes 524304 | tf_op jit(solution)/shard_map/reduce_scatter | solution.py:263
  1249.3 51.1 %reduce-scatter.20.cloned.1.call-done = f32[256,512]{1,0:T(8,128)} async-done(((f32[2048,512]{1,0:T(8,128)}), f32[256,512]{1,0:T(8,128)}) %reduce-scatter.20.cloned.1.call-update) | async-done | bytes 524304 | tf_op jit(solution)/shard_map/reduce_scatter | solution.py:260
  1300.4 169.6 %reduce-scatter.28.cloned.1.call-done = f32[256,2048]{1,0:T(8,128)} async-done(((f32[2048,2048]{1,0:T(8,128)}), f32[256,2048]{1,0:T(8,128)}) %reduce-scatter.28.cloned.1.call-update) | async-done | bytes 2097168 | tf_op jit(solution)/shard_map/reduce_scatter | solution.py:264
  1470.0 169.4 %reduce-scatter.30.cloned.1.call-done = f32[256,2048]{1,0:T(8,128)} async-done(((f32[2048,2048]{1,0:T(8,128)}), f32[256,2048]{1,0:T(8,128)}) %reduce-scatter.30.cloned.1.call-update) | async-done | bytes 2097168 | tf_op jit(solution)/shard_map/reduce_scatter | solution.py:265
  (245 shorter events, 185.6 us)
Async XLA Ops:
  7.2 42.9 %all-gather.12.cloned.1.call-start = ((), (), s32[]{:S(2)}) async-start(), calls=%async_computation.12 | async-start | bytes 2359296 | tf_op jit(solution)/shard_map/all_gather | solution.py:144
  7.9 94.3 %all-gather.10.cloned.1.call-start = ((), (), s32[]{:S(2)}) async-start(), calls=%async_computation.11 | async-start | bytes 5242880 | tf_op jit(solution)/shard_map/all_gather | solution.py:160
  10.1 92.1 %copy-start.32 = (f32[256]{0:T(256)}, f32[256]{0:T(256)S(1)}, u32[]{:S(2)}) copy-start(f32[256]{0:T(256)S(1)} %get-tuple-element.229) | copy-start | bytes 3076
  12.6 124.0 %all-gather.14.cloned.1.call-start = ((), (), s32[]{:S(2)}) async-start(), calls=%async_computation.13 | async-start | bytes 2359296 | tf_op jit(solution)/shard_map/all_gather | solution.py:147
  13.4 217.9 %reduce-scatter.12.cloned.1.call-start = ((), (), s32[]{:S(2)}) async-start(), calls=%async_computation.14 | async-start | bytes 10485760 | tf_op jit(solution)/shard_map/reduce_scatter | solution.py:182
  13.8 103.3 %copy-start.13 = (f32[512,64]{0,1:T(8,128)}, f32[512,64]{0,1:T(8,128)S(1)}, u32[]{:S(2)}) copy-start(f32[512,64]{0,1:T(8,128)S(1)} %get-tuple-element.227) | copy-start | bytes 393220
  13.8 103.3 %copy-start.15 = (f32[512,64]{0,1:T(8,128)}, f32[512,64]{0,1:T(8,128)S(1)}, u32[]{:S(2)}) copy-start(f32[512,64]{0,1:T(8,128)S(1)} %get-tuple-element.226) | copy-start | bytes 393220
  32.5 82.0 %copy-start.10 = (bf16[2048,128]{1,0:T(8,128)(2,1)}, bf16[2048,128]{1,0:T(8,128)(2,1)S(1)}, u32[]{:S(2)}) copy-start(bf16[2048,128]{1,0:T(8,128)(2,1)S(1)} %all_gather.35) | copy-start | bytes 1572868
  144.7 86.6 %copy-start.4 = (bf16[256,2048]{1,0:T(8,128)(2,1)S(1)}, bf16[256,2048]{1,0:T(8,128)(2,1)}, u32[]{:S(2)}) copy-start(bf16[256,2048]{1,0:T(8,128)(2,1)} %param.16) | copy-start | bytes 3145732
  144.8 88.5 %copy-start.28 = (f32[2048]{0:T(1024)S(1)}, f32[2048]{0:T(1024)}, u32[]{:S(2)}) copy-start(f32[2048]{0:T(1024)} %param.22) | copy-start | bytes 24580
  144.8 170.0 %all-gather.18.cloned.1.call-start = ((), (), s32[]{:S(2)}) async-start(), calls=%async_computation.16 | async-start | bytes 9437184 | tf_op jit(solution)/shard_map/all_gather | solution.py:148
  145.4 222.8 %all-gather.16.cloned.1.call-start = ((), (), s32[]{:S(2)}) async-start(), calls=%async_computation.15 | async-start | bytes 5242880 | tf_op jit(solution)/shard_map/all_gather | solution.py:186
  234.5 217.4 %all-gather.20.cloned.1.call-start = ((), (), s32[]{:S(2)}) async-start(), calls=%async_computation.17 | async-start | bytes 9437184 | tf_op jit(solution)/shard_map/all_gather | solution.py:149
  235.3 269.5 %all-gather.24.cloned.1.call-start = ((), (), s32[]{:S(2)}) async-start(), calls=%async_computation.20 | async-start | bytes 5242880 | tf_op jit(solution)/shard_map/all_gather | solution.py:203
  236.0 352.5 %all-gather.22.cloned.1.call-start = ((), (), s32[]{:S(2)}) async-start(), calls=%async_computation.18 | async-start | bytes 9437184 | tf_op jit(solution)/shard_map/all_gather | solution.py:150
  236.7 487.1 %reduce-scatter.16.cloned.1.call-start = ((), (), s32[]{:S(2)}) async-start(), calls=%async_computation.21 | async-start | bytes 10485760 | tf_op jit(solution)/shard_map/reduce_scatter | solution.py:212
  638.9 174.4 %reduce-scatter.14.cloned.1.call-start = ((), (), s32[]{:S(2)}) async-start(), calls=%async_computation.19 | async-start | bytes 10485760 | tf_op jit(solution)/shard_map/reduce_scatter | solution.py:199
  653.5 159.8 %copy-start.12 = (bf16[256,2048]{1,0:T(8,128)(2,1)S(1)}, bf16[256,2048]{1,0:T(8,128)(2,1)}, u32[]{:S(2)}) copy-start(bf16[256,2048]{1,0:T(8,128)(2,1)} %param.27) | copy-start | bytes 3145732
  653.5 217.5 %all-gather.26.cloned.1.call-start = ((), (), s32[]{:S(2)}) async-start(), calls=%async_computation.22 | async-start | bytes 5242880 | tf_op jit(solution)/shard_map/all_gather | solution.py:222
  818.2 237.2 %reduce-scatter.32.cloned.1.call-start = ((), (), s32[]{:S(2)}) async-start(), calls=%async_computation.30 | async-start | bytes 18874368 | tf_op jit(solution)/shard_map/reduce_scatter | solution.py:266
  833.9 295.3 %reduce-scatter.18.cloned.1.call-start = ((), (), s32[]{:S(2)}) async-start(), calls=%async_computation.23 | async-start | bytes 10485760 | tf_op jit(solution)/shard_map/reduce_scatter | solution.py:247
  876.5 109.4 %copy-start.14 = (f32[512,64]{0,1:T(8,128)S(1)}, f32[512,64]{0,1:T(8,128)}, u32[]{:S(2)}) copy-start(f32[512,64]{0,1:T(8,128)} %copy-done.13) | copy-start | bytes 393220
  1001.6 172.9 %reduce-scatter.22.cloned.1.call-start = ((), (), s32[]{:S(2)}) async-start(), calls=%async_computation.25 | async-start | bytes 1179648 | tf_op jit(solution)/shard_map/reduce_scatter | solution.py:261
  1006.2 192.2 %reduce-scatter.24.cloned.1.call-start = ((), (), s32[]{:S(2)}) async-start(), calls=%async_computation.26 | async-start | bytes 1179648 | tf_op jit(solution)/shard_map/reduce_scatter | solution.py:262
  1010.9 238.4 %reduce-scatter.26.cloned.1.call-start = ((), (), s32[]{:S(2)}) async-start(), calls=%async_computation.27 | async-start | bytes 4718592 | tf_op jit(solution)/shard_map/reduce_scatter | solution.py:263
  1017.7 282.7 %reduce-scatter.20.cloned.1.call-start = ((), (), s32[]{:S(2)}) async-start(), calls=%async_computation.24 | async-start | bytes 4718592 | tf_op jit(solution)/shard_map/reduce_scatter | solution.py:260
  1024.5 445.6 %reduce-scatter.28.cloned.1.call-start = ((), (), s32[]{:S(2)}) async-start(), calls=%async_computation.28 | async-start | bytes 18874368 | tf_op jit(solution)/shard_map/reduce_scatter | solution.py:264
  1039.7 599.7 %reduce-scatter.30.cloned.1.call-start = ((), (), s32[]{:S(2)}) async-start(), calls=%async_computation.29 | async-start | bytes 18874368 | tf_op jit(solution)/shard_map/reduce_scatter | solution.py:265
  1055.3 73.9 %copy-start.5 = (bf16[256,2048]{1,0:T(8,128)(2,1)S(1)}, bf16[256,2048]{1,0:T(8,128)(2,1)}, u32[]{:S(2)}) copy-start(bf16[256,2048]{1,0:T(8,128)(2,1)} %param.16) | copy-start | bytes 3145732
  1055.4 73.9 %copy-start.27 = (f32[2048]{0:T(1024)S(1)}, f32[2048]{0:T(1024)}, u32[]{:S(2)}) copy-start(f32[2048]{0:T(1024)} %param.17) | copy-start | bytes 24580
  1055.4 76.2 %copy-start.31 = (f32[2048]{0:T(1024)S(1)}, f32[2048]{0:T(1024)}, u32[]{:S(2)}) copy-start(f32[2048]{0:T(1024)} %get-tuple-element.164) | copy-start | bytes 24580
  1055.4 115.9 %copy-start.36 = (f32[256]{0:T(256)S(1)}, f32[256]{0:T(256)}, u32[]{:S(2)}) copy-start(f32[256]{0:T(256)} %get-tuple-element.228) | copy-start | bytes 3076
  (34 other events, 591.9 us)
Sparse Core Ops, SparseCore 0:
  9.6 36.8 all-gather.11
  48.9 53.2 all-gather.9
  103.8 29.1 all-gather.13
  144.9 86.3 reduce-scatter.11
  232.8 82.0 all-gather.17
  317.1 51.0 all-gather.15
  369.8 82.0 all-gather.19
  453.7 51.0 all-gather.23
  506.4 82.0 all-gather.21
  639.0 84.7 reduce-scatter.15
  726.9 86.2 reduce-scatter.13
  818.4 52.5 all-gather.25
  873.3 168.1 reduce-scatter.31
  1044.5 84.7 reduce-scatter.17
  1132.0 32.7 reduce-scatter.21
  1167.5 30.8 reduce-scatter.23
  1201.1 48.1 reduce-scatter.25
  1252.0 48.3 reduce-scatter.19
  1303.4 166.6 reduce-scatter.27
  1472.8 166.6 reduce-scatter.29
where the time goes:
time: 1660 us; the launch traced here: 1650 us
  waiting for transfers between devices  1190 us (72%)
  matrix products  239 us (14%)
  blocking collectives  76 us (5%)
  local copies, waits for them, and re-layouts  68.4 us (4%)
  other arithmetic  51.8 us (3%)
    reduce_scatter x1, waiting for transfers between devices, per_device(): lax.psum_scatter(grad_gate, 'dp', scatter_dimension=0, tiled=True)  170 us
    reduce_scatter x1, waiting for transfers between devices, per_device(): lax.psum_scatter(grad_up, 'dp', scatter_dimension=0, tiled=True)  169 us
    reduce_scatter x1, waiting for transfers between devices, per_device(): lax.psum_scatter(contract_cols(hidden, down_full), 'tensor', scatter_dime...  86.7 us
    reduce_scatter x1, waiting for transfers between devices, per_device(): lax.psum_scatter(contract_cols(mixed_all, out_full), 'tensor', scatter_di...  85.9 us
    all_gather x1, waiting for transfers between devices, per_device(): lax.all_gather(w_down, 'dp', axis=0, tiled=True)  83.7 us
    all_gather x1, waiting for transfers between devices, per_device(): lax.all_gather(w_gate, 'dp', axis=0, tiled=True)  78 us
    reduce_scatter x1, waiting for transfers between devices, per_device(): lax.psum_scatter(contract_cols(grad_query_rows, query_full) + contract_co...  70.7 us
    reduce_scatter x1, waiting for transfers between devices, per_device(): lax.psum_scatter(contract_cols(grad_gate_pre, gate_full) + contract_cols(...  70.3 us
  transfers between devices with their start and end apart: 20, of which 16 were waited for; matrix products, arithmetic and copies ran while one was open for 18% of the time, Pallas kernels for 0%

commit v1 on v0

--- a/solution.py
+++ b/solution.py
@@ -124,6 +124,12 @@
         "gjst,sgjd->tgd", grad_scores, grouped, preferred_element_type=jnp.float32
     ) * head_dim ** (-0.5)
     return (grad_queries.reshape(seq_len, head_count, head_dim), grad_keys, grad_values)
+
+
+def sum_rows(partial, axis):
+    return lax.psum_scatter(
+        partial.astype(jnp.bfloat16), axis, scatter_dimension=0, tiled=True
+    ).astype(jnp.float32)
 
 
 def per_device(
@@ -179,9 +185,7 @@
     doc_slots = doc_ids.reshape(slot_count, SEQ)
     mixed_slots, log_total = lax.map(attend, (query_rows, key_rows, value_rows, doc_slots))
     mixed_all = mixed_slots.reshape(total_rows, local_heads * HD)
-    residual_own = input_own + lax.psum_scatter(
-        contract_cols(mixed_all, out_full), "tensor", scatter_dimension=0, tiled=True
-    )
+    residual_own = input_own + sum_rows(contract_cols(mixed_all, out_full), "tensor")
     scale_two_own = norm_scale(residual_own)
     normed_two = lax.all_gather(
         (residual_own * scale_two_own * mlp_gain[None, :]).astype(jnp.bfloat16),
@@ -196,9 +200,7 @@
     hidden = (silu_gate * up_pre).astype(jnp.bfloat16)
     block_output = (
         residual_own
-        + lax.psum_scatter(
-            contract_cols(hidden, down_full), "tensor", scatter_dimension=0, tiled=True
-        )
+        + sum_rows(contract_cols(hidden, down_full), "tensor")
     ).astype(jnp.bfloat16)
     grad_full = lax.all_gather(cotangent, "tensor", axis=0, tiled=True)
     grad_hidden = jnp.dot(grad_full, down_full, preferred_element_type=jnp.float32)
@@ -209,11 +211,9 @@
     grad_up_pre = (grad_hidden * silu_gate).astype(jnp.bfloat16)
     grad_gate = contract_rows(normed_two, grad_gate_pre)
     grad_up = contract_rows(normed_two, grad_up_pre)
-    grad_normed_own = lax.psum_scatter(
+    grad_normed_own = sum_rows(
         contract_cols(grad_gate_pre, gate_full) + contract_cols(grad_up_pre, up_full),
         "tensor",
-        scatter_dimension=0,
-        tiled=True,
     )
     grad_mlp_gain = jnp.sum(grad_normed_own * residual_own * scale_two_own, axis=0)
     grad_residual_own = cotangent.astype(jnp.float32) + norm_back(
@@ -244,26 +244,24 @@
     grad_query = contract_rows(normed_one, grad_query_rows)
     grad_key = contract_rows(normed_one, grad_key_rows)
     grad_value = contract_rows(normed_one, grad_value_rows)
-    grad_normed_one = lax.psum_scatter(
+    grad_normed_one = sum_rows(
         contract_cols(grad_query_rows, query_full)
         + contract_cols(grad_key_rows, key_full)
         + contract_cols(grad_value_rows, value_full),
         "tensor",
-        scatter_dimension=0,
-        tiled=True,
     )
     grad_attn_gain = jnp.sum(grad_normed_one * input_own * scale_one, axis=0)
     input_grad = (
         grad_residual_own + norm_back(grad_normed_one, input_own, scale_one, attn_gain)
     ).astype(jnp.bfloat16)
     summed = (
-        lax.psum_scatter(grad_query, "dp", scatter_dimension=0, tiled=True),
-        lax.psum_scatter(grad_key, "dp", scatter_dimension=0, tiled=True),
-        lax.psum_scatter(grad_value, "dp", scatter_dimension=0, tiled=True),
-        lax.psum_scatter(grad_out, "dp", scatter_dimension=0, tiled=True),
-        lax.psum_scatter(grad_gate, "dp", scatter_dimension=0, tiled=True),
-        lax.psum_scatter(grad_up, "dp", scatter_dimension=0, tiled=True),
-        lax.psum_scatter(grad_down, "dp", scatter_dimension=0, tiled=True),
+        sum_rows(grad_query, "dp"),
+        sum_rows(grad_key, "dp"),
+        sum_rows(grad_value, "dp"),
+        sum_rows(grad_out, "dp"),
+        sum_rows(grad_gate, "dp"),
+        sum_rows(grad_up, "dp"),
+        sum_rows(grad_down, "dp"),
     )
     gains = lax.psum((grad_attn_gain, grad_mlp_gain), ("dp", "tensor"))
     return (

time: 1660 us -> 1370 us (0.83)
  waiting for transfers between devices: 1190 us -> 909 us
    reduce_scatter x11, waiting for transfers between devices: 779 us -> 480 us  [sum_rows(): lax.psum_scatter(partial.astype(jnp.bfloat16), axis, scatter_dimension=0,...]
  transfers between devices with their start and end apart: 20 -> 20, of which waited for: 16 -> 16; matrix products, arithmetic and copies ran while one was open for 18% -> 13% of each run, Pallas kernels for 0% -> 0%
where the time goes in v1:
time: 1370 us; the launch traced here: 1360 us
  waiting for transfers between devices  909 us (66%)
  matrix products  226 us (16%)
  blocking collectives  76.9 us (6%)
  local copies, waits for them, and re-layouts  64.8 us (5%)
  other arithmetic  63.8 us (5%)
  between operations  15.4 us (1%)
    reduce_scatter x11, waiting for transfers between devices, sum_rows(): lax.psum_scatter(partial.astype(jnp.bfloat16), axis, scatter_dimension=0,...  480 us
    all_gather x1, waiting for transfers between devices, per_device(): lax.all_gather(w_down, 'dp', axis=0, tiled=True)  83.7 us
    all_gather x1, waiting for transfers between devices, per_device(): lax.all_gather(w_gate, 'dp', axis=0, tiled=True)  76.9 us
    all_gather x1, waiting for transfers between devices, per_device(): lax.all_gather(w_up, 'dp', axis=0, tiled=True)  69.1 us
    dot_general x7, matrix products, contract_rows(): lax.dot_general(left_side, right_side, (((0,), (0,)), ((), ())), preferre...  58.9 us
    dot_general x7, matrix products, contract_cols(): lax.dot_general(left_side, right_side, (((1,), (1,)), ((), ())), preferre...  56.5 us
    all_gather x1, waiting for transfers between devices, per_device(): lax.all_gather((residual_own * scale_two_own * mlp_gain[None, :]).astype(...  53.4 us
    all_gather x1, waiting for transfers between devices, per_device(): lax.all_gather(grad_residual_own.astype(jnp.bfloat16), 'tensor', axis=0,...  52.6 us
  transfers between devices with their start and end apart: 20, of which 16 were waited for; matrix products, arithmetic and copies ran while one was open for 13% of the time, Pallas kernels for 0%

profile of v1, /device:TPU:0, one launch (start us, length us, event | category | flops | bytes accessed | tf_op | source)
XLA Modules:
  0.0 1358.6 jit_solution(2568812626579666158)
XLA Ops:
  14.4 18.8 %all_gather.35 = bf16[2048,128]{1,0:T(8,128)(2,1)S(1)} all-gather(bf16[256,128]{1,0:T(8,128)(2,1)S(1)} %copy-done.32), channel_id=1, replica_groups=mesh['dp'=8,'tensor'=4] {'dp'}, dimensions={0}, use_global_device_ids=true | all-gather | bytes 589824 | tf_op jit(solution)/shard_map/all_gather | solution.py:151
  33.2 18.2 %all_gather.34 = bf16[2048,128]{1,0:T(8,128)(2,1)} all-gather(bf16[256,128]{1,0:T(8,128)(2,1)S(1)} %copy-done.33), channel_id=1, replica_groups=mesh['dp'=8,'tensor'=4] {'dp'}, dimensions={0}, use_global_device_ids=true | all-gather | bytes 589824 | tf_op jit(solution)/shard_map/all_gather | solution.py:152
  51.5 50.4 %all-gather.10.cloned.1.call-done = bf16[1024,2048]{1,0:T(8,128)(2,1)} async-done(((bf16[256,2048]{1,0:T(8,128)(2,1)}), bf16[1024,2048]{1,0:T(8,128)(2,1)}) %all-gather.10.cloned.1.call-update) | async-done | bytes 4194320 | tf_op jit(solution)/shard_map/all_gather | solution.py:166
  121.3 15.1 %while.26 = (s32[]{:T(128)}, bf16[2,512,512]{2,1,0:T(8,128)(2,1)}, f32[2,2,4,512,1]{3,2,1,4,0:T(4,128)S(1)}, bf16[2,512,2,64]{1,3,2,0:T(8,128)(2,1)S(1)}, s32[2,...) while((s32[]{:T(128)}, bf16[2,512,512]{2,1,0:T(8,128)(2,1)}, ...), condition=%wide.region_4.5_spmd, body=%wide.region_1.4_spmd.sunk | while | flops 564130816 | bytes 32913000 | solution.py:186
  143.5 52.2 %reduce-scatter.12.cloned.1.call-done = bf16[256,2048]{1,0:T(8,128)(2,1)} async-done(((bf16[1024,2048]{1,0:T(8,128)(2,1)}), bf16[256,2048]{1,0:T(8,128)(2,1)}) %reduce-scatter.12.cloned.1.call-update) | async-done | bytes 1048592 | tf_op jit(solution)/shard_map/reduce_scatter | solution.py:130
  202.3 76.9 %all-gather.18.cloned.1.call-done = bf16[2048,2048]{1,0:T(8,128)(2,1)} async-done(((bf16[256,2048]{1,0:T(8,128)(2,1)}), bf16[2048,2048]{1,0:T(8,128)(2,1)}) %all-gather.18.cloned.1.call-update) | async-done | bytes 8388624 | tf_op jit(solution)/shard_map/all_gather | solution.py:154
  279.3 53.4 %all-gather.16.cloned.1.call-done = bf16[1024,2048]{1,0:T(8,128)(2,1)} async-done(((bf16[256,2048]{1,0:T(8,128)(2,1)}), bf16[1024,2048]{1,0:T(8,128)(2,1)}) %all-gather.16.cloned.1.call-update) | async-done | bytes 4194320 | tf_op jit(solution)/shard_map/all_gather | solution.py:190
  332.6 14.6 %fusion.75 = f32[1024,2048]{1,0:T(8,128)} fusion(bf16[1024,2048]{1,0:T(8,128)(2,1)} %all-gather.16.cloned.1.call-done, bf16[2048,2048]{1,0:T(8,128)(2,1)} %all-gather.18.cloned.1.call-done), kind=kOutput, calls=%fused_computation.143 | convolution fusion | flops 8589934592 | bytes 20971520 | tf_op jit(solution)/shard_map/dot_general | solution.py:196
  347.2 69.1 %all-gather.20.cloned.1.call-done = bf16[2048,2048]{1,0:T(8,128)(2,1)} async-done(((bf16[256,2048]{1,0:T(8,128)(2,1)}), bf16[2048,2048]{1,0:T(8,128)(2,1)}) %all-gather.20.cloned.1.call-update) | async-done | bytes 8388624 | tf_op jit(solution)/shard_map/all_gather | solution.py:155
  416.3 14.5 %fusion.76 = f32[1024,2048]{1,0:T(8,128)} fusion(bf16[1024,2048]{1,0:T(8,128)(2,1)} %all-gather.16.cloned.1.call-done, bf16[2048,2048]{1,0:T(8,128)(2,1)} %all-gather.20.cloned.1.call-done), kind=kOutput, calls=%fused_computation.144 | convolution fusion | flops 8589934592 | bytes 20971520 | tf_op jit(solution)/shard_map/dot_general | solution.py:197
  430.8 38.5 %all-gather.24.cloned.1.call-done = bf16[1024,2048]{1,0:T(8,128)(2,1)} async-done(((bf16[256,2048]{1,0:T(8,128)(2,1)}), bf16[1024,2048]{1,0:T(8,128)(2,1)}) %all-gather.24.cloned.1.call-update) | async-done | bytes 4194320 | tf_op jit(solution)/shard_map/all_gather | solution.py:205
  469.2 83.7 %all-gather.22.cloned.1.call-done = bf16[2048,2048]{1,0:T(8,128)(2,1)} async-done(((bf16[256,2048]{1,0:T(8,128)(2,1)}), bf16[2048,2048]{1,0:T(8,128)(2,1)}) %all-gather.22.cloned.1.call-update) | async-done | bytes 8388624 | tf_op jit(solution)/shard_map/all_gather | solution.py:156
  552.9 21.1 %multiply_convert_fusion.1 = (bf16[1024,2048]{1,0:T(8,128)(2,1)S(1)}, bf16[1024,2048]{1,0:T(8,128)(2,1)}, bf16[1024,2048]{1,0:T(8,128)(2,1)}) fusion(f32[1024,2048]{1,0:T(8,128)} %fusion.75, f32[1024,2048]{1,0:T(8,128)} %fusion.76, bf16[1024,2048]{1,0:T(8,128)(2,1)} %all-gather.24.cloned.1.call-done, bf16[2048,2048]{1,0:T(8,128)(2,1)} %all-gather.22.cloned.1.call-done), kind=kOutput, calls=%fused_computation.64 | convolution fusion | flops 8621391872 | bytes 41943040 | tf_op jit(solution)/shard_map/dot_general | solution.py:206
  574.0 16.3 %fusion.77 = f32[1024,2048]{1,0:T(8,128)} fusion(bf16[1024,2048]{1,0:T(8,128)(2,1)} %get-tuple-element.211, bf16[2048,2048]{1,0:T(8,128)(2,1)} %all-gather.18.cloned.1.call-done), kind=kOutput, calls=%fused_computation.145 | convolution fusion | flops 8589934592 | bytes 20971520 | tf_op jit(solution)/shard_map/dot_general | solution.py:69
  590.4 12.4 add_convert_fusion.1
  602.8 51.2 %reduce-scatter.16.cloned.1.call-done = bf16[256,2048]{1,0:T(8,128)(2,1)} async-done(((bf16[1024,2048]{1,0:T(8,128)(2,1)}), bf16[256,2048]{1,0:T(8,128)(2,1)}) %reduce-scatter.16.cloned.1.call-update) | async-done | bytes 1048592 | tf_op jit(solution)/shard_map/reduce_scatter | solution.py:130
  660.0 52.6 %all-gather.26.cloned.1.call-done = bf16[1024,2048]{1,0:T(8,128)(2,1)} async-done(((bf16[256,2048]{1,0:T(8,128)(2,1)}), bf16[1024,2048]{1,0:T(8,128)(2,1)}) %all-gather.26.cloned.1.call-update) | async-done | bytes 4194320 | tf_op jit(solution)/shard_map/all_gather | solution.py:222
  717.9 106.1 %while.27 = (s32[]{:T(128)}, f32[2,512,8,64]{1,0,3,2:T(2,128)}, f32[2,512,2,64]{1,0,3,2:T(2,128)}, bf16[2,512,2,64]{1,3,2,0:T(8,128)(2,1)}, bf16[2,512,2,64]{1,3...) while((s32[]{:T(128)}, f32[2,512,8,64]{1,0,3,2:T(2,128)}, ...), condition=%wide.region_12.13_spmd, body=%wide.region_10.12_spmd.sunk | while | flops 1365045760 | bytes 147417520 | solution.py:230
  738.8 19.7 %dynamic_update_slice.30 = f32[2,512,8,64]{1,0,3,2:T(2,128)} dynamic-update-slice(f32[2,512,8,64]{1,0,3,2:T(2,128)} %get-tuple-element.382, f32[1,512,8,64]{1,0,3,2:T(1,128)S(1)} %copy.94, s32[]{:T(128)} %get-tuple-element.381, s32[]{:T(128)} %constant.45.clone.1..sunk, s32[]{:T(128)} %constant.45.clone.1..sunk, s32[]{:T(128)} %constant.45.clone.1..sunk) | dynamic-update-slice | bytes 2097156 | tf_op jit(solution)/shard_map/while/body/jit(dynamic_update_index_in_dim)/dynamic_update_slice | solution.py:230
  791.7 19.7 %dynamic_update_slice.30 = f32[2,512,8,64]{1,0,3,2:T(2,128)} dynamic-update-slice(f32[2,512,8,64]{1,0,3,2:T(2,128)} %get-tuple-element.382, f32[1,512,8,64]{1,0,3,2:T(1,128)S(1)} %copy.94, s32[]{:T(128)} %get-tuple-element.381, s32[]{:T(128)} %constant.45.clone.1..sunk, s32[]{:T(128)} %constant.45.clone.1..sunk, s32[]{:T(128)} %constant.45.clone.1..sunk) | dynamic-update-slice | bytes 2097156 | tf_op jit(solution)/shard_map/while/body/jit(dynamic_update_index_in_dim)/dynamic_update_slice | solution.py:230
  834.3 14.1 %convolution_convert_fusion.1 = bf16[2048,2048]{1,0:T(8,128)(2,1)} fusion(bf16[1024,2048]{1,0:T(8,128)(2,1)} %all-gather.16.cloned.1.call-done, bf16[1024,2048]{1,0:T(8,128)(2,1)} %get-tuple-element.211), kind=kOutput, calls=%fused_computation.70 | convolution fusion | flops 8594128896 | bytes 16777216 | tf_op jit(solution)/shard_map/dot_general | solution.py:63
  848.5 14.2 %convolution_convert_fusion = bf16[2048,2048]{1,0:T(8,128)(2,1)} fusion(bf16[1024,2048]{1,0:T(8,128)(2,1)} %all-gather.16.cloned.1.call-done, bf16[1024,2048]{1,0:T(8,128)(2,1)} %copy-done.48), kind=kOutput, calls=%fused_computation.69 | convolution fusion | flops 8594128896 | bytes 16777216 | tf_op jit(solution)/shard_map/dot_general | solution.py:63
  863.0 14.0 %convert_bitcast_fusion = bf16[2048,2048]{0,1:T(8,128)(2,1)} fusion(bf16[1024,2048]{1,0:T(8,128)(2,1)} %get-tuple-element.212, bf16[1024,2048]{1,0:T(8,128)(2,1)} %all-gather.24.cloned.1.call-done), kind=kOutput, calls=%fused_computation.61 | convolution fusion | flops 8594128896 | bytes 16777216 | tf_op jit(solution)/shard_map/dot_general | solution.py:63
  899.0 14.4 %convolution_convert_fusion.2 = bf16[1024,2048]{1,0:T(8,128)(2,1)} fusion(bf16[1024,2048]{1,0:T(8,128)(2,1)} %get-tuple-element.212, bf16[2048,2048]{1,0:T(8,128)(2,1)} %all-gather.22.cloned.1.call-done), kind=kOutput, calls=%fused_computation.77 | convolution fusion | flops 8592031744 | bytes 16777216 | tf_op jit(solution)/shard_map/dot_general | solution.py:69
  916.5 66.7 %reduce-scatter.28.cloned.1.call-done = bf16[256,2048]{1,0:T(8,128)(2,1)} async-done(((bf16[2048,2048]{1,0:T(8,128)(2,1)}), bf16[256,2048]{1,0:T(8,128)(2,1)}) %reduce-scatter.28.cloned.1.call-update) | async-done | bytes 1048592 | tf_op jit(solution)/shard_map/reduce_scatter | solution.py:130
  986.0 87.4 %reduce-scatter.30.cloned.1.call-done = bf16[256,2048]{1,0:T(8,128)(2,1)} async-done(((bf16[2048,2048]{1,0:T(8,128)(2,1)}), bf16[256,2048]{1,0:T(8,128)(2,1)}) %reduce-scatter.30.cloned.1.call-update) | async-done | bytes 1048592 | tf_op jit(solution)/shard_map/reduce_scatter | solution.py:130
  1076.2 87.3 %reduce-scatter.32.cloned.1.call-done = bf16[256,2048]{0,1:T(8,128)(2,1)} async-done(((bf16[2048,2048]{0,1:T(8,128)(2,1)}), bf16[256,2048]{0,1:T(8,128)(2,1)}) %reduce-scatter.32.cloned.1.call-update) | async-done | bytes 1048592 | tf_op jit(solution)/shard_map/reduce_scatter | solution.py:130
  1166.1 34.0 %reduce-scatter.26.cloned.1.call-done = bf16[256,512]{1,0:T(8,128)(2,1)} async-done(((bf16[2048,512]{1,0:T(8,128)(2,1)}), bf16[256,512]{1,0:T(8,128)(2,1)}) %reduce-scatter.26.cloned.1.call-update) | async-done | bytes 262160 | tf_op jit(solution)/shard_map/reduce_scatter | solution.py:130
  1201.8 35.1 %reduce-scatter.20.cloned.1.call-done = bf16[256,512]{1,0:T(8,128)(2,1)} async-done(((bf16[2048,512]{1,0:T(8,128)(2,1)}), bf16[256,512]{1,0:T(8,128)(2,1)}) %reduce-scatter.20.cloned.1.call-update) | async-done | bytes 262160 | tf_op jit(solution)/shard_map/reduce_scatter | solution.py:130
  1238.8 52.3 %reduce-scatter.18.cloned.1.call-done = bf16[256,2048]{1,0:T(8,128)(2,1)} async-done(((bf16[1024,2048]{1,0:T(8,128)(2,1)}), bf16[256,2048]{1,0:T(8,128)(2,1)}) %reduce-scatter.18.cloned.1.call-update) | async-done | bytes 1048592 | tf_op jit(solution)/shard_map/reduce_scatter | solution.py:130
  1293.0 39.8 %all-reduce = (f32[2048]{0:T(1024)}, f32[2048]{0:T(1024)}) all-reduce(f32[2048]{0:T(1024)S(1)} %get-tuple-element.166, f32[2048]{0:T(1024)S(1)} %copy-done.34), channel_id=1, replica_groups=mesh['dp'=8,'tensor'=4] {'dp','tensor'}, use_global_device_ids=true, to_apply=%region_23.24 | all-reduce | flops 4096 | bytes 32768 | tf_op jit(solution)/shard_map/psum | solution.py:266
  1332.9 14.0 %reduce-scatter.14.cloned.1.call-done = bf16[256,2048]{1,0:T(8,128)(2,1)} async-done(((bf16[1024,2048]{1,0:T(8,128)(2,1)}), bf16[256,2048]{1,0:T(8,128)(2,1)}) %reduce-scatter.14.cloned.1.call-update) | async-done | bytes 1048592 | tf_op jit(solution)/shard_map/reduce_scatter | solution.py:130
  (275 shorter events, 185.3 us)
Async XLA Ops:
  7.2 44.2 %all-gather.12.cloned.1.call-start = ((), (), s32[]{:S(2)}) async-start(), calls=%async_computation.12 | async-start | bytes 2359296 | tf_op jit(solution)/shard_map/all_gather | solution.py:150
  7.9 93.9 %all-gather.10.cloned.1.call-start = ((), (), s32[]{:S(2)}) async-start(), calls=%async_computation.11 | async-start | bytes 5242880 | tf_op jit(solution)/shard_map/all_gather | solution.py:166
  13.2 123.3 %all-gather.14.cloned.1.call-start = ((), (), s32[]{:S(2)}) async-start(), calls=%async_computation.13 | async-start | bytes 2359296 | tf_op jit(solution)/shard_map/all_gather | solution.py:153
  13.9 181.8 %reduce-scatter.12.cloned.1.call-start = ((), (), s32[]{:S(2)}) async-start(), calls=%async_computation.14 | async-start | bytes 5242880 | tf_op jit(solution)/shard_map/reduce_scatter | solution.py:130
  142.9 136.3 %all-gather.18.cloned.1.call-start = ((), (), s32[]{:S(2)}) async-start(), calls=%async_computation.16 | async-start | bytes 9437184 | tf_op jit(solution)/shard_map/all_gather | solution.py:154
  143.5 189.1 %all-gather.16.cloned.1.call-start = ((), (), s32[]{:S(2)}) async-start(), calls=%async_computation.15 | async-start | bytes 5242880 | tf_op jit(solution)/shard_map/all_gather | solution.py:190
  197.4 459.1 %copy-start.35 = (f32[256]{0:T(256)}, f32[256]{0:T(256)S(1)}, u32[]{:S(2)}) copy-start(f32[256]{0:T(256)S(1)} %get-tuple-element.228) | copy-start | bytes 3076
  197.4 459.1 %copy-start.41 = (f32[256]{0:T(256)}, f32[256]{0:T(256)S(1)}, u32[]{:S(2)}) copy-start(f32[256]{0:T(256)S(1)} %get-tuple-element.227) | copy-start | bytes 3076
  200.1 216.2 %all-gather.20.cloned.1.call-start = ((), (), s32[]{:S(2)}) async-start(), calls=%async_computation.17 | async-start | bytes 9437184 | tf_op jit(solution)/shard_map/all_gather | solution.py:155
  200.8 268.4 %all-gather.24.cloned.1.call-start = ((), (), s32[]{:S(2)}) async-start(), calls=%async_computation.20 | async-start | bytes 5242880 | tf_op jit(solution)/shard_map/all_gather | solution.py:205
  201.6 351.3 %all-gather.22.cloned.1.call-start = ((), (), s32[]{:S(2)}) async-start(), calls=%async_computation.18 | async-start | bytes 9437184 | tf_op jit(solution)/shard_map/all_gather | solution.py:156
  202.3 451.7 %reduce-scatter.16.cloned.1.call-start = ((), (), s32[]{:S(2)}) async-start(), calls=%async_computation.21 | async-start | bytes 5242880 | tf_op jit(solution)/shard_map/reduce_scatter | solution.py:130
  602.8 109.9 %all-gather.26.cloned.1.call-start = ((), (), s32[]{:S(2)}) async-start(), calls=%async_computation.22 | async-start | bytes 5242880 | tf_op jit(solution)/shard_map/all_gather | solution.py:222
  659.9 253.5 %reduce-scatter.22.cloned.1.call-start = ((), (), s32[]{:S(2)}) async-start(), calls=%async_computation.25 | async-start | bytes 589824 | tf_op jit(solution)/shard_map/reduce_scatter | solution.py:130
  829.4 85.6 %reduce-scatter.24.cloned.1.call-start = ((), (), s32[]{:S(2)}) async-start(), calls=%async_computation.26 | async-start | bytes 589824 | tf_op jit(solution)/shard_map/reduce_scatter | solution.py:130
  834.3 148.9 %reduce-scatter.28.cloned.1.call-start = ((), (), s32[]{:S(2)}) async-start(), calls=%async_computation.28 | async-start | bytes 9437184 | tf_op jit(solution)/shard_map/reduce_scatter | solution.py:130
  848.5 224.9 %reduce-scatter.30.cloned.1.call-start = ((), (), s32[]{:S(2)}) async-start(), calls=%async_computation.29 | async-start | bytes 9437184 | tf_op jit(solution)/shard_map/reduce_scatter | solution.py:130
  862.7 300.8 %reduce-scatter.32.cloned.1.call-start = ((), (), s32[]{:S(2)}) async-start(), calls=%async_computation.30 | async-start | bytes 9437184 | tf_op jit(solution)/shard_map/reduce_scatter | solution.py:130
  877.1 323.0 %reduce-scatter.26.cloned.1.call-start = ((), (), s32[]{:S(2)}) async-start(), calls=%async_computation.27 | async-start | bytes 2359296 | tf_op jit(solution)/shard_map/reduce_scatter | solution.py:130
  883.5 353.5 %reduce-scatter.20.cloned.1.call-start = ((), (), s32[]{:S(2)}) async-start(), calls=%async_computation.24 | async-start | bytes 2359296 | tf_op jit(solution)/shard_map/reduce_scatter | solution.py:130
  891.3 399.9 %reduce-scatter.18.cloned.1.call-start = ((), (), s32[]{:S(2)}) async-start(), calls=%async_computation.23 | async-start | bytes 5242880 | tf_op jit(solution)/shard_map/reduce_scatter | solution.py:130
  899.0 447.9 %reduce-scatter.14.cloned.1.call-start = ((), (), s32[]{:S(2)}) async-start(), calls=%async_computation.19 | async-start | bytes 5242880 | tf_op jit(solution)/shard_map/reduce_scatter | solution.py:130
  985.9 305.2 %copy-start.3 = (bf16[256,2048]{1,0:T(8,128)(2,1)S(1)}, bf16[256,2048]{1,0:T(8,128)(2,1)}, u32[]{:S(2)}) copy-start(bf16[256,2048]{1,0:T(8,128)(2,1)} %param.16) | copy-start | bytes 3145732
  985.9 305.2 %copy-start.31 = (f32[2048]{0:T(1024)S(1)}, f32[2048]{0:T(1024)}, u32[]{:S(2)}) copy-start(f32[2048]{0:T(1024)} %param.17) | copy-start | bytes 24580
  985.9 305.2 %copy-start.38 = (f32[256]{0:T(256)S(1)}, f32[256]{0:T(256)}, u32[]{:S(2)}) copy-start(f32[256]{0:T(256)} %copy-done.37) | copy-start | bytes 3076
  1076.1 270.8 %copy-start.7 = (bf16[256,2048]{1,0:T(8,128)(2,1)S(1)}, bf16[256,2048]{1,0:T(8,128)(2,1)}, u32[]{:S(2)}) copy-start(bf16[256,2048]{1,0:T(8,128)(2,1)} %reduce-scatter.12.cloned.1.call-done) | copy-start | bytes 3145732
  1076.1 270.8 %copy-start.8 = (bf16[256,2048]{1,0:T(8,128)(2,1)S(1)}, bf16[256,2048]{1,0:T(8,128)(2,1)}, u32[]{:S(2)}) copy-start(bf16[256,2048]{1,0:T(8,128)(2,1)} %param.27) | copy-start | bytes 3145732
  1076.1 270.8 %copy-start.30 = (f32[2048]{0:T(1024)S(1)}, f32[2048]{0:T(1024)}, u32[]{:S(2)}) copy-start(f32[2048]{0:T(1024)} %param.22) | copy-start | bytes 24580
  1076.1 270.8 %copy-start.36 = (f32[256]{0:T(256)S(1)}, f32[256]{0:T(256)}, u32[]{:S(2)}) copy-start(f32[256]{0:T(256)} %copy-done.35) | copy-start | bytes 3076
  1076.1 270.8 %copy-start.42 = (f32[256]{0:T(256)S(1)}, f32[256]{0:T(256)}, u32[]{:S(2)}) copy-start(f32[256]{0:T(256)} %copy-done.41) | copy-start | bytes 3076
  1076.1 270.8 %copy-start.44 = (f32[256]{0:T(256)S(1)}, f32[256]{0:T(256)}, u32[]{:S(2)}) copy-start(f32[256]{0:T(256)} %copy-done.43) | copy-start | bytes 3076
  1076.1 270.8 %copy-start.45 = (f32[256]{0:T(256)S(1)}, f32[256]{0:T(256)}, u32[]{:S(2)}) copy-start(f32[256]{0:T(256)} %get-tuple-element.225) | copy-start | bytes 3076
  (46 other events, 1143.5 us)
Sparse Core Ops, SparseCore 0:
  9.6 37.0 all-gather.11
  49.1 52.6 all-gather.9
  103.5 29.1 all-gather.13
  143.0 52.6 reduce-scatter.11
  197.2 82.0 all-gather.17
  281.5 51.0 all-gather.15
  334.2 82.0 all-gather.19
  418.1 51.0 all-gather.23
  470.8 82.0 all-gather.21
  602.9 51.0 reduce-scatter.15
  660.1 52.5 all-gather.25
  829.5 31.2 reduce-scatter.21
  863.7 29.5 reduce-scatter.23
  895.4 87.7 reduce-scatter.27
  985.3 87.9 reduce-scatter.29
  1075.5 87.9 reduce-scatter.31
  1165.6 34.3 reduce-scatter.25
  1202.2 34.7 reduce-scatter.19
  1240.0 51.1 reduce-scatter.17
  1294.0 52.8 reduce-scatter.13

commit v2 on v1

v2 whole, which is shorter than its diff:
```python
import functools

import jax
import jax.numpy as jnp
from jax import lax
from jax.experimental import pallas as pl
from jax.experimental.pallas import tpu as pltpu
from jax.sharding import PartitionSpec as P

HD = 64
SEQ = 512
QUERY_TILE = 256

EPSILON = 1e-05
ROPE_BASE = 500000.0
NEG_LARGE = -1e30


def rotary_tables(length, head_dim, copies):
    half_dim = head_dim // 2
    frequency = ROPE_BASE ** (-(jnp.arange(half_dim, dtype=jnp.float32) * (2.0 / head_dim)))
    angles = jnp.arange(length, dtype=jnp.float32)[:, None] * frequency[None, :]
    angles = jnp.concatenate([angles, angles] * copies, axis=1)
    return (jnp.cos(angles), jnp.sin(angles))


def norm_scale(tensor_rows):
    return lax.rsqrt(jnp.mean(tensor_rows * tensor_rows, axis=1, keepdims=True) + EPSILON)


def norm_back(grad_normed, tensor_rows, row_scale, gain_row):
    weighted = grad_normed * gain_row[None, :]
    inner_mean = jnp.mean(weighted * tensor_rows, axis=1, keepdims=True)
    return row_scale * weighted - tensor_rows * (row_scale * row_scale * row_scale) * inner_mean


def contract_rows(left_side, right_side):
    return lax.dot_general(
        left_side, right_side, (((0,), (0,)), ((), ())), preferred_element_type=jnp.float32
    )


def contract_cols(left_side, right_side):
    return lax.dot_general(
        left_side, right_side, (((1,), (1,)), ((), ())), preferred_element_type=jnp.float32
    )


def matmul(left_side, right_side):
    return jnp.dot(left_side, right_side, preferred_element_type=jnp.float32)


def half_turn(rows):
    width = rows.shape[1]
    first = lax.broadcasted_iota(jnp.int32, rows.shape, 1) % HD < HD // 2
    if width % 128 == 0:
        later = pltpu.roll(rows, width - HD // 2, axis=1)
        before = pltpu.roll(rows, HD // 2, axis=1)
        return jnp.where(first, later, before), first
    halves = [rows[:, at : at + HD // 2] for at in range(0, width, HD // 2)]
    swapped = [halves[i ^ 1] for i in range(len(halves))]
    return jnp.concatenate(swapped, axis=1), first


def rotate(rows, cosine, sine):
    turned, first = half_turn(rows)
    return rows * cosine + jnp.where(first, -turned, turned) * sine


def unrotate(rows, cosine, sine):
    turned, first = half_turn(rows * sine)
    return rows * cosine + jnp.where(first, turned, -turned)


def group_columns(rows, group, groups):
    picked = rows[:, :HD]
    for other in range(1, groups):
        picked = jnp.where(group == other, rows[:, other * HD : (other + 1) * HD], picked)
    return picked


def tile_bias(doc_row, doc_col, start, tile, keys):
    query_doc = doc_row[0, :, start : start + tile]
    key_doc = doc_col[:keys, :]
    key_at = lax.broadcasted_iota(jnp.int32, (keys, tile), 0)
    query_at = lax.broadcasted_iota(jnp.int32, (keys, tile), 1) + start
    same = (query_doc == key_doc) & (key_doc >= 0) & (key_at <= query_at)
    live = (query_doc >= 0).astype(jnp.float32)
    return jnp.where(same | (key_at == query_at), 0.0, NEG_LARGE), live


def tile_probs(keys_rows, query_tile, bias):
    scores = contract_cols(keys_rows, query_tile) * HD ** (-0.5) + bias
    weights = jnp.exp(scores - jnp.max(scores, axis=0, keepdims=True))
    return weights * (1.0 / jnp.sum(weights, axis=0, keepdims=True))


def attend_kernel(
    groups, q_ref, k_ref, v_ref, row_ref, col_ref, cos_ref, sin_ref,
    q_out, k_out, v_out, mixed_ref
):
    group = pl.program_id(1)
    width = q_ref.shape[1]
    narrow = k_ref.shape[1]
    query_rows = rotate(q_ref[...], cos_ref[...], sin_ref[...]).astype(jnp.bfloat16)
    key_all = rotate(k_ref[...], cos_ref[:, :narrow], sin_ref[:, :narrow]).astype(jnp.bfloat16)
    value_all = v_ref[...].astype(jnp.bfloat16)
    q_out[...] = query_rows
    k_out[...] = key_all
    v_out[...] = value_all
    key_rows = group_columns(key_all, group, groups)
    value_rows = group_columns(value_all, group, groups)
    for start in range(0, SEQ, QUERY_TILE):
        keys = start + QUERY_TILE
        bias, live = tile_bias(row_ref, col_ref, start, QUERY_TILE, keys)
        mixed = []
        for head in range(width // HD):
            query_tile = query_rows[start:keys, head * HD : (head + 1) * HD]
            probs = tile_probs(key_rows[:keys], query_tile, bias).astype(jnp.bfloat16)
            mixed.append(contract_rows(value_rows[:keys], probs) * live)
        mixed_ref[start:keys, :] = jnp.concatenate(mixed, axis=0).T.astype(jnp.bfloat16)


def attend_back_kernel(
    groups, q_ref, k_ref, v_ref, grad_ref, row_ref, col_ref, cos_ref, sin_ref,
    dq_ref, dk_ref, dv_ref, dk_sum, dv_sum
):
    group = pl.program_id(1)
    width = q_ref.shape[1]
    key_rows = group_columns(k_ref[...], group, groups)
    value_rows = group_columns(v_ref[...], group, groups)
    cosine, sine = cos_ref[...], sin_ref[...]
    dk_sum[...] = jnp.zeros_like(dk_sum)
    dv_sum[...] = jnp.zeros_like(dv_sum)
    for start in range(0, SEQ, QUERY_TILE):
        keys = start + QUERY_TILE
        bias, _ = tile_bias(row_ref, col_ref, start, QUERY_TILE, keys)
        grad_queries = []
        for head in range(width // HD):
            columns = slice(head * HD, (head + 1) * HD)
            query_tile = q_ref[start:keys, columns]
            grad_tile = grad_ref[start:keys, columns]
            probs = tile_probs(key_rows[:keys], query_tile, bias)
            grad_probs = contract_cols(value_rows[:keys], grad_tile)
            delta = jnp.sum(probs * grad_probs, axis=0, keepdims=True)
            grad_scores = (probs * (grad_probs - delta)).astype(jnp.bfloat16)
            dv_sum[:keys, :] += matmul(probs.astype(jnp.bfloat16), grad_tile)
            dk_sum[:keys, :] += matmul(grad_scores, query_tile)
            grad_queries.append(contract_rows(key_rows[:keys], grad_scores))
        turned = jnp.concatenate(grad_queries, axis=0).T * HD ** (-0.5)
        dq_ref[start:keys, :] = unrotate(
            turned, cosine[start:keys], sine[start:keys]
        ).astype(jnp.bfloat16)
    for own in range(groups):

        @pl.when(group == own)
        def _():
            columns = slice(own * HD, (own + 1) * HD)
            dk_ref[:, columns] = dk_sum[...] * HD ** (-0.5)
            dv_ref[:, columns] = dv_sum[...].astype(jnp.bfloat16)

    @pl.when(group == groups - 1)
    def _():
        narrow = dk_ref.shape[1]
        dk_ref[...] = unrotate(dk_ref[...], cosine[:, :narrow], sine[:, :narrow])


def attention_specs(rows, heads_width, keys_width):
    groups = keys_width // HD
    width = heads_width // groups
    grid = (rows // SEQ, groups)
    wide = pl.BlockSpec((SEQ, width), lambda s, g: (s, g))
    narrow = pl.BlockSpec((SEQ, keys_width), lambda s, g: (s, 0))
    docs = [
        pl.BlockSpec((1, 1, SEQ), lambda s, g: (s, 0, 0)),
        pl.BlockSpec((SEQ, 1), lambda s, g: (s, 0)),
    ]
    tables = [pl.BlockSpec((SEQ, width), lambda s, g: (0, 0))] * 2
    return groups, grid, wide, narrow, docs, tables


def attention_cost(rows, heads_width, matmuls):
    pairs = rows * SEQ * (heads_width // HD)
    return pl.CostEstimate(
        flops=2 * matmuls * pairs * HD, transcendentals=pairs, bytes_accessed=16 * rows * heads_width
    )


def attend(query_pre, key_pre, value_pre, doc_row, doc_col, tables):
    rows, heads_width = query_pre.shape
    keys_width = key_pre.shape[1]
    groups, grid, wide, narrow, docs, table_specs = attention_specs(rows, heads_width, keys_width)
    bf = jnp.bfloat16
    return pl.pallas_call(
        functools.partial(attend_kernel, groups),
        name="attend",
        grid=grid,
        in_specs=[wide, narrow, narrow] + docs + table_specs,
        out_specs=[wide, narrow, narrow, wide],
        out_shape=[
            jax.ShapeDtypeStruct((rows, heads_width), bf),
            jax.ShapeDtypeStruct((rows, keys_width), bf),
            jax.ShapeDtypeStruct((rows, keys_width), bf),
            jax.ShapeDtypeStruct((rows, heads_width), bf),
        ],
        cost_estimate=attention_cost(rows, heads_width, 2),
    )(query_pre, key_pre, value_pre, doc_row, doc_col, *tables)


def attend_back(query_rows, key_rows, value_rows, grad_mixed, doc_row, doc_col, tables):
    rows, heads_width = query_rows.shape
    keys_width = key_rows.shape[1]
    groups, grid, wide, narrow, docs, table_specs = attention_specs(rows, heads_width, keys_width)
    bf = jnp.bfloat16
    return pl.pallas_call(
        functools.partial(attend_back_kernel, groups),
        name="attend_back",
        grid=grid,
        in_specs=[wide, narrow, narrow, wide] + docs + table_specs,
        out_specs=[wide, narrow, narrow],
        out_shape=[
            jax.ShapeDtypeStruct((rows, heads_width), bf),
            jax.ShapeDtypeStruct((rows, keys_width), jnp.float32),
            jax.ShapeDtypeStruct((rows, keys_width), bf),
        ],
        scratch_shapes=[pltpu.VMEM((SEQ, HD), jnp.float32)] * 2,
        cost_estimate=attention_cost(rows, heads_width, 5),
    )(query_rows, key_rows, value_rows, grad_mixed, doc_row, doc_col, *tables)


def swap(array, axis, size, bit):
    return lax.ppermute(array, axis, [(i, i ^ bit) for i in range(size)])


def gather_rows(own, size):
    if size != 4:
        return lax.all_gather(own, "tensor", axis=0, tiled=True)
    me = lax.axis_index("tensor")
    rows = own.shape[0]
    half = rows // 2
    near_x = swap(own, "tensor", size, 1)
    near_y = swap(own, "tensor", size, 2)
    far_low = swap(near_x[:half], "tensor", size, 2)
    far_high = swap(near_y[half:], "tensor", size, 1)
    whole = jnp.zeros((size * rows,) + own.shape[1:], own.dtype)
    far = (me ^ 3) * rows
    for piece, at in (
        (own, me * rows),
        (near_x, (me ^ 1) * rows),
        (near_y, (me ^ 2) * rows),
        (far_low, far),
        (far_high, far + half),
    ):
        whole = lax.dynamic_update_slice_in_dim(whole, piece, at, 0)
    return whole


def sum_rows(partial, size):
    partial = partial.astype(jnp.bfloat16)
    if size != 4:
        return lax.psum_scatter(
            partial, "tensor", scatter_dimension=0, tiled=True
        ).astype(jnp.float32)
    me = lax.axis_index("tensor")
    rows = partial.shape[0] // size
    half = rows // 2

    def part(index, start=0, count=rows):
        return lax.dynamic_slice_in_dim(partial, index * rows + start, count, 0)

    from_x = swap(part(me ^ 3, 0, half), "tensor", size, 1)
    from_y = swap(part(me ^ 3, half, half), "tensor", size, 2)
    wide = jnp.float32
    to_y = jnp.concatenate(
        [
            (part(me ^ 2, 0, half).astype(wide) + from_x.astype(wide)).astype(jnp.bfloat16),
            part(me ^ 2, half, half),
        ]
    )
    to_x = jnp.concatenate(
        [
            part(me ^ 1, 0, half),
            (part(me ^ 1, half, half).astype(wide) + from_y.astype(wide)).astype(jnp.bfloat16),
        ]
    )
    last_y = swap(to_y, "tensor", size, 2)
    last_x = swap(to_x, "tensor", size, 1)
    return part(me).astype(wide) + last_x.astype(wide) + last_y.astype(wide)


def sum_all(array, axis, size):
    if size & (size - 1):
        return lax.psum(array, axis)
    bit = 1
    while bit < size:
        array = array + swap(array, axis, size, bit)
        bit *= 2
    return array


def parity_columns(rows, size):
    mine = lax.axis_index("dp") % 2
    cut = rows.reshape(rows.shape[0], size // 2, 2, rows.shape[1] // size)

    def pick(which):
        return lax.dynamic_index_in_dim(cut, which, 2, keepdims=False).reshape(rows.shape[0], -1)

    return pick(mine), pick(1 - mine)


def weight_grad(parities, right_side, size):
    mine, other = parities
    from_pair = swap(contract_rows(other, right_side).astype(jnp.bfloat16), "dp", size, 1)
    pair_sum = contract_rows(mine, right_side) + from_pair.astype(jnp.float32)
    groups = [list(range(0, size, 2)), list(range(1, size, 2))]
    return lax.psum_scatter(
        pair_sum.astype(jnp.bfloat16),
        "dp",
        scatter_dimension=0,
        tiled=True,
        axis_index_groups=groups,
    ).astype(jnp.float32)


def per_device(
    dp,
    tp,
    block_input,
    attn_gain,
    w_query,
    w_key,
    w_value,
    w_out,
    mlp_gain,
    w_gate,
    w_up,
    w_down,
    doc_ids,
    cotangent,
):
    heads_width, keys_width = w_query.shape[1], w_key.shape[1]
    splits = (heads_width, heads_width + keys_width)

    def gather(weight):
        return lax.all_gather(weight, "dp", axis=0, tiled=True)

    qkv_full = gather(jnp.concatenate([w_query, w_key, w_value], axis=1))
    out_full = gather(w_out)
    gate_full = gather(w_gate)
    up_full = gather(w_up)
    down_full = gather(w_down)

    live_all = (doc_ids >= 0).astype(jnp.float32)
    doc_row = doc_ids.reshape(-1, 1, SEQ)
    doc_col = doc_ids.reshape(-1, 1)
    tables = rotary_tables(SEQ, HD, heads_width // keys_width)

    input_own = block_input.astype(jnp.float32)
    scale_one = norm_scale(input_own)
    normed_one = gather_rows(
        (input_own * scale_one * attn_gain[None, :]).astype(jnp.bfloat16), tp
    )
    grad_full = gather_rows(cotangent, tp)

    qkv_pre = matmul(normed_one, qkv_full)
    query_rows, key_rows, value_rows, mixed_all = attend(
        *jnp.split(qkv_pre, splits, axis=1), doc_row, doc_col, tables
    )
    residual_own = input_own + sum_rows(contract_cols(mixed_all, out_full), tp)
    scale_two_own = norm_scale(residual_own)
    normed_two = gather_rows(
        (residual_own * scale_two_own * mlp_gain[None, :]).astype(jnp.bfloat16), tp
    )
    gate_pre = matmul(normed_two, gate_full)
    up_pre = matmul(normed_two, up_full)
    sigmoid_gate = jax.nn.sigmoid(gate_pre)
    silu_gate = gate_pre * sigmoid_gate
    hidden = (silu_gate * up_pre).astype(jnp.bfloat16)
    grad_down = weight_grad(parity_columns(grad_full, dp), hidden, dp)

    grad_hidden = matmul(grad_full, down_full)
    grad_gate_pre = (
        grad_hidden * up_pre * sigmoid_gate * (1.0 + gate_pre * (1.0 - sigmoid_gate))
    ).astype(jnp.bfloat16)
    grad_up_pre = (grad_hidden * silu_gate).astype(jnp.bfloat16)
    normed_two_parities = parity_columns(normed_two, dp)
    grad_gate = weight_grad(normed_two_parities, grad_gate_pre, dp)
    grad_up = weight_grad(normed_two_parities, grad_up_pre, dp)
    grad_normed_own = sum_rows(
        contract_cols(grad_gate_pre, gate_full) + contract_cols(grad_up_pre, up_full), tp
    )
    block_output = (residual_own + sum_rows(contract_cols(hidden, down_full), tp)).astype(
        jnp.bfloat16
    )
    grad_mlp_gain = jnp.sum(grad_normed_own * residual_own * scale_two_own, axis=0)
    grad_residual_own = cotangent.astype(jnp.float32) + norm_back(
        grad_normed_own, residual_own, scale_two_own, mlp_gain
    )
    grad_residual_bf = gather_rows(grad_residual_own.astype(jnp.bfloat16), tp)
    grad_out = weight_grad(parity_columns(grad_residual_bf, dp), mixed_all, dp)
    grad_mixed = (matmul(grad_residual_bf, out_full) * live_all[:, None]).astype(jnp.bfloat16)
    grad_query_rows, grad_keys, grad_value_rows = attend_back(
        query_rows, key_rows, value_rows, grad_mixed, doc_row, doc_col, tables
    )
    grad_qkv_rows = jnp.concatenate(
        [grad_query_rows, grad_keys.astype(jnp.bfloat16), grad_value_rows], axis=1
    )
    grad_qkv = weight_grad(parity_columns(normed_one, dp), grad_qkv_rows, dp)
    grad_query, grad_key, grad_value = jnp.split(grad_qkv, splits, axis=1)
    grad_normed_one = sum_rows(contract_cols(grad_qkv_rows, qkv_full), tp)
    grad_attn_gain = jnp.sum(grad_normed_one * input_own * scale_one, axis=0)
    input_grad = (
        grad_residual_own + norm_back(grad_normed_one, input_own, scale_one, attn_gain)
    ).astype(jnp.bfloat16)
    gains = jnp.stack([grad_attn_gain, grad_mlp_gain])
    gains = sum_all(sum_all(gains, "tensor", tp), "dp", dp)
    return (
        block_output,
        input_grad,
        grad_query,
        grad_key,
        grad_value,
        grad_out,
        grad_gate,
        grad_up,
        grad_down,
        gains[0],
        gains[1],
    )


def solution(mesh):
    in_specs = (
        P(("dp", "tensor"), None),
        P(),
        P("dp", "tensor"),
        P("dp", "tensor"),
        P("dp", "tensor"),
        P("dp", "tensor"),
        P(),
        P("dp", "tensor"),
        P("dp", "tensor"),
        P("dp", "tensor"),
        P("dp"),
        P(("dp", "tensor"), None),
    )
    out_specs = (
        P(("dp", "tensor"), None),
        P(("dp", "tensor"), None),
        P("dp", "tensor"),
        P("dp", "tensor"),
        P("dp", "tensor"),
        P("dp", "tensor"),
        P("dp", "tensor"),
        P("dp", "tensor"),
        P("dp", "tensor"),
        P(),
        P(),
    )
    return jax.shard_map(
        functools.partial(per_device, mesh.shape["dp"], mesh.shape["tensor"]),
        mesh=mesh,
        in_specs=in_specs,
        out_specs=out_specs,
        check_vma=False,
    )
```

time: 1370 us -> 870 us (0.64)
  waiting for transfers between devices: 909 us -> 462 us
  blocking collectives: 76.9 us -> 0 us
  matrix products: 226 us -> 168 us
  starting transfers between devices: 1.44 us -> 44.6 us
  Pallas kernels: 0 us -> 40.9 us
  local copies, waits for them, and re-layouts: 64.8 us -> 99.4 us
  other arithmetic: 63.8 us -> 29.2 us
    all_gather x9 -> x5, waiting for transfers between devices: 425 us -> 85 us  [gather(): return lax.all_gather(weight, 'dp', axis=0, tiled=True)]
    reduce_scatter x11 -> x5, waiting for transfers between devices: 480 us -> 159 us  [weight_grad(): lax.psum_scatter(pair_sum.astype(jnp.bfloat16), 'dp', scatter_dimension=0...]
    ppermute x0 -> x42, waiting for transfers between devices: none -> 215 us  [swap(): return lax.ppermute(array, axis, [(i, i ^ bit) for i in range(size)])]
    dot_general x21 -> x5, matrix products: 111 us -> 63.8 us  [matmul(): return jnp.dot(left_side, right_side, preferred_element_type=jnp.float32)]
    ppermute x0 -> x42, starting transfers between devices: none -> 44.2 us  [swap(): return lax.ppermute(array, axis, [(i, i ^ bit) for i in range(size)])]
    pallas_call x0 -> x2, Pallas kernels: none -> 40.9 us  [the longest x1 23 us: attend_back(): pl.pallas_call(functools.partial(attend_back_kernel, groups), name='atten...]
    psum x1 -> x0, blocking collectives: 39.8 us -> none  [per_device(): gains = lax.psum((grad_attn_gain, grad_mlp_gain), ('dp', 'tensor'))]
    all_gather x2 -> x0, blocking collectives: 37.1 us -> none  [the longest x1 18.8 us: per_device(): lax.all_gather(w_key, 'dp', axis=0, tiled=True)]
  transfers between devices with their start and end apart: 20 -> 52, of which waited for: 16 -> 32; matrix products, arithmetic and copies ran while one was open for 13% -> 26% of each run, Pallas kernels for 0% -> 5%
where the time goes in v2:
time: 870 us; the launch traced here: 860 us
  waiting for transfers between devices  462 us (53%)
  matrix products  168 us (19%)
  local copies, waits for them, and re-layouts  99.4 us (11%)
  starting transfers between devices  44.6 us (5%)
  Pallas kernels  40.9 us (5%)
  other arithmetic  29.2 us (3%)
  between operations  15.3 us (2%)
    ppermute x42, waiting for transfers between devices, swap(): return lax.ppermute(array, axis, [(i, i ^ bit) for i in range(size)])  215 us
    reduce_scatter x5, waiting for transfers between devices, weight_grad(): lax.psum_scatter(pair_sum.astype(jnp.bfloat16), 'dp', scatter_dimension=0...  159 us
    all_gather x5, waiting for transfers between devices, gather(): return lax.all_gather(weight, 'dp', axis=0, tiled=True)  85 us
    dot_general x5, matrix products, matmul(): return jnp.dot(left_side, right_side, preferred_element_type=jnp.float32)  63.8 us
    dot_general x10, matrix products, contract_rows(): lax.dot_general(left_side, right_side, (((0,), (0,)), ((), ())), preferre...  54.8 us
    dot_general x5, matrix products, contract_cols(): lax.dot_general(left_side, right_side, (((1,), (1,)), ((), ())), preferre...  49.8 us
    ppermute x42, starting transfers between devices, swap(): return lax.ppermute(array, axis, [(i, i ^ bit) for i in range(size)])  44.2 us
    pallas_call x1, Pallas kernels, attend_back(): pl.pallas_call(functools.partial(attend_back_kernel, groups), name='atten...  23 us
  transfers between devices with their start and end apart: 52, of which 32 were waited for; matrix products, arithmetic and copies ran while one was open for 26% of the time, Pallas kernels for 5%

profile of v2, /device:TPU:0, one launch (start us, length us, event | category | flops | bytes accessed | tf_op | source)
XLA Modules:
  0.0 860.2 jit_solution(1429018111232011389)
XLA Ops:
  23.2 16.1 %collective-permute-done = bf16[256,2048]{1,0:T(8,128)(2,1)} collective-permute-done((bf16[256,2048]{1,0:T(8,128)(2,1)S(1)}, bf16[256,2048]{1,0:T(8,128)(2,1)}, u32[]{:S(2)}, u32[]{:S(2)}) %collective-permute-start) | collective-permute-done | bytes 1048608 | tf_op jit(solution)/shard_map/ppermute | solution.py:232
  60.9 6.2 fusion.18
  69.8 17.9 %attend.1 = (bf16[1024,512]{1,0:T(8,128)(2,1)}, bf16[1024,128]{1,0:T(8,128)(2,1)}, bf16[1024,128]{1,0:T(8,128)(2,1)}, bf16[1024,512]{1,0:T(8,128)(2,1)}) custom-call(f32[1024,512]{1,0:T(8,128)} %split.24.q_ref, f32[1024,128]{1,0:T(8,128)} %get-tuple-element.69.k_ref, f32[1024,128]{1,0:T(8,128)} %get-tuple-element.68.v_ref, s32[2,1,512]{2,1,0:T(1,128)} %bitcast.71, ...), custom_call_target="tpu_custom_call" | custom-call | flops 1073741824 | bytes 8388608 | tf_op jit(solution)/shard_map/attend/pallas_call | solution.py:194
  99.7 8.2 collective-permute-done.4
  116.7 16.7 %collective-permute-done.16 = bf16[256,2048]{0,1:T(8,128)(2,1)S(1)} collective-permute-done((bf16[256,2048]{0,1:T(8,128)(2,1)}, bf16[256,2048]{0,1:T(8,128)(2,1)S(1)}, u32[]{:S(2)}, u32[]{:S(2)}) %collective-permute-start.16) | collective-permute-done | bytes 1048608 | tf_op jit(solution)/shard_map/ppermute | solution.py:232
  135.2 17.7 %collective-permute-done.5 = bf16[256,2048]{1,0:T(8,128)(2,1)S(1)} collective-permute-done((bf16[256,2048]{1,0:T(8,128)(2,1)S(1)}, bf16[256,2048]{1,0:T(8,128)(2,1)S(1)}, u32[]{:S(2)}, u32[]{:S(2)}) %collective-permute-start.5) | collective-permute-done | bytes 1048608 | tf_op jit(solution)/shard_map/ppermute | solution.py:232
  167.0 7.4 collective-permute-done.18
  175.2 14.7 %collective-permute-done.19 = bf16[128,2048]{0,1:T(8,128)(2,1)S(1)} collective-permute-done((bf16[128,2048]{0,1:T(8,128)(2,1)S(1)}, bf16[128,2048]{0,1:T(8,128)(2,1)S(1)}, u32[]{:S(2)}, u32[]{:S(2)}) %collective-permute-start.19) | collective-permute-done | bytes 524320 | tf_op jit(solution)/shard_map/ppermute | solution.py:232
  213.7 14.5 %fusion.19 = f32[1024,2048]{1,0:T(8,128)} fusion(bf16[1024,2048]{0,1:T(8,128)(2,1)} %constant_dynamic-update-slice_fusion.10, bf16[2048,2048]{1,0:T(8,128)(2,1)} %all-gather.10.cloned.1.call-done), kind=kOutput, calls=%fused_computation.124 | convolution fusion | flops 8589934592 | bytes 20971520 | tf_op jit(solution)/shard_map/dot_general | solution.py:50
  228.2 17.7 %all-gather.12.cloned.1.call-done = bf16[2048,2048]{1,0:T(8,128)(2,1)} async-done(((bf16[256,2048]{1,0:T(8,128)(2,1)}), bf16[2048,2048]{1,0:T(8,128)(2,1)}) %all-gather.12.cloned.1.call-update) | async-done | bytes 8388624 | tf_op jit(solution)/shard_map/all_gather | solution.py:345
  246.0 14.7 %fusion.20 = f32[1024,2048]{1,0:T(8,128)} fusion(bf16[1024,2048]{0,1:T(8,128)(2,1)} %constant_dynamic-update-slice_fusion.10, bf16[2048,2048]{1,0:T(8,128)(2,1)} %all-gather.12.cloned.1.call-done), kind=kOutput, calls=%fused_computation.125 | convolution fusion | flops 8589934592 | bytes 20971520 | tf_op jit(solution)/shard_map/dot_general | solution.py:50
  260.7 67.3 %all-gather.14.cloned.1.call-done = bf16[2048,2048]{1,0:T(8,128)(2,1)} async-done(((bf16[256,2048]{1,0:T(8,128)(2,1)}), bf16[2048,2048]{1,0:T(8,128)(2,1)}) %all-gather.14.cloned.1.call-update) | async-done | bytes 8388624 | tf_op jit(solution)/shard_map/all_gather | solution.py:345
  328.0 22.7 %multiply_convert_fusion = (bf16[1024,2048]{1,0:T(8,128)(2,1)}, bf16[1024,2048]{1,0:T(8,128)(2,1)}, bf16[1024,2048]{1,0:T(8,128)(2,1)}) fusion(f32[1024,2048]{1,0:T(8,128)} %fusion.19, f32[1024,2048]{1,0:T(8,128)} %fusion.20, bf16[1024,2048]{0,1:T(8,128)(2,1)} %constant_dynamic-update-slice_fusion.5, bf16[2048,2048]{1,0:T(8,128)(2,1)} %all-gather.14.cloned.1.call-done), kind=kOutput, calls=%fused_computation.4 | convolution fusion | flops 8621391872 | bytes 41943040 | tf_op jit(solution)/shard_map/dot_general | solution.py:50
  350.7 14.8 %fusion.21 = f32[1024,2048]{1,0:T(8,128)} fusion(bf16[1024,2048]{1,0:T(8,128)(2,1)} %get-tuple-element.34, bf16[2048,2048]{1,0:T(8,128)(2,1)} %all-gather.10.cloned.1.call-done), kind=kOutput, calls=%fused_computation.126 | convolution fusion | flops 8589934592 | bytes 20971520 | tf_op jit(solution)/shard_map/dot_general | solution.py:44
  365.5 13.8 %add_convert_fusion.3 = bf16[1024,2048]{1,0:T(8,128)(2,1)S(1)} fusion(f32[1024,2048]{1,0:T(8,128)} %fusion.21, bf16[1024,2048]{1,0:T(8,128)(2,1)} %get-tuple-element.33, bf16[2048,2048]{1,0:T(8,128)(2,1)} %all-gather.12.cloned.1.call-done), kind=kOutput, calls=%fused_computation.3 | convolution fusion | flops 8594128896 | bytes 25165824 | tf_op jit(solution)/shard_map/dot_general | solution.py:44
  382.6 11.1 %convolution_convert_fusion = bf16[1024,2048]{1,0:T(8,128)(2,1)S(1)} fusion(bf16[1024,2048]{1,0:T(8,128)(2,1)} %get-tuple-element.35, bf16[2048,2048]{1,0:T(8,128)(2,1)S(1)} %bitcast.77), kind=kOutput, calls=%fused_computation.15 | convolution fusion | flops 8592031744 | bytes 16777216 | tf_op jit(solution)/shard_map/dot_general | solution.py:44
  398.9 10.0 %collective-permute-done.12 = bf16[128,2048]{1,0:T(8,128)(2,1)S(1)} collective-permute-done((bf16[128,2048]{1,0:T(8,128)(2,1)S(1)}, bf16[128,2048]{1,0:T(8,128)(2,1)S(1)}, u32[]{:S(2)}, u32[]{:S(2)}) %collective-permute-start.12) | collective-permute-done | bytes 524320 | tf_op jit(solution)/shard_map/ppermute | solution.py:232
  412.2 19.6 %collective-permute-done.21 = bf16[256,2048]{1,0:T(8,128)(2,1)S(1)} collective-permute-done((bf16[256,2048]{1,0:T(8,128)(2,1)S(1)}, bf16[256,2048]{1,0:T(8,128)(2,1)S(1)}, u32[]{:S(2)}, u32[]{:S(2)}) %collective-permute-start.21) | collective-permute-done | bytes 1048608 | tf_op jit(solution)/shard_map/ppermute | solution.py:232
  432.8 19.9 %collective-permute-done.13 = bf16[256,2048]{1,0:T(8,128)(2,1)S(1)} collective-permute-done((bf16[256,2048]{1,0:T(8,128)(2,1)S(1)}, bf16[256,2048]{1,0:T(8,128)(2,1)S(1)}, u32[]{:S(2)}, u32[]{:S(2)}) %collective-permute-start.13) | collective-permute-done | bytes 1048608 | tf_op jit(solution)/shard_map/ppermute | solution.py:232
  468.9 11.0 %collective-permute-done.24 = bf16[256,2048]{1,0:T(8,128)(2,1)S(1)} collective-permute-done((bf16[256,2048]{1,0:T(8,128)(2,1)}, bf16[256,2048]{1,0:T(8,128)(2,1)S(1)}, u32[]{:S(2)}, u32[]{:S(2)}) %collective-permute-start.24) | collective-permute-done | bytes 1048608 | tf_op jit(solution)/shard_map/ppermute | solution.py:232
  500.4 6.5 constant_dynamic-slice_fusion.2
  521.6 23.0 %attend_back.1 = (bf16[1024,512]{1,0:T(8,128)(2,1)}, f32[1024,128]{1,0:T(8,128)}, bf16[1024,128]{1,0:T(8,128)(2,1)}) custom-call(bf16[1024,512]{1,0:T(8,128)(2,1)} %get-tuple-element.19.q_ref, bf16[1024,128]{1,0:T(8,128)(2,1)} %get-tuple-element.20.k_ref, bf16[1024,128]{1,0:T(8,128)(2,1)} %get-tuple-element.21.v_ref, ...), custom_call_target="tpu_custom_call" | custom-call | flops 2684354560 | bytes 8388608 | tf_op jit(solution)/shard_map/attend_back/pallas_call | solution.py:215
  561.1 9.2 %add_convert_fusion = bf16[1024,2048]{1,0:T(8,128)(2,1)} fusion(bf16[1024,2048]{1,0:T(8,128)(2,1)} %collective-permute-done.36, bf16[1024,1024]{0,1:T(8,128)(2,1)S(1)} %bitcast.55, bf16[1024,2048]{1,0:T(8,128)(2,1)} %get-tuple-element.35), kind=kOutput, calls=%fused_computation | convolution fusion | flops 4301258752 | bytes 14680064 | tf_op jit(solution)/shard_map/dot_general | solution.py:38
  570.4 7.5 convolution_convert_fusion.4
  578.3 6.8 collective-permute-done.35
  591.3 7.5 convolution_convert_fusion.5
  599.3 6.8 collective-permute-done.34
  606.1 6.3 add_convert_fusion.2
  620.6 13.0 %collective-permute-done.28 = bf16[128,2048]{1,0:T(8,128)(2,1)S(1)} collective-permute-done((bf16[128,2048]{1,0:T(8,128)(2,1)S(1)}, bf16[128,2048]{1,0:T(8,128)(2,1)S(1)}, u32[]{:S(2)}, u32[]{:S(2)}) %collective-permute-start.28) | collective-permute-done | bytes 524320 | tf_op jit(solution)/shard_map/ppermute | solution.py:232
  636.8 22.2 %collective-permute-done.29 = bf16[256,2048]{1,0:T(8,128)(2,1)S(1)} collective-permute-done((bf16[256,2048]{1,0:T(8,128)(2,1)S(1)}, bf16[256,2048]{1,0:T(8,128)(2,1)S(1)}, u32[]{:S(2)}, u32[]{:S(2)}) %collective-permute-start.29) | collective-permute-done | bytes 1048608 | tf_op jit(solution)/shard_map/ppermute | solution.py:232
  693.8 76.8 %reduce-scatter.12.cloned.1.call-done = bf16[256,2048]{1,0:T(8,128)(2,1)} async-done(((bf16[1024,2048]{1,0:T(8,128)(2,1)}), bf16[256,2048]{1,0:T(8,128)(2,1)}) %reduce-scatter.12.cloned.1.call-update) | async-done | bytes 1048592 | tf_op jit(solution)/shard_map/reduce_scatter | solution.py:316
  773.4 76.7 %reduce-scatter.10.cloned.1.call-done = bf16[256,2048]{1,0:T(8,128)(2,1)} async-done(((bf16[1024,2048]{1,0:T(8,128)(2,1)}), bf16[256,2048]{1,0:T(8,128)(2,1)}) %reduce-scatter.10.cloned.1.call-update) | async-done | bytes 1048592 | tf_op jit(solution)/shard_map/reduce_scatter | solution.py:316
  (271 shorter events, 240.4 us)
Async XLA Ops:
  7.2 53.7 %all-gather.6.cloned.1.call-start = ((), (), s32[]{:S(2)}) async-start(), calls=%async_computation.5 | async-start | bytes 3538944 | tf_op jit(solution)/shard_map/all_gather | solution.py:345
  9.1 78.6 %all-gather.8.cloned.1.call-start = ((), (), s32[]{:S(2)}) async-start(), calls=%async_computation.6 | async-start | bytes 2359296 | tf_op jit(solution)/shard_map/all_gather | solution.py:345
  9.9 203.8 %all-gather.10.cloned.1.call-start = ((), (), s32[]{:S(2)}) async-start(), calls=%async_computation.7 | async-start | bytes 9437184 | tf_op jit(solution)/shard_map/all_gather | solution.py:345
  10.6 235.3 %all-gather.12.cloned.1.call-start = ((), (), s32[]{:S(2)}) async-start(), calls=%async_computation.8 | async-start | bytes 9437184 | tf_op jit(solution)/shard_map/all_gather | solution.py:345
  11.2 316.8 %all-gather.14.cloned.1.call-start = ((), (), s32[]{:S(2)}) async-start(), calls=%async_computation.9 | async-start | bytes 9437184 | tf_op jit(solution)/shard_map/all_gather | solution.py:345
  11.8 668.1 %reduce-scatter.8.cloned.1.call-start = ((), (), s32[]{:S(2)}) async-start(), calls=%async_computation.11 | async-start | bytes 1310720 | tf_op jit(solution)/shard_map/reduce_scatter | solution.py:316
  13.0 26.3 %collective-permute-start = (bf16[256,2048]{1,0:T(8,128)(2,1)S(1)}, bf16[256,2048]{1,0:T(8,128)(2,1)}, u32[]{:S(2)}, u32[]{:S(2)}) collective-permute-start(bf16[256,2048]{1,0:T(8,128)(2,1)S(1)} %fusion.3), channel_id=1, source_target_pairs={{0,1},{1,0},{2,3},{3,2},{4,5},{5,4},{6,7},{7,6},{8,9},{9,8},{10,11... | collective-permute-start | bytes 3145736 | tf_op jit(solution)/shard_map/ppermute | solution.py:232
  16.1 26.9 %collective-permute-start.1 = (bf16[256,2048]{1,0:T(8,128)(2,1)S(1)}, bf16[256,2048]{1,0:T(8,128)(2,1)}, u32[]{:S(2)}, u32[]{:S(2)}) collective-permute-start(bf16[256,2048]{1,0:T(8,128)(2,1)S(1)} %fusion.3), channel_id=1, source_target_pairs={{0,2},{1,3},{2,0},{3,1},{4,6},{5,7},{6,4},{7,5},{8,10},{9,11},{10,... | collective-permute-start | bytes 3145736 | tf_op jit(solution)/shard_map/ppermute | solution.py:232
  99.1 34.3 %collective-permute-start.16 = (bf16[256,2048]{0,1:T(8,128)(2,1)}, bf16[256,2048]{0,1:T(8,128)(2,1)S(1)}, u32[]{:S(2)}, u32[]{:S(2)}) collective-permute-start(bf16[256,2048]{0,1:T(8,128)(2,1)} %copy.36), channel_id=1, source_target_pairs={{0,1},{1,0},{2,3},{3,2},{4,5},{5,4},{6,7},{7,6},{8,9},{9,8},{10,11... | collective-permute-start | bytes 3145736 | tf_op jit(solution)/shard_map/ppermute | solution.py:232
  113.0 39.9 %collective-permute-start.5 = (bf16[256,2048]{1,0:T(8,128)(2,1)S(1)}, bf16[256,2048]{1,0:T(8,128)(2,1)S(1)}, u32[]{:S(2)}, u32[]{:S(2)}) collective-permute-start(bf16[256,2048]{1,0:T(8,128)(2,1)S(1)} %pad_maximum_fusion.1), channel_id=1, source_target_pairs={{0,1},{1,0},{2,3},{3,2},{4,5},{5,4},{6,7},{7,6},{8,9},{9,8},{10,11... | collective-permute-start | bytes 3145736 | tf_op jit(solution)/shard_map/ppermute | solution.py:232
  114.6 38.3 %collective-permute-start.7 = (bf16[256,2048]{1,0:T(8,128)(2,1)S(1)}, bf16[256,2048]{1,0:T(8,128)(2,1)S(1)}, u32[]{:S(2)}, u32[]{:S(2)}) collective-permute-start(bf16[256,2048]{1,0:T(8,128)(2,1)S(1)} %pad_maximum_fusion.2), channel_id=1, source_target_pairs={{0,2},{1,3},{2,0},{3,1},{4,6},{5,7},{6,4},{7,5},{8,10},{9,11},{10,... | collective-permute-start | bytes 3145736 | tf_op jit(solution)/shard_map/ppermute | solution.py:232
  116.4 47.3 %collective-permute-start.17 = (bf16[256,2048]{0,1:T(8,128)(2,1)}, bf16[256,2048]{0,1:T(8,128)(2,1)S(1)}, u32[]{:S(2)}, u32[]{:S(2)}) collective-permute-start(bf16[256,2048]{0,1:T(8,128)(2,1)} %copy.36), channel_id=1, source_target_pairs={{0,2},{1,3},{2,0},{3,1},{4,6},{5,7},{6,4},{7,5},{8,10},{9,11},{10,... | collective-permute-start | bytes 3145736 | tf_op jit(solution)/shard_map/ppermute | solution.py:232
  133.4 41.0 %collective-permute-start.18 = (bf16[128,2048]{0,1:T(8,128)(2,1)S(1)}, bf16[128,2048]{0,1:T(8,128)(2,1)S(1)}, u32[]{:S(2)}, u32[]{:S(2)}) collective-permute-start(bf16[128,2048]{0,1:T(8,128)(2,1)S(1)} %slice.44), channel_id=1, source_target_pairs={{0,2},{1,3},{2,0},{3,1},{4,6},{5,7},{6,4},{7,5},{8,10},{9,11},{10,... | collective-permute-start | bytes 1572872 | tf_op jit(solution)/shard_map/ppermute | solution.py:232
  156.1 36.1 %collective-permute-start.8 = (bf16[256,2048]{1,0:T(8,128)(2,1)}, bf16[256,2048]{1,0:T(8,128)(2,1)}, u32[]{:S(2)}, u32[]{:S(2)}) collective-permute-start(bf16[256,2048]{1,0:T(8,128)(2,1)} %multiply_convert_fusion.4), channel_id=1, source_target_pairs={{0,1},{1,0},{2,3},{3,2},{4,5},{5,4},{6,7},{7,6},{8,9},{9,8},{10,11... | collective-permute-start | bytes 3145736 | tf_op jit(solution)/shard_map/ppermute | solution.py:232
  157.1 38.4 %collective-permute-start.9 = (bf16[256,2048]{1,0:T(8,128)(2,1)}, bf16[256,2048]{1,0:T(8,128)(2,1)}, u32[]{:S(2)}, u32[]{:S(2)}) collective-permute-start(bf16[256,2048]{1,0:T(8,128)(2,1)} %multiply_convert_fusion.4), channel_id=1, source_target_pairs={{0,2},{1,3},{2,0},{3,1},{4,6},{5,7},{6,4},{7,5},{8,10},{9,11},{10,... | collective-permute-start | bytes 3145736 | tf_op jit(solution)/shard_map/ppermute | solution.py:232
  163.7 26.2 %collective-permute-start.19 = (bf16[128,2048]{0,1:T(8,128)(2,1)S(1)}, bf16[128,2048]{0,1:T(8,128)(2,1)S(1)}, u32[]{:S(2)}, u32[]{:S(2)}) collective-permute-start(bf16[128,2048]{0,1:T(8,128)(2,1)S(1)} %slice.45), channel_id=1, source_target_pairs={{0,1},{1,0},{2,3},{3,2},{4,5},{5,4},{6,7},{7,6},{8,9},{9,8},{10,11... | collective-permute-start | bytes 1572872 | tf_op jit(solution)/shard_map/ppermute | solution.py:232
  194.2 15.2 %collective-permute-start.10 = (bf16[128,2048]{1,0:T(8,128)(2,1)}, bf16[128,2048]{1,0:T(8,128)(2,1)}, u32[]{:S(2)}, u32[]{:S(2)}) collective-permute-start(bf16[128,2048]{1,0:T(8,128)(2,1)} %slice.42), channel_id=1, source_target_pairs={{0,2},{1,3},{2,0},{3,1},{4,6},{5,7},{6,4},{7,5},{8,10},{9,11},{10,... | collective-permute-start | bytes 1572872 | tf_op jit(solution)/shard_map/ppermute | solution.py:232
  379.5 15.6 %collective-permute-start.20 = (bf16[128,2048]{1,0:T(8,128)(2,1)S(1)}, bf16[128,2048]{1,0:T(8,128)(2,1)S(1)}, u32[]{:S(2)}, u32[]{:S(2)}) collective-permute-start(bf16[128,2048]{1,0:T(8,128)(2,1)S(1)} %get-tuple-element.53), channel_id=1, source_target_pairs={{0,2},{1,3},{2,0},{3,1},{4,6},{5,7},{6,4},{7,5},{8,10},{9,11},{10,... | collective-permute-start | bytes 1572872 | tf_op jit(solution)/shard_map/ppermute | solution.py:232
  395.7 36.2 %collective-permute-start.21 = (bf16[256,2048]{1,0:T(8,128)(2,1)S(1)}, bf16[256,2048]{1,0:T(8,128)(2,1)S(1)}, u32[]{:S(2)}, u32[]{:S(2)}) collective-permute-start(bf16[256,2048]{1,0:T(8,128)(2,1)S(1)} %pad_maximum_fusion.5), channel_id=1, source_target_pairs={{0,1},{1,0},{2,3},{3,2},{4,5},{5,4},{6,7},{7,6},{8,9},{9,8},{10,11... | collective-permute-start | bytes 3145736 | tf_op jit(solution)/shard_map/ppermute | solution.py:232
  397.3 34.5 %collective-permute-start.23 = (bf16[256,2048]{1,0:T(8,128)(2,1)S(1)}, bf16[256,2048]{1,0:T(8,128)(2,1)S(1)}, u32[]{:S(2)}, u32[]{:S(2)}) collective-permute-start(bf16[256,2048]{1,0:T(8,128)(2,1)S(1)} %pad_maximum_fusion.6), channel_id=1, source_target_pairs={{0,2},{1,3},{2,0},{3,1},{4,6},{5,7},{6,4},{7,5},{8,10},{9,11},{10,... | collective-permute-start | bytes 3145736 | tf_op jit(solution)/shard_map/ppermute | solution.py:232
  409.9 42.8 %collective-permute-start.13 = (bf16[256,2048]{1,0:T(8,128)(2,1)S(1)}, bf16[256,2048]{1,0:T(8,128)(2,1)S(1)}, u32[]{:S(2)}, u32[]{:S(2)}) collective-permute-start(bf16[256,2048]{1,0:T(8,128)(2,1)S(1)} %pad_maximum_fusion.3), channel_id=1, source_target_pairs={{0,1},{1,0},{2,3},{3,2},{4,5},{5,4},{6,7},{7,6},{8,9},{9,8},{10,11... | collective-permute-start | bytes 3145736 | tf_op jit(solution)/shard_map/ppermute | solution.py:232
  410.7 42.1 %collective-permute-start.15 = (bf16[256,2048]{1,0:T(8,128)(2,1)S(1)}, bf16[256,2048]{1,0:T(8,128)(2,1)S(1)}, u32[]{:S(2)}, u32[]{:S(2)}) collective-permute-start(bf16[256,2048]{1,0:T(8,128)(2,1)S(1)} %pad_maximum_fusion.4), channel_id=1, source_target_pairs={{0,2},{1,3},{2,0},{3,1},{4,6},{5,7},{6,4},{7,5},{8,10},{9,11},{10,... | collective-permute-start | bytes 3145736 | tf_op jit(solution)/shard_map/ppermute | solution.py:232
  456.1 23.8 %collective-permute-start.24 = (bf16[256,2048]{1,0:T(8,128)(2,1)}, bf16[256,2048]{1,0:T(8,128)(2,1)S(1)}, u32[]{:S(2)}, u32[]{:S(2)}) collective-permute-start(bf16[256,2048]{1,0:T(8,128)(2,1)} %get-tuple-element.29), channel_id=1, source_target_pairs={{0,1},{1,0},{2,3},{3,2},{4,5},{5,4},{6,7},{7,6},{8,9},{9,8},{10,11... | collective-permute-start | bytes 3145736 | tf_op jit(solution)/shard_map/ppermute | solution.py:232
  456.6 29.2 %collective-permute-start.25 = (bf16[256,2048]{1,0:T(8,128)(2,1)}, bf16[256,2048]{1,0:T(8,128)(2,1)S(1)}, u32[]{:S(2)}, u32[]{:S(2)}) collective-permute-start(bf16[256,2048]{1,0:T(8,128)(2,1)} %get-tuple-element.29), channel_id=1, source_target_pairs={{0,2},{1,3},{2,0},{3,1},{4,6},{5,7},{6,4},{7,5},{8,10},{9,11},{10,... | collective-permute-start | bytes 3145736 | tf_op jit(solution)/shard_map/ppermute | solution.py:232
  508.1 37.5 %collective-permute-start.33 = (bf16[1024,512]{1,0:T(8,128)(2,1)S(1)}, bf16[1024,512]{1,0:T(8,128)(2,1)S(1)}, u32[]{:S(2)}, u32[]{:S(2)}) collective-permute-start(bf16[1024,512]{1,0:T(8,128)(2,1)S(1)} %convolution_convert_fusion.7), channel_id=1, source_target_pairs={{0,4},{4,0},{8,12},{12,8},{16,20},{20,16},{24,28},{28,24},{1,5},{5... | collective-permute-start | bytes 3145736 | tf_op jit(solution)/shard_map/ppermute | solution.py:232
  515.9 45.1 %collective-permute-start.36 = (bf16[1024,2048]{1,0:T(8,128)(2,1)}, bf16[1024,2048]{1,0:T(8,128)(2,1)}, u32[]{:S(2)}, u32[]{:S(2)}) collective-permute-start(bf16[1024,2048]{1,0:T(8,128)(2,1)} %convolution_convert_fusion.3), channel_id=1, source_target_pairs={{0,4},{4,0},{8,12},{12,8},{16,20},{20,16},{24,28},{28,24},{1,5},{5... | collective-permute-start | bytes 12582920 | tf_op jit(solution)/shard_map/ppermute | solution.py:232
  551.2 130.6 %reduce-scatter.6.cloned.1.call-start = ((), (), s32[]{:S(2)}) async-start(), calls=%async_computation.10 | async-start | bytes 1966080 | tf_op jit(solution)/shard_map/reduce_scatter | solution.py:316
  561.0 130.0 %reduce-scatter.14.cloned.1.call-start = ((), (), s32[]{:S(2)}) async-start(), calls=%async_computation.14 | async-start | bytes 5242880 | tf_op jit(solution)/shard_map/reduce_scatter | solution.py:316
  570.3 200.3 %reduce-scatter.12.cloned.1.call-start = ((), (), s32[]{:S(2)}) async-start(), calls=%async_computation.13 | async-start | bytes 5242880 | tf_op jit(solution)/shard_map/reduce_scatter | solution.py:316
  591.3 258.8 %reduce-scatter.10.cloned.1.call-start = ((), (), s32[]{:S(2)}) async-start(), calls=%async_computation.12 | async-start | bytes 5242880 | tf_op jit(solution)/shard_map/reduce_scatter | solution.py:316
  634.5 24.4 %collective-permute-start.29 = (bf16[256,2048]{1,0:T(8,128)(2,1)S(1)}, bf16[256,2048]{1,0:T(8,128)(2,1)S(1)}, u32[]{:S(2)}, u32[]{:S(2)}) collective-permute-start(bf16[256,2048]{1,0:T(8,128)(2,1)S(1)} %pad_maximum_fusion.7), channel_id=1, source_target_pairs={{0,1},{1,0},{2,3},{3,2},{4,5},{5,4},{6,7},{7,6},{8,9},{9,8},{10,11... | collective-permute-start | bytes 3145736 | tf_op jit(solution)/shard_map/ppermute | solution.py:232
  635.2 24.2 %collective-permute-start.31 = (bf16[256,2048]{1,0:T(8,128)(2,1)S(1)}, bf16[256,2048]{1,0:T(8,128)(2,1)S(1)}, u32[]{:S(2)}, u32[]{:S(2)}) collective-permute-start(bf16[256,2048]{1,0:T(8,128)(2,1)S(1)} %pad_maximum_fusion.8), channel_id=1, source_target_pairs={{0,2},{1,3},{2,0},{3,1},{4,6},{5,7},{6,4},{7,5},{8,10},{9,11},{10,... | collective-permute-start | bytes 3145736 | tf_op jit(solution)/shard_map/ppermute | solution.py:232
  (52 other events, 696.4 us)
Sparse Core Ops, SparseCore 0:
  10.2 40.9 all-gather.5
  52.8 28.0 all-gather.7
  82.5 81.4 all-gather.9
  165.4 80.5 all-gather.11
  247.4 80.5 all-gather.13
  551.3 24.1 reduce-scatter.7
  578.4 33.9 reduce-scatter.5
  614.6 76.3 reduce-scatter.13
  693.3 77.2 reduce-scatter.11
  772.8 77.2 reduce-scatter.9

commit v3 on v2

--- a/solution.py
+++ b/solution.py
@@ -308,13 +308,17 @@
     return pick(mine), pick(1 - mine)
 
 
-def weight_grad(parities, right_side, size):
+def pair_grad(parities, right_side, size):
     mine, other = parities
     from_pair = swap(contract_rows(other, right_side).astype(jnp.bfloat16), "dp", size, 1)
     pair_sum = contract_rows(mine, right_side) + from_pair.astype(jnp.float32)
+    return pair_sum.astype(jnp.bfloat16)
+
+
+def sum_pairs(pair_sum, size):
     groups = [list(range(0, size, 2)), list(range(1, size, 2))]
     return lax.psum_scatter(
-        pair_sum.astype(jnp.bfloat16),
+        pair_sum,
         "dp",
         scatter_dimension=0,
         tiled=True,
@@ -376,38 +380,56 @@
     sigmoid_gate = jax.nn.sigmoid(gate_pre)
     silu_gate = gate_pre * sigmoid_gate
     hidden = (silu_gate * up_pre).astype(jnp.bfloat16)
-    grad_down = weight_grad(parity_columns(grad_full, dp), hidden, dp)
+    pair_down = pair_grad(parity_columns(grad_full, dp), hidden, dp)
+    pair_down, down_full = lax.optimization_barrier((pair_down, down_full))
+    grad_down = sum_pairs(pair_down, dp)
 
     grad_hidden = matmul(grad_full, down_full)
     grad_gate_pre = (
         grad_hidden * up_pre * sigmoid_gate * (1.0 + gate_pre * (1.0 - sigmoid_gate))
     ).astype(jnp.bfloat16)
     grad_up_pre = (grad_hidden * silu_gate).astype(jnp.bfloat16)
+    grad_normed_part = (
+        contract_cols(grad_gate_pre, gate_full) + contract_cols(grad_up_pre, up_full)
+    ).astype(jnp.bfloat16)
+    grad_normed_part, grad_gate_pre, grad_up_pre = lax.optimization_barrier(
+        (grad_normed_part, grad_gate_pre, grad_up_pre)
+    )
     normed_two_parities = parity_columns(normed_two, dp)
-    grad_gate = weight_grad(normed_two_parities, grad_gate_pre, dp)
-    grad_up = weight_grad(normed_two_parities, grad_up_pre, dp)
-    grad_normed_own = sum_rows(
-        contract_cols(grad_gate_pre, gate_full) + contract_cols(grad_up_pre, up_full), tp
-    )
-    block_output = (residual_own + sum_rows(contract_cols(hidden, down_full), tp)).astype(
-        jnp.bfloat16
-    )
+    pair_gate = pair_grad(normed_two_parities, grad_gate_pre, dp)
+    pair_up = pair_grad(normed_two_parities, grad_up_pre, dp)
+    grad_normed_own = sum_rows(grad_normed_part, tp)
+    grad_normed_own, pair_gate, pair_up = lax.optimization_barrier(
+        (grad_normed_own, pair_gate, pair_up)
+    )
+    grad_gate = sum_pairs(pair_gate, dp)
+    grad_up = sum_pairs(pair_up, dp)
     grad_mlp_gain = jnp.sum(grad_normed_own * residual_own * scale_two_own, axis=0)
     grad_residual_own = cotangent.astype(jnp.float32) + norm_back(
         grad_normed_own, residual_own, scale_two_own, mlp_gain
     )
     grad_residual_bf = gather_rows(grad_residual_own.astype(jnp.bfloat16), tp)
-    grad_out = weight_grad(parity_columns(grad_residual_bf, dp), mixed_all, dp)
+    grad_residual_bf, hidden = lax.optimization_barrier((grad_residual_bf, hidden))
     grad_mixed = (matmul(grad_residual_bf, out_full) * live_all[:, None]).astype(jnp.bfloat16)
+    block_output = (residual_own + sum_rows(contract_cols(hidden, down_full), tp)).astype(
+        jnp.bfloat16
+    )
     grad_query_rows, grad_keys, grad_value_rows = attend_back(
         query_rows, key_rows, value_rows, grad_mixed, doc_row, doc_col, tables
     )
     grad_qkv_rows = jnp.concatenate(
         [grad_query_rows, grad_keys.astype(jnp.bfloat16), grad_value_rows], axis=1
     )
-    grad_qkv = weight_grad(parity_columns(normed_one, dp), grad_qkv_rows, dp)
+    grad_one_part = contract_cols(grad_qkv_rows, qkv_full).astype(jnp.bfloat16)
+    grad_one_part, grad_qkv_rows, mixed_all = lax.optimization_barrier(
+        (grad_one_part, grad_qkv_rows, mixed_all)
+    )
+    pair_out = pair_grad(parity_columns(grad_residual_bf, dp), mixed_all, dp)
+    pair_qkv = pair_grad(parity_columns(normed_one, dp), grad_qkv_rows, dp)
+    grad_out = sum_pairs(pair_out, dp)
+    grad_qkv = sum_pairs(pair_qkv, dp)
     grad_query, grad_key, grad_value = jnp.split(grad_qkv, splits, axis=1)
-    grad_normed_one = sum_rows(contract_cols(grad_qkv_rows, qkv_full), tp)
+    grad_normed_one = sum_rows(grad_one_part, tp)
     grad_attn_gain = jnp.sum(grad_normed_one * input_own * scale_one, axis=0)
     input_grad = (
         grad_residual_own + norm_back(grad_normed_one, input_own, scale_one, attn_gain)

time: 870 us -> 796 us (0.915)
  waiting for transfers between devices: 462 us -> 376 us
  other arithmetic: 29.2 us -> 40.5 us
    reduce_scatter x5, waiting for transfers between devices: 159 us -> 117 us  [sum_pairs(): lax.psum_scatter(pair_sum, 'dp', scatter_dimension=0, tiled=True, axis_in...]
    ppermute x42, waiting for transfers between devices: 215 us -> 183 us  [swap(): return lax.ppermute(array, axis, [(i, i ^ bit) for i in range(size)])]
    all_gather x5, waiting for transfers between devices: 85 us -> 73.6 us  [gather(): return lax.all_gather(weight, 'dp', axis=0, tiled=True)]
  transfers between devices with their start and end apart: 52 -> 52, of which waited for: 32 -> 30; matrix products, arithmetic and copies ran while one was open for 26% -> 31% of each run, Pallas kernels for 5% -> 5%
where the time goes in v3:
time: 796 us; the launch traced here: 785 us
  waiting for transfers between devices  376 us (47%)
  matrix products  176 us (22%)
  local copies, waits for them, and re-layouts  96.4 us (12%)
  Pallas kernels  41.3 us (5%)
  starting transfers between devices  40.6 us (5%)
  other arithmetic  40.5 us (5%)
  between operations  15.1 us (2%)
    ppermute x42, waiting for transfers between devices, swap(): return lax.ppermute(array, axis, [(i, i ^ bit) for i in range(size)])  183 us
    reduce_scatter x5, waiting for transfers between devices, sum_pairs(): lax.psum_scatter(pair_sum, 'dp', scatter_dimension=0, tiled=True, axis_in...  117 us
    all_gather x5, waiting for transfers between devices, gather(): return lax.all_gather(weight, 'dp', axis=0, tiled=True)  73.6 us
    dot_general x5, matrix products, matmul(): return jnp.dot(left_side, right_side, preferred_element_type=jnp.float32)  64.9 us
    dot_general x10, matrix products, contract_rows(): lax.dot_general(left_side, right_side, (((0,), (0,)), ((), ())), preferre...  57.5 us
    dot_general x5, matrix products, contract_cols(): lax.dot_general(left_side, right_side, (((1,), (1,)), ((), ())), preferre...  53.1 us
    ppermute x42, starting transfers between devices, swap(): return lax.ppermute(array, axis, [(i, i ^ bit) for i in range(size)])  39.6 us
    pallas_call x1, Pallas kernels, attend_back(): pl.pallas_call(functools.partial(attend_back_kernel, groups), name='atten...  23.4 us
  transfers between devices with their start and end apart: 52, of which 30 were waited for; matrix products, arithmetic and copies ran while one was open for 31% of the time, Pallas kernels for 5%

profile of v3, /device:TPU:0, one launch (start us, length us, event | category | flops | bytes accessed | tf_op | source)
XLA Modules:
  0.0 785.4 jit_solution(5527526204349746368)
XLA Ops:
  22.7 16.1 %collective-permute-done = bf16[256,2048]{1,0:T(8,128)(2,1)} collective-permute-done((bf16[256,2048]{1,0:T(8,128)(2,1)S(1)}, bf16[256,2048]{1,0:T(8,128)(2,1)}, u32[]{:S(2)}, u32[]{:S(2)}) %collective-permute-start) | collective-permute-done | bytes 1048608 | tf_op jit(solution)/shard_map/ppermute | solution.py:232
  60.3 6.2 fusion.17
  69.2 17.9 %attend.1 = (bf16[1024,512]{1,0:T(8,128)(2,1)}, bf16[1024,128]{1,0:T(8,128)(2,1)}, bf16[1024,128]{1,0:T(8,128)(2,1)}, bf16[1024,512]{1,0:T(8,128)(2,1)}) custom-call(f32[1024,512]{1,0:T(8,128)} %split.24.q_ref, f32[1024,128]{1,0:T(8,128)} %get-tuple-element.94.k_ref, f32[1024,128]{1,0:T(8,128)} %get-tuple-element.93.v_ref, s32[2,1,512]{2,1,0:T(1,128)} %bitcast.73, ...), custom_call_target="tpu_custom_call" | custom-call | flops 1073741824 | bytes 8388608 | tf_op jit(solution)/shard_map/attend/pallas_call | solution.py:194
  97.7 10.5 %collective-permute-done.4 = bf16[128,2048]{1,0:T(8,128)(2,1)} collective-permute-done((bf16[128,2048]{1,0:T(8,128)(2,1)}, bf16[128,2048]{1,0:T(8,128)(2,1)}, u32[]{:S(2)}, u32[]{:S(2)}) %collective-permute-start.4) | collective-permute-done | bytes 524320 | tf_op jit(solution)/shard_map/ppermute | solution.py:232
  120.6 11.3 %collective-permute-done.8 = bf16[256,2048]{0,1:T(8,128)(2,1)S(1)} collective-permute-done((bf16[256,2048]{0,1:T(8,128)(2,1)S(1)}, bf16[256,2048]{0,1:T(8,128)(2,1)S(1)}, u32[]{:S(2)}, u32[]{:S(2)}) %collective-permute-start.8) | collective-permute-done | bytes 1048608 | tf_op jit(solution)/shard_map/ppermute | solution.py:232
  135.1 19.3 %collective-permute-done.5 = bf16[256,2048]{1,0:T(8,128)(2,1)} collective-permute-done((bf16[256,2048]{1,0:T(8,128)(2,1)}, bf16[256,2048]{1,0:T(8,128)(2,1)}, u32[]{:S(2)}, u32[]{:S(2)}) %collective-permute-start.5) | collective-permute-done | bytes 1048608 | tf_op jit(solution)/shard_map/ppermute | solution.py:232
  171.7 14.1 %collective-permute-done.12 = bf16[256,2048]{1,0:T(8,128)(2,1)} collective-permute-done((bf16[256,2048]{1,0:T(8,128)(2,1)S(1)}, bf16[256,2048]{1,0:T(8,128)(2,1)}, u32[]{:S(2)}, u32[]{:S(2)}) %collective-permute-start.12) | collective-permute-done | bytes 1048608 | tf_op jit(solution)/shard_map/ppermute | solution.py:232
  203.8 14.8 %fusion.18 = f32[1024,2048]{1,0:T(8,128)} fusion(bf16[1024,2048]{0,1:T(8,128)(2,1)} %constant_dynamic-update-slice_fusion.5, bf16[2048,2048]{1,0:T(8,128)(2,1)} %all-gather.10.cloned.1.call-done), kind=kOutput, calls=%fused_computation.123 | convolution fusion | flops 8589934592 | bytes 20971520 | tf_op jit(solution)/shard_map/dot_general | solution.py:50
  218.6 27.4 %all-gather.12.cloned.1.call-done = bf16[2048,2048]{1,0:T(8,128)(2,1)} async-done(((bf16[256,2048]{1,0:T(8,128)(2,1)}), bf16[2048,2048]{1,0:T(8,128)(2,1)}) %all-gather.12.cloned.1.call-update) | async-done | bytes 8388624 | tf_op jit(solution)/shard_map/all_gather | solution.py:349
  246.0 17.0 %multiply_convert_fusion.2 = (bf16[1024,2048]{1,0:T(8,128)(2,1)S(1)}, f32[1024,2048]{1,0:T(8,128)}) fusion(f32[1024,2048]{1,0:T(8,128)} %fusion.18, bf16[1024,2048]{0,1:T(8,128)(2,1)} %constant_dynamic-update-slice_fusion.5, bf16[2048,2048]{1,0:T(8,128)(2,1)} %all-gather.12.cloned.1.call-done), kind=kOutput, calls=%fused_computation.6 | convolution fusion | flops 8602517504 | bytes 33554432 | tf_op jit(solution)/shard_map/dot_general | solution.py:50
  263.0 5.1 convolution_convert_fusion.5
  275.7 6.1 add_convert_fusion.3
  281.8 46.2 %all-gather.14.cloned.1.call-done = bf16[2048,2048]{1,0:T(8,128)(2,1)} async-done(((bf16[256,2048]{1,0:T(8,128)(2,1)}), bf16[2048,2048]{1,0:T(8,128)(2,1)}) %all-gather.14.cloned.1.call-update) | async-done | bytes 8388624 | tf_op jit(solution)/shard_map/all_gather | solution.py:349
  328.0 20.7 %multiply_convert_fusion = (bf16[1024,2048]{1,0:T(8,128)(2,1)}, bf16[1024,2048]{1,0:T(8,128)(2,1)S(1)}) fusion(f32[1024,2048]{1,0:T(8,128)} %fusion.18, f32[1024,2048]{1,0:T(8,128)} %get-tuple-element.106, bf16[1024,2048]{0,1:T(8,128)(2,1)} %constant_dynamic-update-slice_fusion.10, bf16[2048,2048]{1,0:T(8,128)(2,1)} %all-gather.14.cloned.1.call-done), kind=kOutput, calls=%fused_computation.3 | convolution fusion | flops 8617197568 | bytes 37748736 | tf_op jit(solution)/shard_map/dot_general | solution.py:50
  348.7 15.1 %fusion.19 = f32[1024,2048]{1,0:T(8,128)} fusion(bf16[1024,2048]{1,0:T(8,128)(2,1)S(1)} %get-tuple-element.34, bf16[2048,2048]{1,0:T(8,128)(2,1)} %all-gather.10.cloned.1.call-done), kind=kOutput, calls=%fused_computation.124 | convolution fusion | flops 8589934592 | bytes 20971520 | tf_op jit(solution)/shard_map/dot_general | solution.py:44
  363.8 13.9 %add_convert_fusion.2 = bf16[1024,2048]{1,0:T(8,128)(2,1)S(1)} fusion(f32[1024,2048]{1,0:T(8,128)} %fusion.19, bf16[1024,2048]{1,0:T(8,128)(2,1)} %get-tuple-element.35, bf16[2048,2048]{1,0:T(8,128)(2,1)} %all-gather.12.cloned.1.call-done), kind=kOutput, calls=%fused_computation.2 | convolution fusion | flops 8594128896 | bytes 25165824 | tf_op jit(solution)/shard_map/dot_general | solution.py:44
  377.7 9.8 %convolution_convert_fusion.3 = bf16[1024,2048]{1,0:T(8,128)(2,1)} fusion(bf16[1024,1024]{0,1:T(8,128)(2,1)S(1)} %bitcast.61, bf16[1024,2048]{1,0:T(8,128)(2,1)} %get-tuple-element.35), kind=kOutput, calls=%fused_computation.18 | convolution fusion | flops 4297064448 | bytes 10485760 | tf_op jit(solution)/shard_map/dot_general | solution.py:38
  391.0 6.1 convolution_convert_fusion.4
  407.3 21.0 %collective-permute-done.18 = bf16[256,2048]{1,0:T(8,128)(2,1)} collective-permute-done((bf16[256,2048]{1,0:T(8,128)(2,1)S(1)}, bf16[256,2048]{1,0:T(8,128)(2,1)}, u32[]{:S(2)}, u32[]{:S(2)}) %collective-permute-start.18) | collective-permute-done | bytes 1048608 | tf_op jit(solution)/shard_map/ppermute | solution.py:232
  434.5 7.7 add_convert_fusion
  442.2 10.7 %add_convert_fusion.1 = bf16[1024,2048]{1,0:T(8,128)(2,1)} fusion(bf16[1024,2048]{1,0:T(8,128)(2,1)} %collective-permute-done.21, bf16[1024,1024]{0,1:T(8,128)(2,1)} %bitcast.58, bf16[1024,2048]{1,0:T(8,128)(2,1)} %copy-done.32), kind=kOutput, calls=%fused_computation.1 | convolution fusion | flops 4301258752 | bytes 14680064 | tf_op jit(solution)/shard_map/dot_general | solution.py:38
  460.5 20.7 %collective-permute-done.23 = bf16[256,2048]{1,0:T(8,128)(2,1)} collective-permute-done((bf16[256,2048]{1,0:T(8,128)(2,1)}, bf16[256,2048]{1,0:T(8,128)(2,1)}, u32[]{:S(2)}, u32[]{:S(2)}) %collective-permute-start.23) | collective-permute-done | bytes 1048608 | tf_op jit(solution)/shard_map/ppermute | solution.py:232
  501.4 6.2 multiply_convert_fusion.3.grad_ref
  507.6 23.4 %attend_back.1 = (bf16[1024,512]{1,0:T(8,128)(2,1)}, f32[1024,128]{1,0:T(8,128)}, bf16[1024,128]{1,0:T(8,128)(2,1)}) custom-call(bf16[1024,512]{1,0:T(8,128)(2,1)} %get-tuple-element.38.q_ref, bf16[1024,128]{1,0:T(8,128)(2,1)} %get-tuple-element.39.k_ref, bf16[1024,128]{1,0:T(8,128)(2,1)} %get-tuple-element.40.v_ref, ...), custom_call_target="tpu_custom_call" | custom-call | flops 2684354560 | bytes 8388608 | tf_op jit(solution)/shard_map/attend_back/pallas_call | solution.py:215
  533.5 8.3 %convolution_convert_fusion.2 = bf16[1024,2048]{1,0:T(8,128)(2,1)} fusion(bf16[2048,768]{1,0:T(8,128)(2,1)} %all-gather.6.cloned.1.call-done, bf16[1024,128]{1,0:T(8,128)(2,1)} %get-tuple-element.44, bf16[1024,128]{1,0:T(8,128)(2,1)S(1)} %convert_element_type.269, bf16[1024,512]{1,0:T(8,128)(2,1)} %get-tuple-element.42), kind=kOutput, calls=%fused_computation.17 | convolution fusion | flops 3228041216 | bytes 8912896 | tf_op jit(solution)/shard_map/dot_general | solution.py:44
  541.9 5.8 constant_dynamic-slice_fusion
  555.9 5.4 add_convert_fusion.4
  567.3 11.3 %convolution_convert_fusion = bf16[1024,2048]{1,0:T(8,128)(2,1)S(1)} fusion(bf16[1024,2048]{1,0:T(8,128)(2,1)S(1)} %copy-done.31, bf16[2048,2048]{1,0:T(8,128)(2,1)} %all-gather.14.cloned.1.call-done), kind=kOutput, calls=%fused_computation.15 | convolution fusion | flops 8592031744 | bytes 16777216 | tf_op jit(solution)/shard_map/dot_general | solution.py:44
  585.0 32.3 %collective-permute-done.27 = bf16[128,2048]{1,0:T(8,128)(2,1)S(1)} collective-permute-done((bf16[128,2048]{1,0:T(8,128)(2,1)S(1)}, bf16[128,2048]{1,0:T(8,128)(2,1)S(1)}, u32[]{:S(2)}, u32[]{:S(2)}) %collective-permute-start.27) | collective-permute-done | bytes 524320 | tf_op jit(solution)/shard_map/ppermute | solution.py:232
  634.0 9.5 %collective-permute-done.28 = bf16[256,2048]{1,0:T(8,128)(2,1)S(1)} collective-permute-done((bf16[256,2048]{1,0:T(8,128)(2,1)S(1)}, bf16[256,2048]{1,0:T(8,128)(2,1)S(1)}, u32[]{:S(2)}, u32[]{:S(2)}) %collective-permute-start.28) | collective-permute-done | bytes 1048608 | tf_op jit(solution)/shard_map/ppermute | solution.py:232
  656.3 40.0 %reduce-scatter.10.cloned.1.call-done = bf16[256,2048]{1,0:T(8,128)(2,1)} async-done(((bf16[1024,2048]{1,0:T(8,128)(2,1)}), bf16[256,2048]{1,0:T(8,128)(2,1)}) %reduce-scatter.10.cloned.1.call-update) | async-done | bytes 1048592 | tf_op jit(solution)/shard_map/reduce_scatter | solution.py:320
  699.0 76.6 %reduce-scatter.12.cloned.1.call-done = bf16[256,2048]{1,0:T(8,128)(2,1)} async-done(((bf16[1024,2048]{1,0:T(8,128)(2,1)}), bf16[256,2048]{1,0:T(8,128)(2,1)}) %reduce-scatter.12.cloned.1.call-update) | async-done | bytes 1048592 | tf_op jit(solution)/shard_map/reduce_scatter | solution.py:320
  (277 shorter events, 213.8 us)
Async XLA Ops:
  7.2 53.1 %all-gather.6.cloned.1.call-start = ((), (), s32[]{:S(2)}) async-start(), calls=%async_computation.5 | async-start | bytes 3538944 | tf_op jit(solution)/shard_map/all_gather | solution.py:349
  9.1 78.0 %all-gather.8.cloned.1.call-start = ((), (), s32[]{:S(2)}) async-start(), calls=%async_computation.6 | async-start | bytes 2359296 | tf_op jit(solution)/shard_map/all_gather | solution.py:349
  9.9 193.9 %all-gather.10.cloned.1.call-start = ((), (), s32[]{:S(2)}) async-start(), calls=%async_computation.7 | async-start | bytes 9437184 | tf_op jit(solution)/shard_map/all_gather | solution.py:349
  10.6 235.4 %all-gather.12.cloned.1.call-start = ((), (), s32[]{:S(2)}) async-start(), calls=%async_computation.8 | async-start | bytes 9437184 | tf_op jit(solution)/shard_map/all_gather | solution.py:349
  11.2 316.8 %all-gather.14.cloned.1.call-start = ((), (), s32[]{:S(2)}) async-start(), calls=%async_computation.9 | async-start | bytes 9437184 | tf_op jit(solution)/shard_map/all_gather | solution.py:349
  12.4 26.3 %collective-permute-start = (bf16[256,2048]{1,0:T(8,128)(2,1)S(1)}, bf16[256,2048]{1,0:T(8,128)(2,1)}, u32[]{:S(2)}, u32[]{:S(2)}) collective-permute-start(bf16[256,2048]{1,0:T(8,128)(2,1)S(1)} %fusion.3), channel_id=1, source_target_pairs={{0,1},{1,0},{2,3},{3,2},{4,5},{5,4},{6,7},{7,6},{8,9},{9,8},{10,11... | collective-permute-start | bytes 3145736 | tf_op jit(solution)/shard_map/ppermute | solution.py:232
  15.5 26.9 %collective-permute-start.1 = (bf16[256,2048]{1,0:T(8,128)(2,1)S(1)}, bf16[256,2048]{1,0:T(8,128)(2,1)}, u32[]{:S(2)}, u32[]{:S(2)}) collective-permute-start(bf16[256,2048]{1,0:T(8,128)(2,1)S(1)} %fusion.3), channel_id=1, source_target_pairs={{0,2},{1,3},{2,0},{3,1},{4,6},{5,7},{6,4},{7,5},{8,10},{9,11},{10,... | collective-permute-start | bytes 3145736 | tf_op jit(solution)/shard_map/ppermute | solution.py:232
  96.2 35.6 %collective-permute-start.8 = (bf16[256,2048]{0,1:T(8,128)(2,1)S(1)}, bf16[256,2048]{0,1:T(8,128)(2,1)S(1)}, u32[]{:S(2)}, u32[]{:S(2)}) collective-permute-start(bf16[256,2048]{0,1:T(8,128)(2,1)S(1)} %copy.31), channel_id=1, source_target_pairs={{0,1},{1,0},{2,3},{3,2},{4,5},{5,4},{6,7},{7,6},{8,9},{9,8},{10,11... | collective-permute-start | bytes 3145736 | tf_op jit(solution)/shard_map/ppermute | solution.py:232
  97.0 35.6 %collective-permute-start.9 = (bf16[256,2048]{0,1:T(8,128)(2,1)S(1)}, bf16[256,2048]{0,1:T(8,128)(2,1)}, u32[]{:S(2)}, u32[]{:S(2)}) collective-permute-start(bf16[256,2048]{0,1:T(8,128)(2,1)S(1)} %copy.31), channel_id=1, source_target_pairs={{0,2},{1,3},{2,0},{3,1},{4,6},{5,7},{6,4},{7,5},{8,10},{9,11},{10,... | collective-permute-start | bytes 3145736 | tf_op jit(solution)/shard_map/ppermute | solution.py:232
  113.5 40.9 %collective-permute-start.5 = (bf16[256,2048]{1,0:T(8,128)(2,1)}, bf16[256,2048]{1,0:T(8,128)(2,1)}, u32[]{:S(2)}, u32[]{:S(2)}) collective-permute-start(bf16[256,2048]{1,0:T(8,128)(2,1)} %pad_maximum_fusion.1), channel_id=1, source_target_pairs={{0,1},{1,0},{2,3},{3,2},{4,5},{5,4},{6,7},{7,6},{8,9},{9,8},{10,11... | collective-permute-start | bytes 3145736 | tf_op jit(solution)/shard_map/ppermute | solution.py:232
  116.0 38.5 %collective-permute-start.7 = (bf16[256,2048]{1,0:T(8,128)(2,1)}, bf16[256,2048]{1,0:T(8,128)(2,1)}, u32[]{:S(2)}, u32[]{:S(2)}) collective-permute-start(bf16[256,2048]{1,0:T(8,128)(2,1)} %pad_maximum_fusion.2), channel_id=1, source_target_pairs={{0,2},{1,3},{2,0},{3,1},{4,6},{5,7},{6,4},{7,5},{8,10},{9,11},{10,... | collective-permute-start | bytes 3145736 | tf_op jit(solution)/shard_map/ppermute | solution.py:232
  116.7 531.6 %reduce-scatter.14.cloned.1.call-start = ((), (), s32[]{:S(2)}) async-start(), calls=%async_computation.14 | async-start | bytes 5242880 | tf_op jit(solution)/shard_map/reduce_scatter | solution.py:320
  131.9 32.3 %collective-permute-start.10 = (bf16[128,2048]{0,1:T(8,128)(2,1)S(1)}, bf16[128,2048]{0,1:T(8,128)(2,1)S(1)}, u32[]{:S(2)}, u32[]{:S(2)}) collective-permute-start(bf16[128,2048]{0,1:T(8,128)(2,1)S(1)} %slice.42), channel_id=1, source_target_pairs={{0,2},{1,3},{2,0},{3,1},{4,6},{5,7},{6,4},{7,5},{8,10},{9,11},{10,... | collective-permute-start | bytes 1572872 | tf_op jit(solution)/shard_map/ppermute | solution.py:232
  133.7 31.9 %collective-permute-start.11 = (bf16[128,2048]{0,1:T(8,128)(2,1)S(1)}, bf16[128,2048]{0,1:T(8,128)(2,1)S(1)}, u32[]{:S(2)}, u32[]{:S(2)}) collective-permute-start(bf16[128,2048]{0,1:T(8,128)(2,1)S(1)} %slice.43), channel_id=1, source_target_pairs={{0,1},{1,0},{2,3},{3,2},{4,5},{5,4},{6,7},{7,6},{8,9},{9,8},{10,11... | collective-permute-start | bytes 1572872 | tf_op jit(solution)/shard_map/ppermute | solution.py:232
  157.9 27.9 %collective-permute-start.12 = (bf16[256,2048]{1,0:T(8,128)(2,1)S(1)}, bf16[256,2048]{1,0:T(8,128)(2,1)}, u32[]{:S(2)}, u32[]{:S(2)}) collective-permute-start(bf16[256,2048]{1,0:T(8,128)(2,1)S(1)} %multiply_convert_fusion.4), channel_id=1, source_target_pairs={{0,1},{1,0},{2,3},{3,2},{4,5},{5,4},{6,7},{7,6},{8,9},{9,8},{10,11... | collective-permute-start | bytes 3145736 | tf_op jit(solution)/shard_map/ppermute | solution.py:232
  159.3 28.1 %collective-permute-start.13 = (bf16[256,2048]{1,0:T(8,128)(2,1)S(1)}, bf16[256,2048]{1,0:T(8,128)(2,1)}, u32[]{:S(2)}, u32[]{:S(2)}) collective-permute-start(bf16[256,2048]{1,0:T(8,128)(2,1)S(1)} %multiply_convert_fusion.4), channel_id=1, source_target_pairs={{0,2},{1,3},{2,0},{3,1},{4,6},{5,7},{6,4},{7,5},{8,10},{9,11},{10,... | collective-permute-start | bytes 3145736 | tf_op jit(solution)/shard_map/ppermute | solution.py:232
  387.5 46.9 %collective-permute-start.22 = (bf16[1024,2048]{1,0:T(8,128)(2,1)}, bf16[1024,2048]{1,0:T(8,128)(2,1)}, u32[]{:S(2)}, u32[]{:S(2)}) collective-permute-start(bf16[1024,2048]{1,0:T(8,128)(2,1)} %convolution_convert_fusion.3), channel_id=1, source_target_pairs={{0,4},{4,0},{8,12},{12,8},{16,20},{20,16},{24,28},{28,24},{1,5},{5... | collective-permute-start | bytes 12582920 | tf_op jit(solution)/shard_map/ppermute | solution.py:232
  397.1 45.1 %collective-permute-start.21 = (bf16[1024,2048]{1,0:T(8,128)(2,1)}, bf16[1024,2048]{1,0:T(8,128)(2,1)}, u32[]{:S(2)}, u32[]{:S(2)}) collective-permute-start(bf16[1024,2048]{1,0:T(8,128)(2,1)} %convolution_convert_fusion.4), channel_id=1, source_target_pairs={{0,4},{4,0},{8,12},{12,8},{16,20},{20,16},{24,28},{28,24},{1,5},{5... | collective-permute-start | bytes 12582920 | tf_op jit(solution)/shard_map/ppermute | solution.py:232
  403.9 24.4 %collective-permute-start.18 = (bf16[256,2048]{1,0:T(8,128)(2,1)S(1)}, bf16[256,2048]{1,0:T(8,128)(2,1)}, u32[]{:S(2)}, u32[]{:S(2)}) collective-permute-start(bf16[256,2048]{1,0:T(8,128)(2,1)S(1)} %pad_maximum_fusion.3), channel_id=1, source_target_pairs={{0,1},{1,0},{2,3},{3,2},{4,5},{5,4},{6,7},{7,6},{8,9},{9,8},{10,11... | collective-permute-start | bytes 3145736 | tf_op jit(solution)/shard_map/ppermute | solution.py:232
  406.5 24.2 %collective-permute-start.20 = (bf16[256,2048]{1,0:T(8,128)(2,1)}, bf16[256,2048]{1,0:T(8,128)(2,1)}, u32[]{:S(2)}, u32[]{:S(2)}) collective-permute-start(bf16[256,2048]{1,0:T(8,128)(2,1)} %pad_maximum_fusion.4), channel_id=1, source_target_pairs={{0,2},{1,3},{2,0},{3,1},{4,6},{5,7},{6,4},{7,5},{8,10},{9,11},{10,... | collective-permute-start | bytes 3145736 | tf_op jit(solution)/shard_map/ppermute | solution.py:232
  407.0 244.0 %reduce-scatter.8.cloned.1.call-start = ((), (), s32[]{:S(2)}) async-start(), calls=%async_computation.11 | async-start | bytes 1310720 | tf_op jit(solution)/shard_map/reduce_scatter | solution.py:320
  457.9 23.2 %collective-permute-start.23 = (bf16[256,2048]{1,0:T(8,128)(2,1)}, bf16[256,2048]{1,0:T(8,128)(2,1)}, u32[]{:S(2)}, u32[]{:S(2)}) collective-permute-start(bf16[256,2048]{1,0:T(8,128)(2,1)} %get-tuple-element.55), channel_id=1, source_target_pairs={{0,1},{1,0},{2,3},{3,2},{4,5},{5,4},{6,7},{7,6},{8,9},{9,8},{10,11... | collective-permute-start | bytes 3145736 | tf_op jit(solution)/shard_map/ppermute | solution.py:232
  458.3 25.4 %collective-permute-start.24 = (bf16[256,2048]{1,0:T(8,128)(2,1)}, bf16[256,2048]{1,0:T(8,128)(2,1)}, u32[]{:S(2)}, u32[]{:S(2)}) collective-permute-start(bf16[256,2048]{1,0:T(8,128)(2,1)} %get-tuple-element.55), channel_id=1, source_target_pairs={{0,2},{1,3},{2,0},{3,1},{4,6},{5,7},{6,4},{7,5},{8,10},{9,11},{10,... | collective-permute-start | bytes 3145736 | tf_op jit(solution)/shard_map/ppermute | solution.py:232
  554.8 98.1 %reduce-scatter.6.cloned.1.call-start = ((), (), s32[]{:S(2)}) async-start(), calls=%async_computation.10 | async-start | bytes 1966080 | tf_op jit(solution)/shard_map/reduce_scatter | solution.py:320
  561.3 134.9 %reduce-scatter.10.cloned.1.call-start = ((), (), s32[]{:S(2)}) async-start(), calls=%async_computation.12 | async-start | bytes 5242880 | tf_op jit(solution)/shard_map/reduce_scatter | solution.py:320
  562.1 213.6 %reduce-scatter.12.cloned.1.call-start = ((), (), s32[]{:S(2)}) async-start(), calls=%async_computation.13 | async-start | bytes 5242880 | tf_op jit(solution)/shard_map/reduce_scatter | solution.py:320
  580.4 37.4 %collective-permute-start.32 = (bf16[256,2048]{1,0:T(8,128)(2,1)S(1)}, bf16[256,2048]{1,0:T(8,128)(2,1)S(1)}, u32[]{:S(2)}, u32[]{:S(2)}) collective-permute-start(bf16[256,2048]{1,0:T(8,128)(2,1)S(1)} %pad_maximum_fusion.7), channel_id=1, source_target_pairs={{0,1},{1,0},{2,3},{3,2},{4,5},{5,4},{6,7},{7,6},{8,9},{9,8},{10,11... | collective-permute-start | bytes 3145736 | tf_op jit(solution)/shard_map/ppermute | solution.py:232
  581.9 35.9 %collective-permute-start.34 = (bf16[256,2048]{1,0:T(8,128)(2,1)S(1)}, bf16[256,2048]{1,0:T(8,128)(2,1)S(1)}, u32[]{:S(2)}, u32[]{:S(2)}) collective-permute-start(bf16[256,2048]{1,0:T(8,128)(2,1)S(1)} %pad_maximum_fusion.8), channel_id=1, source_target_pairs={{0,2},{1,3},{2,0},{3,1},{4,6},{5,7},{6,4},{7,5},{8,10},{9,11},{10,... | collective-permute-start | bytes 3145736 | tf_op jit(solution)/shard_map/ppermute | solution.py:232
  582.9 34.5 %collective-permute-start.27 = (bf16[128,2048]{1,0:T(8,128)(2,1)S(1)}, bf16[128,2048]{1,0:T(8,128)(2,1)S(1)}, u32[]{:S(2)}, u32[]{:S(2)}) collective-permute-start(bf16[128,2048]{1,0:T(8,128)(2,1)S(1)} %get-tuple-element.74), channel_id=1, source_target_pairs={{0,2},{1,3},{2,0},{3,1},{4,6},{5,7},{6,4},{7,5},{8,10},{9,11},{10,... | collective-permute-start | bytes 1572872 | tf_op jit(solution)/shard_map/ppermute | solution.py:232
  584.3 33.0 %collective-permute-start.29 = (bf16[128,2048]{1,0:T(8,128)(2,1)S(1)}, bf16[128,2048]{1,0:T(8,128)(2,1)S(1)}, u32[]{:S(2)}, u32[]{:S(2)}) collective-permute-start(bf16[128,2048]{1,0:T(8,128)(2,1)S(1)} %get-tuple-element.73), channel_id=1, source_target_pairs={{0,1},{1,0},{2,3},{3,2},{4,5},{5,4},{6,7},{7,6},{8,9},{9,8},{10,11... | collective-permute-start | bytes 1572872 | tf_op jit(solution)/shard_map/ppermute | solution.py:232
  620.2 23.2 %collective-permute-start.28 = (bf16[256,2048]{1,0:T(8,128)(2,1)S(1)}, bf16[256,2048]{1,0:T(8,128)(2,1)S(1)}, u32[]{:S(2)}, u32[]{:S(2)}) collective-permute-start(bf16[256,2048]{1,0:T(8,128)(2,1)S(1)} %pad_maximum_fusion.5), channel_id=1, source_target_pairs={{0,1},{1,0},{2,3},{3,2},{4,5},{5,4},{6,7},{7,6},{8,9},{9,8},{10,11... | collective-permute-start | bytes 3145736 | tf_op jit(solution)/shard_map/ppermute | solution.py:232
  624.1 21.9 %collective-permute-start.30 = (bf16[256,2048]{1,0:T(8,128)(2,1)S(1)}, bf16[256,2048]{1,0:T(8,128)(2,1)S(1)}, u32[]{:S(2)}, u32[]{:S(2)}) collective-permute-start(bf16[256,2048]{1,0:T(8,128)(2,1)S(1)} %pad_maximum_fusion.6), channel_id=1, source_target_pairs={{0,2},{1,3},{2,0},{3,1},{4,6},{5,7},{6,4},{7,5},{8,10},{9,11},{10,... | collective-permute-start | bytes 3145736 | tf_op jit(solution)/shard_map/ppermute | solution.py:232
  (54 other events, 872.5 us)
Sparse Core Ops, SparseCore 0:
  10.2 40.9 all-gather.5
  52.8 28.0 all-gather.7
  82.5 81.4 all-gather.9
  165.4 80.5 all-gather.11
  247.4 80.5 all-gather.13
  407.2 74.3 reduce-scatter.13
  554.9 25.7 reduce-scatter.7
  583.6 33.9 reduce-scatter.5
  619.9 76.3 reduce-scatter.9
  698.3 77.2 reduce-scatter.11

commit v4 on v3

--- a/solution.py
+++ b/solution.py
@@ -6,6 +6,7 @@
 from jax.experimental import pallas as pl
 from jax.experimental.pallas import tpu as pltpu
 from jax.sharding import PartitionSpec as P
+
 
 HD = 64
 SEQ = 512
@@ -348,10 +349,10 @@
     def gather(weight):
         return lax.all_gather(weight, "dp", axis=0, tiled=True)
 
-    qkv_full = gather(jnp.concatenate([w_query, w_key, w_value], axis=1))
-    out_full = gather(w_out)
-    gate_full = gather(w_gate)
-    up_full = gather(w_up)
+    narrow = splits[1] + keys_width
+    small_full = gather(jnp.concatenate([w_query, w_key, w_value, w_out], axis=1))
+    qkv_full, out_full = small_full[:, :narrow], small_full[:, narrow:]
+    gate_full, up_full = jnp.split(gather(jnp.concatenate([w_gate, w_up], axis=1)), 2, axis=1)
     down_full = gather(w_down)
 
     live_all = (doc_ids >= 0).astype(jnp.float32)
@@ -381,7 +382,11 @@
     silu_gate = gate_pre * sigmoid_gate
     hidden = (silu_gate * up_pre).astype(jnp.bfloat16)
     pair_down = pair_grad(parity_columns(grad_full, dp), hidden, dp)
-    pair_down, down_full = lax.optimization_barrier((pair_down, down_full))
+    one_parities = parity_columns(normed_one, dp)
+    two_parities = parity_columns(normed_two, dp)
+    pair_down, down_full, one_parities, two_parities = lax.optimization_barrier(
+        (pair_down, down_full, one_parities, two_parities)
+    )
     grad_down = sum_pairs(pair_down, dp)
 
     grad_hidden = matmul(grad_full, down_full)
@@ -395,15 +400,13 @@
     grad_normed_part, grad_gate_pre, grad_up_pre = lax.optimization_barrier(
         (grad_normed_part, grad_gate_pre, grad_up_pre)
     )
-    normed_two_parities = parity_columns(normed_two, dp)
-    pair_gate = pair_grad(normed_two_parities, grad_gate_pre, dp)
-    pair_up = pair_grad(normed_two_parities, grad_up_pre, dp)
+    pair_gate_up = jnp.concatenate(
+        [pair_grad(two_parities, grad_gate_pre, dp), pair_grad(two_parities, grad_up_pre, dp)],
+        axis=1,
+    )
     grad_normed_own = sum_rows(grad_normed_part, tp)
-    grad_normed_own, pair_gate, pair_up = lax.optimization_barrier(
-        (grad_normed_own, pair_gate, pair_up)
-    )
-    grad_gate = sum_pairs(pair_gate, dp)
-    grad_up = sum_pairs(pair_up, dp)
+    grad_normed_own, pair_gate_up = lax.optimization_barrier((grad_normed_own, pair_gate_up))
+    grad_gate, grad_up = jnp.split(sum_pairs(pair_gate_up, dp), 2, axis=1)
     grad_mlp_gain = jnp.sum(grad_normed_own * residual_own * scale_two_own, axis=0)
     grad_residual_own = cotangent.astype(jnp.float32) + norm_back(
         grad_normed_own, residual_own, scale_two_own, mlp_gain
@@ -424,11 +427,16 @@
     grad_one_part, grad_qkv_rows, mixed_all = lax.optimization_barrier(
         (grad_one_part, grad_qkv_rows, mixed_all)
     )
-    pair_out = pair_grad(parity_columns(grad_residual_bf, dp), mixed_all, dp)
-    pair_qkv = pair_grad(parity_columns(normed_one, dp), grad_qkv_rows, dp)
-    grad_out = sum_pairs(pair_out, dp)
-    grad_qkv = sum_pairs(pair_qkv, dp)
-    grad_query, grad_key, grad_value = jnp.split(grad_qkv, splits, axis=1)
+    pair_small = jnp.concatenate(
+        [
+            pair_grad(one_parities, grad_qkv_rows, dp),
+            pair_grad(parity_columns(grad_residual_bf, dp), mixed_all, dp),
+        ],
+        axis=1,
+    )
+    grad_query, grad_key, grad_value, grad_out = jnp.split(
+        sum_pairs(pair_small, dp), splits + (narrow,), axis=1
+    )
     grad_normed_one = sum_rows(grad_one_part, tp)
     grad_attn_gain = jnp.sum(grad_normed_one * input_own * scale_one, axis=0)
     input_grad = (

time: 796 us -> 755 us (0.948)
  waiting for transfers between devices: 376 us -> 333 us
  matrix products: 176 us -> 167 us
    all_gather x5 -> x3, waiting for transfers between devices: 73.6 us -> 42.6 us  [gather(): return lax.all_gather(weight, 'dp', axis=0, tiled=True)]
    reduce_scatter x5 -> x3, waiting for transfers between devices: 117 us -> 103 us  [sum_pairs(): lax.psum_scatter(pair_sum, 'dp', scatter_dimension=0, tiled=True, axis_in...]
    concatenate x1 -> x4, other arithmetic: 1.87 us -> 15 us  [the longest x1 8.14 us: per_device(): jnp.concatenate([pair_grad(two_parities, grad_gate_pre, dp), pair_grad(tw...]
    dot_general x10, matrix products: 57.5 us -> 48.9 us  [contract_rows(): lax.dot_general(left_side, right_side, (((0,), (0,)), ((), ())), preferre...]
  transfers between devices with their start and end apart: 52 -> 48, of which waited for: 30 -> 29; matrix products, arithmetic and copies ran while one was open for 31% -> 32% of each run, Pallas kernels for 5% -> 6%
where the time goes in v4:
time: 755 us; the launch traced here: 745 us
  waiting for transfers between devices  333 us (44%)
  matrix products  167 us (22%)
  local copies, waits for them, and re-layouts  96 us (13%)
  other arithmetic  46.4 us (6%)
  starting transfers between devices  45.8 us (6%)
  Pallas kernels  41.4 us (5%)
  between operations  15.4 us (2%)
    ppermute x42, waiting for transfers between devices, swap(): return lax.ppermute(array, axis, [(i, i ^ bit) for i in range(size)])  186 us
    reduce_scatter x3, waiting for transfers between devices, sum_pairs(): lax.psum_scatter(pair_sum, 'dp', scatter_dimension=0, tiled=True, axis_in...  103 us
    dot_general x5, matrix products, matmul(): return jnp.dot(left_side, right_side, preferred_element_type=jnp.float32)  65.4 us
    dot_general x5, matrix products, contract_cols(): lax.dot_general(left_side, right_side, (((1,), (1,)), ((), ())), preferre...  52.8 us
    dot_general x10, matrix products, contract_rows(): lax.dot_general(left_side, right_side, (((0,), (0,)), ((), ())), preferre...  48.9 us
    ppermute x42, starting transfers between devices, swap(): return lax.ppermute(array, axis, [(i, i ^ bit) for i in range(size)])  44.7 us
    all_gather x3, waiting for transfers between devices, gather(): return lax.all_gather(weight, 'dp', axis=0, tiled=True)  42.6 us
    pallas_call x1, Pallas kernels, attend_back(): pl.pallas_call(functools.partial(attend_back_kernel, groups), name='atten...  23.2 us
  transfers between devices with their start and end apart: 48, of which 29 were waited for; matrix products, arithmetic and copies ran while one was open for 32% of the time, Pallas kernels for 6%

profile of v4, /device:TPU:0, one launch (start us, length us, event | category | flops | bytes accessed | tf_op | source)
XLA Modules:
  0.0 744.7 jit_solution(639187700409604214)
XLA Ops:
  24.0 16.0 %collective-permute-done = bf16[256,2048]{1,0:T(8,128)(2,1)} collective-permute-done((bf16[256,2048]{1,0:T(8,128)(2,1)S(1)}, bf16[256,2048]{1,0:T(8,128)(2,1)}, u32[]{:S(2)}, u32[]{:S(2)}) %collective-permute-start) | collective-permute-done | bytes 1048608 | tf_op jit(solution)/shard_map/ppermute | solution.py:233
  61.5 7.4 all-gather.4.cloned.1.call-done
  68.9 6.2 fusion.12
  77.8 18.3 %attend.1 = (bf16[1024,512]{1,0:T(8,128)(2,1)}, bf16[1024,128]{1,0:T(8,128)(2,1)}, bf16[1024,128]{1,0:T(8,128)(2,1)}, bf16[1024,512]{1,0:T(8,128)(2,1)}) custom-call(f32[1024,512]{1,0:T(8,128)} %split.44.q_ref, f32[1024,128]{1,0:T(8,128)} %get-tuple-element.133.k_ref, f32[1024,128]{1,0:T(8,128)} %get-tuple-element.132.v_ref, s32[2,1,512]{2,1,0:T(1,128)} %bitcast.66, ...), custom_call_target="tpu_custom_call" | custom-call | flops 1073741824 | bytes 8388608 | tf_op jit(solution)/shard_map/attend/pallas_call | solution.py:195
  107.2 9.7 %collective-permute-done.4 = bf16[128,2048]{1,0:T(8,128)(2,1)} collective-permute-done((bf16[128,2048]{1,0:T(8,128)(2,1)}, bf16[128,2048]{1,0:T(8,128)(2,1)}, u32[]{:S(2)}, u32[]{:S(2)}) %collective-permute-start.4) | collective-permute-done | bytes 524320 | tf_op jit(solution)/shard_map/ppermute | solution.py:233
  127.6 13.3 %collective-permute-done.8 = bf16[256,2048]{0,1:T(8,128)(2,1)} collective-permute-done((bf16[256,2048]{0,1:T(8,128)(2,1)S(1)}, bf16[256,2048]{0,1:T(8,128)(2,1)}, u32[]{:S(2)}, u32[]{:S(2)}) %collective-permute-start.8) | collective-permute-done | bytes 1048608 | tf_op jit(solution)/shard_map/ppermute | solution.py:233
  146.4 16.9 %collective-permute-done.5 = bf16[256,2048]{1,0:T(8,128)(2,1)} collective-permute-done((bf16[256,2048]{1,0:T(8,128)(2,1)}, bf16[256,2048]{1,0:T(8,128)(2,1)}, u32[]{:S(2)}, u32[]{:S(2)}) %collective-permute-start.5) | collective-permute-done | bytes 1048608 | tf_op jit(solution)/shard_map/ppermute | solution.py:233
  176.6 5.8 constant_dynamic-slice_fusion.16
  182.9 13.3 %collective-permute-done.12 = bf16[256,2048]{1,0:T(8,128)(2,1)} collective-permute-done((bf16[256,2048]{1,0:T(8,128)(2,1)S(1)}, bf16[256,2048]{1,0:T(8,128)(2,1)}, u32[]{:S(2)}, u32[]{:S(2)}) %collective-permute-start.12) | collective-permute-done | bytes 1048608 | tf_op jit(solution)/shard_map/ppermute | solution.py:233
  221.0 13.1 %fusion.7 = f32[1024,2048]{1,0:T(8,128)S(1)} fusion(bf16[1024,2048]{0,1:T(8,128)(2,1)} %constant_dynamic-update-slice_fusion.5, bf16[2048,4096]{1,0:T(8,128)(2,1)} %all-gather.6.cloned.1.call-done), kind=kOutput, calls=%fused_computation.16 | convolution fusion | flops 8589934592 | bytes 20971520 | tf_op jit(solution)/shard_map/dot_general | solution.py:51
  234.1 19.0 %multiply_convert_fusion.2 = (bf16[1024,2048]{1,0:T(8,128)(2,1)S(1)}, f32[1024,2048]{1,0:T(8,128)}) fusion(f32[1024,2048]{1,0:T(8,128)S(1)} %fusion.7, bf16[1024,2048]{0,1:T(8,128)(2,1)} %constant_dynamic-update-slice_fusion.5, bf16[2048,4096]{1,0:T(8,128)(2,1)} %all-gather.6.cloned.1.call-done), kind=kOutput, calls=%fused_computation.7 | convolution fusion | flops 8602517504 | bytes 33554432 | tf_op jit(solution)/shard_map/dot_general | solution.py:51
  253.2 4.9 convolution_convert_fusion.5
  265.7 6.1 add_convert_fusion.3
  271.8 31.1 %all-gather.8.cloned.1.call-done = bf16[2048,2048]{1,0:T(8,128)(2,1)} async-done(((bf16[256,2048]{1,0:T(8,128)(2,1)}), bf16[2048,2048]{1,0:T(8,128)(2,1)}) %all-gather.8.cloned.1.call-update) | async-done | bytes 8388624 | tf_op jit(solution)/shard_map/all_gather | solution.py:350
  302.9 20.8 %multiply_convert_fusion.1 = (bf16[1024,2048]{1,0:T(8,128)(2,1)}, bf16[1024,2048]{1,0:T(8,128)(2,1)S(1)}) fusion(f32[1024,2048]{1,0:T(8,128)} %copy-done.31, f32[1024,2048]{1,0:T(8,128)} %get-tuple-element.149, bf16[1024,2048]{0,1:T(8,128)(2,1)} %copy-done.5, bf16[2048,2048]{1,0:T(8,128)(2,1)} %all-gather.8.cloned.1.call-done), kind=kOutput, calls=%fused_computation.5 | convolution fusion | flops 8617197568 | bytes 37748736 | tf_op jit(solution)/shard_map/dot_general | solution.py:51
  323.7 15.1 %fusion.1 = f32[1024,2048]{1,0:T(8,128)} fusion(bf16[1024,2048]{1,0:T(8,128)(2,1)S(1)} %get-tuple-element.40, bf16[2048,4096]{1,0:T(8,128)(2,1)} %all-gather.6.cloned.1.call-done), kind=kOutput, calls=%fused_computation.10 | convolution fusion | flops 8589934592 | bytes 20971520 | tf_op jit(solution)/shard_map/dot_general | solution.py:45
  338.8 13.9 %add_convert_fusion.2 = bf16[1024,2048]{1,0:T(8,128)(2,1)S(1)} fusion(f32[1024,2048]{1,0:T(8,128)} %fusion.1, bf16[1024,2048]{1,0:T(8,128)(2,1)} %get-tuple-element.38, bf16[2048,4096]{1,0:T(8,128)(2,1)} %all-gather.6.cloned.1.call-done), kind=kOutput, calls=%fused_computation.3 | convolution fusion | flops 8594128896 | bytes 25165824 | tf_op jit(solution)/shard_map/dot_general | solution.py:45
  352.7 9.8 %convolution_convert_fusion.4 = bf16[1024,2048]{1,0:T(8,128)(2,1)} fusion(bf16[1024,1024]{0,1:T(8,128)(2,1)S(1)} %bitcast.56, bf16[1024,2048]{1,0:T(8,128)(2,1)} %get-tuple-element.38), kind=kOutput, calls=%fused_computation.28 | convolution fusion | flops 4297064448 | bytes 10485760 | tf_op jit(solution)/shard_map/dot_general | solution.py:39
  366.0 6.1 convolution_convert_fusion.3
  372.0 5.1 collective-permute-done.17
  382.5 20.7 %collective-permute-done.18 = bf16[256,2048]{1,0:T(8,128)(2,1)} collective-permute-done((bf16[256,2048]{1,0:T(8,128)(2,1)S(1)}, bf16[256,2048]{1,0:T(8,128)(2,1)}, u32[]{:S(2)}, u32[]{:S(2)}) %collective-permute-start.18) | collective-permute-done | bytes 1048608 | tf_op jit(solution)/shard_map/ppermute | solution.py:233
  409.4 7.9 %add_convert_fusion.1 = bf16[1024,2048]{1,0:T(8,128)(2,1)} fusion(bf16[1024,2048]{1,0:T(8,128)(2,1)} %collective-permute-done.21, bf16[1024,1024]{0,1:T(8,128)(2,1)S(1)} %bitcast.52, bf16[1024,2048]{1,0:T(8,128)(2,1)S(1)} %copy-done.37), kind=kOutput, calls=%fused_computation.2 | convolution fusion | flops 4301258752 | bytes 14680064 | tf_op jit(solution)/shard_map/dot_general | solution.py:39
  417.3 7.7 %add_convert_fusion = bf16[1024,2048]{1,0:T(8,128)(2,1)} fusion(bf16[1024,2048]{1,0:T(8,128)(2,1)} %collective-permute-done.22, bf16[1024,1024]{0,1:T(8,128)(2,1)S(1)} %bitcast.53, bf16[1024,2048]{1,0:T(8,128)(2,1)S(1)} %copy-done.36), kind=kOutput, calls=%fused_computation.1 | convolution fusion | flops 4301258752 | bytes 14680064 | tf_op jit(solution)/shard_map/dot_general | solution.py:39
  425.0 8.1 %pad_maximum_fusion = bf16[1024,4096]{1,0:T(8,128)(2,1)} fusion(bf16[1024,2048]{1,0:T(8,128)(2,1)} %add_convert_fusion, bf16[1024,2048]{1,0:T(8,128)(2,1)} %add_convert_fusion.1), kind=kLoop, calls=%fused_computation | loop fusion | flops 16777216 | bytes 16777216 | tf_op jit(solution)/shard_map/concatenate | solution.py:403
  440.7 20.7 %collective-permute-done.23 = bf16[256,2048]{1,0:T(8,128)(2,1)} collective-permute-done((bf16[256,2048]{1,0:T(8,128)(2,1)}, bf16[256,2048]{1,0:T(8,128)(2,1)}, u32[]{:S(2)}, u32[]{:S(2)}) %collective-permute-start.23) | collective-permute-done | bytes 1048608 | tf_op jit(solution)/shard_map/ppermute | solution.py:233
  481.4 6.2 multiply_convert_fusion.3.grad_ref
  487.6 23.2 %attend_back.1 = (bf16[1024,512]{1,0:T(8,128)(2,1)}, f32[1024,128]{1,0:T(8,128)}, bf16[1024,128]{1,0:T(8,128)(2,1)}) custom-call(bf16[1024,512]{1,0:T(8,128)(2,1)} %get-tuple-element.43.q_ref, bf16[1024,128]{1,0:T(8,128)(2,1)} %get-tuple-element.44.k_ref, bf16[1024,128]{1,0:T(8,128)(2,1)} %get-tuple-element.45.v_ref, ...), custom_call_target="tpu_custom_call" | custom-call | flops 2684354560 | bytes 8388608 | tf_op jit(solution)/shard_map/attend_back/pallas_call | solution.py:216
  513.3 8.0 %convolution_convert_fusion.2 = bf16[1024,2048]{1,0:T(8,128)(2,1)} fusion(bf16[2048,1280]{1,0:T(8,128)(2,1)} %all-gather.4.cloned.1.call-done, bf16[1024,128]{1,0:T(8,128)(2,1)} %get-tuple-element.49, bf16[1024,128]{1,0:T(8,128)(2,1)S(1)} %convert_element_type.263, bf16[1024,512]{1,0:T(8,128)(2,1)} %get-tuple-element.47), kind=kOutput, calls=%fused_computation.26 | convolution fusion | flops 3228041216 | bytes 8912896 | tf_op jit(solution)/shard_map/dot_general | solution.py:45
  540.7 11.5 %convolution_convert_fusion = bf16[1024,2048]{1,0:T(8,128)(2,1)S(1)} fusion(bf16[1024,2048]{1,0:T(8,128)(2,1)S(1)} %copy-done.34, bf16[2048,2048]{1,0:T(8,128)(2,1)} %all-gather.8.cloned.1.call-done), kind=kOutput, calls=%fused_computation.24 | convolution fusion | flops 8592031744 | bytes 16777216 | tf_op jit(solution)/shard_map/dot_general | solution.py:45
  558.2 32.5 %collective-permute-done.27 = bf16[128,2048]{1,0:T(8,128)(2,1)S(1)} collective-permute-done((bf16[128,2048]{1,0:T(8,128)(2,1)S(1)}, bf16[128,2048]{1,0:T(8,128)(2,1)S(1)}, u32[]{:S(2)}, u32[]{:S(2)}) %collective-permute-start.27) | collective-permute-done | bytes 524320 | tf_op jit(solution)/shard_map/ppermute | solution.py:233
  607.4 9.3 %collective-permute-done.28 = bf16[256,2048]{1,0:T(8,128)(2,1)S(1)} collective-permute-done((bf16[256,2048]{1,0:T(8,128)(2,1)S(1)}, bf16[256,2048]{1,0:T(8,128)(2,1)S(1)}, u32[]{:S(2)}, u32[]{:S(2)}) %collective-permute-start.28) | collective-permute-done | bytes 1048608 | tf_op jit(solution)/shard_map/ppermute | solution.py:233
  629.9 103.4 %reduce-scatter.6.cloned.1.call-done = bf16[256,4096]{1,0:T(8,128)(2,1)} async-done(((bf16[1024,4096]{1,0:T(8,128)(2,1)}), bf16[256,4096]{1,0:T(8,128)(2,1)}) %reduce-scatter.6.cloned.1.call-update) | async-done | bytes 2097168 | tf_op jit(solution)/shard_map/reduce_scatter | solution.py:321
  (278 shorter events, 218.3 us)
Async XLA Ops:
  7.2 61.8 %all-gather.4.cloned.1.call-start = ((), (), s32[]{:S(2)}) async-start(), calls=%async_computation.3 | async-start | bytes 5898240 | tf_op jit(solution)/shard_map/all_gather | solution.py:350
  9.3 211.7 %all-gather.6.cloned.1.call-start = ((), (), s32[]{:S(2)}) async-start(), calls=%async_computation.4 | async-start | bytes 18874368 | tf_op jit(solution)/shard_map/all_gather | solution.py:350
  12.5 290.4 %all-gather.8.cloned.1.call-start = ((), (), s32[]{:S(2)}) async-start(), calls=%async_computation.5 | async-start | bytes 9437184 | tf_op jit(solution)/shard_map/all_gather | solution.py:350
  13.7 26.3 %collective-permute-start = (bf16[256,2048]{1,0:T(8,128)(2,1)S(1)}, bf16[256,2048]{1,0:T(8,128)(2,1)}, u32[]{:S(2)}, u32[]{:S(2)}) collective-permute-start(bf16[256,2048]{1,0:T(8,128)(2,1)S(1)} %fusion.16), channel_id=1, source_target_pairs={{0,1},{1,0},{2,3},{3,2},{4,5},{5,4},{6,7},{7,6},{8,9},{9,8},{10,11... | collective-permute-start | bytes 3145736 | tf_op jit(solution)/shard_map/ppermute | solution.py:233
  16.8 26.9 %collective-permute-start.1 = (bf16[256,2048]{1,0:T(8,128)(2,1)S(1)}, bf16[256,2048]{1,0:T(8,128)(2,1)}, u32[]{:S(2)}, u32[]{:S(2)}) collective-permute-start(bf16[256,2048]{1,0:T(8,128)(2,1)S(1)} %fusion.16), channel_id=1, source_target_pairs={{0,2},{1,3},{2,0},{3,1},{4,6},{5,7},{6,4},{7,5},{8,10},{9,11},{10,... | collective-permute-start | bytes 3145736 | tf_op jit(solution)/shard_map/ppermute | solution.py:233
  41.9 15.0 %collective-permute-start.2 = (bf16[128,2048]{1,0:T(8,128)(2,1)}, bf16[128,2048]{1,0:T(8,128)(2,1)}, u32[]{:S(2)}, u32[]{:S(2)}) collective-permute-start(bf16[128,2048]{1,0:T(8,128)(2,1)} %slice.48), channel_id=1, source_target_pairs={{0,2},{1,3},{2,0},{3,1},{4,6},{5,7},{6,4},{7,5},{8,10},{9,11},{10,... | collective-permute-start | bytes 1572872 | tf_op jit(solution)/shard_map/ppermute | solution.py:233
  101.8 15.1 %collective-permute-start.4 = (bf16[128,2048]{1,0:T(8,128)(2,1)}, bf16[128,2048]{1,0:T(8,128)(2,1)}, u32[]{:S(2)}, u32[]{:S(2)}) collective-permute-start(bf16[128,2048]{1,0:T(8,128)(2,1)} %get-tuple-element.129), channel_id=1, source_target_pairs={{0,2},{1,3},{2,0},{3,1},{4,6},{5,7},{6,4},{7,5},{8,10},{9,11},{10,... | collective-permute-start | bytes 1572872 | tf_op jit(solution)/shard_map/ppermute | solution.py:233
  103.2 15.1 %collective-permute-start.6 = (bf16[128,2048]{1,0:T(8,128)(2,1)}, bf16[128,2048]{1,0:T(8,128)(2,1)}, u32[]{:S(2)}, u32[]{:S(2)}) collective-permute-start(bf16[128,2048]{1,0:T(8,128)(2,1)} %get-tuple-element.128), channel_id=1, source_target_pairs={{0,1},{1,0},{2,3},{3,2},{4,5},{5,4},{6,7},{7,6},{8,9},{9,8},{10,11... | collective-permute-start | bytes 1572872 | tf_op jit(solution)/shard_map/ppermute | solution.py:233
  105.3 35.6 %collective-permute-start.8 = (bf16[256,2048]{0,1:T(8,128)(2,1)S(1)}, bf16[256,2048]{0,1:T(8,128)(2,1)}, u32[]{:S(2)}, u32[]{:S(2)}) collective-permute-start(bf16[256,2048]{0,1:T(8,128)(2,1)S(1)} %copy.43), channel_id=1, source_target_pairs={{0,1},{1,0},{2,3},{3,2},{4,5},{5,4},{6,7},{7,6},{8,9},{9,8},{10,11... | collective-permute-start | bytes 3145736 | tf_op jit(solution)/shard_map/ppermute | solution.py:233
  105.9 37.5 %collective-permute-start.9 = (bf16[256,2048]{0,1:T(8,128)(2,1)S(1)}, bf16[256,2048]{0,1:T(8,128)(2,1)S(1)}, u32[]{:S(2)}, u32[]{:S(2)}) collective-permute-start(bf16[256,2048]{0,1:T(8,128)(2,1)S(1)} %copy.43), channel_id=1, source_target_pairs={{0,2},{1,3},{2,0},{3,1},{4,6},{5,7},{6,4},{7,5},{8,10},{9,11},{10,... | collective-permute-start | bytes 3145736 | tf_op jit(solution)/shard_map/ppermute | solution.py:233
  122.5 40.8 %collective-permute-start.5 = (bf16[256,2048]{1,0:T(8,128)(2,1)}, bf16[256,2048]{1,0:T(8,128)(2,1)}, u32[]{:S(2)}, u32[]{:S(2)}) collective-permute-start(bf16[256,2048]{1,0:T(8,128)(2,1)} %pad_maximum_fusion.4), channel_id=1, source_target_pairs={{0,1},{1,0},{2,3},{3,2},{4,5},{5,4},{6,7},{7,6},{8,9},{9,8},{10,11... | collective-permute-start | bytes 3145736 | tf_op jit(solution)/shard_map/ppermute | solution.py:233
  125.1 38.2 %collective-permute-start.7 = (bf16[256,2048]{1,0:T(8,128)(2,1)}, bf16[256,2048]{1,0:T(8,128)(2,1)}, u32[]{:S(2)}, u32[]{:S(2)}) collective-permute-start(bf16[256,2048]{1,0:T(8,128)(2,1)} %pad_maximum_fusion.5), channel_id=1, source_target_pairs={{0,2},{1,3},{2,0},{3,1},{4,6},{5,7},{6,4},{7,5},{8,10},{9,11},{10,... | collective-permute-start | bytes 3145736 | tf_op jit(solution)/shard_map/ppermute | solution.py:233
  126.5 495.2 %reduce-scatter.8.cloned.1.call-start = ((), (), s32[]{:S(2)}) async-start(), calls=%async_computation.8 | async-start | bytes 5242880 | tf_op jit(solution)/shard_map/reduce_scatter | solution.py:321
  141.9 31.1 %collective-permute-start.10 = (bf16[128,2048]{0,1:T(8,128)(2,1)S(1)}, bf16[128,2048]{0,1:T(8,128)(2,1)S(1)}, u32[]{:S(2)}, u32[]{:S(2)}) collective-permute-start(bf16[128,2048]{0,1:T(8,128)(2,1)S(1)} %slice.52), channel_id=1, source_target_pairs={{0,2},{1,3},{2,0},{3,1},{4,6},{5,7},{6,4},{7,5},{8,10},{9,11},{10,... | collective-permute-start | bytes 1572872 | tf_op jit(solution)/shard_map/ppermute | solution.py:233
  143.4 31.0 %collective-permute-start.11 = (bf16[128,2048]{0,1:T(8,128)(2,1)S(1)}, bf16[128,2048]{0,1:T(8,128)(2,1)S(1)}, u32[]{:S(2)}, u32[]{:S(2)}) collective-permute-start(bf16[128,2048]{0,1:T(8,128)(2,1)S(1)} %slice.53), channel_id=1, source_target_pairs={{0,1},{1,0},{2,3},{3,2},{4,5},{5,4},{6,7},{7,6},{8,9},{9,8},{10,11... | collective-permute-start | bytes 1572872 | tf_op jit(solution)/shard_map/ppermute | solution.py:233
  167.5 28.6 %collective-permute-start.12 = (bf16[256,2048]{1,0:T(8,128)(2,1)S(1)}, bf16[256,2048]{1,0:T(8,128)(2,1)}, u32[]{:S(2)}, u32[]{:S(2)}) collective-permute-start(bf16[256,2048]{1,0:T(8,128)(2,1)S(1)} %multiply_convert_fusion.4), channel_id=1, source_target_pairs={{0,1},{1,0},{2,3},{3,2},{4,5},{5,4},{6,7},{7,6},{8,9},{9,8},{10,11... | collective-permute-start | bytes 3145736 | tf_op jit(solution)/shard_map/ppermute | solution.py:233
  169.1 29.7 %collective-permute-start.13 = (bf16[256,2048]{1,0:T(8,128)(2,1)S(1)}, bf16[256,2048]{1,0:T(8,128)(2,1)}, u32[]{:S(2)}, u32[]{:S(2)}) collective-permute-start(bf16[256,2048]{1,0:T(8,128)(2,1)S(1)} %multiply_convert_fusion.4), channel_id=1, source_target_pairs={{0,2},{1,3},{2,0},{3,1},{4,6},{5,7},{6,4},{7,5},{8,10},{9,11},{10,... | collective-permute-start | bytes 3145736 | tf_op jit(solution)/shard_map/ppermute | solution.py:233
  362.5 47.0 %collective-permute-start.21 = (bf16[1024,2048]{1,0:T(8,128)(2,1)}, bf16[1024,2048]{1,0:T(8,128)(2,1)}, u32[]{:S(2)}, u32[]{:S(2)}) collective-permute-start(bf16[1024,2048]{1,0:T(8,128)(2,1)} %convolution_convert_fusion.4), channel_id=1, source_target_pairs={{0,4},{4,0},{8,12},{12,8},{16,20},{20,16},{24,28},{28,24},{1,5},{5... | collective-permute-start | bytes 12582920 | tf_op jit(solution)/shard_map/ppermute | solution.py:233
  372.0 45.3 %collective-permute-start.22 = (bf16[1024,2048]{1,0:T(8,128)(2,1)}, bf16[1024,2048]{1,0:T(8,128)(2,1)}, u32[]{:S(2)}, u32[]{:S(2)}) collective-permute-start(bf16[1024,2048]{1,0:T(8,128)(2,1)} %convolution_convert_fusion.3), channel_id=1, source_target_pairs={{0,4},{4,0},{8,12},{12,8},{16,20},{20,16},{24,28},{28,24},{1,5},{5... | collective-permute-start | bytes 12582920 | tf_op jit(solution)/shard_map/ppermute | solution.py:233
  378.8 24.4 %collective-permute-start.18 = (bf16[256,2048]{1,0:T(8,128)(2,1)S(1)}, bf16[256,2048]{1,0:T(8,128)(2,1)}, u32[]{:S(2)}, u32[]{:S(2)}) collective-permute-start(bf16[256,2048]{1,0:T(8,128)(2,1)S(1)} %pad_maximum_fusion.6), channel_id=1, source_target_pairs={{0,1},{1,0},{2,3},{3,2},{4,5},{5,4},{6,7},{7,6},{8,9},{9,8},{10,11... | collective-permute-start | bytes 3145736 | tf_op jit(solution)/shard_map/ppermute | solution.py:233
  381.4 24.2 %collective-permute-start.20 = (bf16[256,2048]{1,0:T(8,128)(2,1)}, bf16[256,2048]{1,0:T(8,128)(2,1)}, u32[]{:S(2)}, u32[]{:S(2)}) collective-permute-start(bf16[256,2048]{1,0:T(8,128)(2,1)} %pad_maximum_fusion.7), channel_id=1, source_target_pairs={{0,2},{1,3},{2,0},{3,1},{4,6},{5,7},{6,4},{7,5},{8,10},{9,11},{10,... | collective-permute-start | bytes 3145736 | tf_op jit(solution)/shard_map/ppermute | solution.py:233
  382.0 242.4 %reduce-scatter.4.cloned.1.call-start = ((), (), s32[]{:S(2)}) async-start(), calls=%async_computation.6 | async-start | bytes 3276800 | tf_op jit(solution)/shard_map/reduce_scatter | solution.py:321
  438.1 23.3 %collective-permute-start.23 = (bf16[256,2048]{1,0:T(8,128)(2,1)}, bf16[256,2048]{1,0:T(8,128)(2,1)}, u32[]{:S(2)}, u32[]{:S(2)}) collective-permute-start(bf16[256,2048]{1,0:T(8,128)(2,1)} %get-tuple-element.94), channel_id=1, source_target_pairs={{0,1},{1,0},{2,3},{3,2},{4,5},{5,4},{6,7},{7,6},{8,9},{9,8},{10,11... | collective-permute-start | bytes 3145736 | tf_op jit(solution)/shard_map/ppermute | solution.py:233
  438.6 25.3 %collective-permute-start.24 = (bf16[256,2048]{1,0:T(8,128)(2,1)}, bf16[256,2048]{1,0:T(8,128)(2,1)}, u32[]{:S(2)}, u32[]{:S(2)}) collective-permute-start(bf16[256,2048]{1,0:T(8,128)(2,1)} %get-tuple-element.94), channel_id=1, source_target_pairs={{0,2},{1,3},{2,0},{3,1},{4,6},{5,7},{6,4},{7,5},{8,10},{9,11},{10,... | collective-permute-start | bytes 3145736 | tf_op jit(solution)/shard_map/ppermute | solution.py:233
  535.2 198.1 %reduce-scatter.6.cloned.1.call-start = ((), (), s32[]{:S(2)}) async-start(), calls=%async_computation.7 | async-start | bytes 10485760 | tf_op jit(solution)/shard_map/reduce_scatter | solution.py:321
  537.7 14.5 %collective-permute-start.31 = (bf16[128,2048]{1,0:T(8,128)(2,1)S(1)}, bf16[128,2048]{1,0:T(8,128)(2,1)S(1)}, u32[]{:S(2)}, u32[]{:S(2)}) collective-permute-start(bf16[128,2048]{1,0:T(8,128)(2,1)S(1)} %get-tuple-element.105), channel_id=1, source_target_pairs={{0,2},{1,3},{2,0},{3,1},{4,6},{5,7},{6,4},{7,5},{8,10},{9,11},{10,... | collective-permute-start | bytes 1572872 | tf_op jit(solution)/shard_map/ppermute | solution.py:233
  553.7 37.5 %collective-permute-start.32 = (bf16[256,2048]{1,0:T(8,128)(2,1)S(1)}, bf16[256,2048]{1,0:T(8,128)(2,1)S(1)}, u32[]{:S(2)}, u32[]{:S(2)}) collective-permute-start(bf16[256,2048]{1,0:T(8,128)(2,1)S(1)} %pad_maximum_fusion.10), channel_id=1, source_target_pairs={{0,1},{1,0},{2,3},{3,2},{4,5},{5,4},{6,7},{7,6},{8,9},{9,8},{10,11... | collective-permute-start | bytes 3145736 | tf_op jit(solution)/shard_map/ppermute | solution.py:233
  555.3 35.9 %collective-permute-start.34 = (bf16[256,2048]{1,0:T(8,128)(2,1)S(1)}, bf16[256,2048]{1,0:T(8,128)(2,1)S(1)}, u32[]{:S(2)}, u32[]{:S(2)}) collective-permute-start(bf16[256,2048]{1,0:T(8,128)(2,1)S(1)} %pad_maximum_fusion.11), channel_id=1, source_target_pairs={{0,2},{1,3},{2,0},{3,1},{4,6},{5,7},{6,4},{7,5},{8,10},{9,11},{10,... | collective-permute-start | bytes 3145736 | tf_op jit(solution)/shard_map/ppermute | solution.py:233
  556.3 34.5 %collective-permute-start.27 = (bf16[128,2048]{1,0:T(8,128)(2,1)S(1)}, bf16[128,2048]{1,0:T(8,128)(2,1)S(1)}, u32[]{:S(2)}, u32[]{:S(2)}) collective-permute-start(bf16[128,2048]{1,0:T(8,128)(2,1)S(1)} %get-tuple-element.111), channel_id=1, source_target_pairs={{0,2},{1,3},{2,0},{3,1},{4,6},{5,7},{6,4},{7,5},{8,10},{9,11},{10,... | collective-permute-start | bytes 1572872 | tf_op jit(solution)/shard_map/ppermute | solution.py:233
  557.6 33.1 %collective-permute-start.29 = (bf16[128,2048]{1,0:T(8,128)(2,1)S(1)}, bf16[128,2048]{1,0:T(8,128)(2,1)S(1)}, u32[]{:S(2)}, u32[]{:S(2)}) collective-permute-start(bf16[128,2048]{1,0:T(8,128)(2,1)S(1)} %get-tuple-element.110), channel_id=1, source_target_pairs={{0,1},{1,0},{2,3},{3,2},{4,5},{5,4},{6,7},{7,6},{8,9},{9,8},{10,11... | collective-permute-start | bytes 1572872 | tf_op jit(solution)/shard_map/ppermute | solution.py:233
  593.4 23.2 %collective-permute-start.28 = (bf16[256,2048]{1,0:T(8,128)(2,1)S(1)}, bf16[256,2048]{1,0:T(8,128)(2,1)S(1)}, u32[]{:S(2)}, u32[]{:S(2)}) collective-permute-start(bf16[256,2048]{1,0:T(8,128)(2,1)S(1)} %pad_maximum_fusion.8), channel_id=1, source_target_pairs={{0,1},{1,0},{2,3},{3,2},{4,5},{5,4},{6,7},{7,6},{8,9},{9,8},{10,11... | collective-permute-start | bytes 3145736 | tf_op jit(solution)/shard_map/ppermute | solution.py:233
  597.5 21.9 %collective-permute-start.30 = (bf16[256,2048]{1,0:T(8,128)(2,1)S(1)}, bf16[256,2048]{1,0:T(8,128)(2,1)S(1)}, u32[]{:S(2)}, u32[]{:S(2)}) collective-permute-start(bf16[256,2048]{1,0:T(8,128)(2,1)S(1)} %pad_maximum_fusion.9), channel_id=1, source_target_pairs={{0,2},{1,3},{2,0},{3,1},{4,6},{5,7},{6,4},{7,5},{8,10},{9,11},{10,... | collective-permute-start | bytes 3145736 | tf_op jit(solution)/shard_map/ppermute | solution.py:233
  (54 other events, 628.0 us)
Sparse Core Ops, SparseCore 0:
  10.2 58.6 all-gather.3
  71.1 149.8 all-gather.5
  222.6 80.2 all-gather.7
  382.1 74.3 reduce-scatter.7
  535.4 50.8 reduce-scatter.3
  588.5 144.8 reduce-scatter.5

commit v5 on v4

--- a/solution.py
+++ b/solution.py
@@ -256,7 +256,7 @@
     return whole
 
 
-def sum_rows(partial, size):
+def sum_rows(partial, size, beside=None):
     partial = partial.astype(jnp.bfloat16)
     if size != 4:
         return lax.psum_scatter(
@@ -286,7 +286,10 @@
     )
     last_y = swap(to_y, "tensor", size, 2)
     last_x = swap(to_x, "tensor", size, 1)
-    return part(me).astype(wide) + last_x.astype(wide) + last_y.astype(wide)
+    own = part(me)
+    if beside is not None:
+        own, _ = lax.optimization_barrier((own, beside))
+    return own.astype(wide) + last_x.astype(wide) + last_y.astype(wide)
 
 
 def sum_all(array, axis, size):
@@ -352,7 +355,8 @@
     narrow = splits[1] + keys_width
     small_full = gather(jnp.concatenate([w_query, w_key, w_value, w_out], axis=1))
     qkv_full, out_full = small_full[:, :narrow], small_full[:, narrow:]
-    gate_full, up_full = jnp.split(gather(jnp.concatenate([w_gate, w_up], axis=1)), 2, axis=1)
+    gate_up_full = gather(jnp.concatenate([w_gate, w_up], axis=1))
+    gate_full, up_full = jnp.split(gate_up_full, 2, axis=1)
     down_full = gather(w_down)
 
     live_all = (doc_ids >= 0).astype(jnp.float32)
@@ -394,29 +398,27 @@
         grad_hidden * up_pre * sigmoid_gate * (1.0 + gate_pre * (1.0 - sigmoid_gate))
     ).astype(jnp.bfloat16)
     grad_up_pre = (grad_hidden * silu_gate).astype(jnp.bfloat16)
-    grad_normed_part = (
-        contract_cols(grad_gate_pre, gate_full) + contract_cols(grad_up_pre, up_full)
-    ).astype(jnp.bfloat16)
-    grad_normed_part, grad_gate_pre, grad_up_pre = lax.optimization_barrier(
-        (grad_normed_part, grad_gate_pre, grad_up_pre)
-    )
-    pair_gate_up = jnp.concatenate(
-        [pair_grad(two_parities, grad_gate_pre, dp), pair_grad(two_parities, grad_up_pre, dp)],
-        axis=1,
-    )
-    grad_normed_own = sum_rows(grad_normed_part, tp)
+    grad_gate_up = jnp.concatenate(
+        lax.optimization_barrier((grad_gate_pre, grad_up_pre)), axis=1
+    )
+    grad_normed_part = contract_cols(grad_gate_up, gate_up_full).astype(jnp.bfloat16)
+    grad_normed_part, grad_gate_up = lax.optimization_barrier((grad_normed_part, grad_gate_up))
+    pair_gate_up = pair_grad(two_parities, grad_gate_up, dp)
+    grad_normed_own = sum_rows(grad_normed_part, tp, beside=pair_gate_up)
     grad_normed_own, pair_gate_up = lax.optimization_barrier((grad_normed_own, pair_gate_up))
     grad_gate, grad_up = jnp.split(sum_pairs(pair_gate_up, dp), 2, axis=1)
     grad_mlp_gain = jnp.sum(grad_normed_own * residual_own * scale_two_own, axis=0)
     grad_residual_own = cotangent.astype(jnp.float32) + norm_back(
         grad_normed_own, residual_own, scale_two_own, mlp_gain
     )
-    grad_residual_bf = gather_rows(grad_residual_own.astype(jnp.bfloat16), tp)
-    grad_residual_bf, hidden = lax.optimization_barrier((grad_residual_bf, hidden))
+    to_gather, hidden = lax.optimization_barrier(
+        (grad_residual_own.astype(jnp.bfloat16), hidden)
+    )
+    grad_residual_bf = gather_rows(to_gather, tp)
+    block_part = contract_cols(hidden, down_full).astype(jnp.bfloat16)
+    grad_residual_bf, block_part = lax.optimization_barrier((grad_residual_bf, block_part))
     grad_mixed = (matmul(grad_residual_bf, out_full) * live_all[:, None]).astype(jnp.bfloat16)
-    block_output = (residual_own + sum_rows(contract_cols(hidden, down_full), tp)).astype(
-        jnp.bfloat16
-    )
+    block_output = (residual_own + sum_rows(block_part, tp)).astype(jnp.bfloat16)
     grad_query_rows, grad_keys, grad_value_rows = attend_back(
         query_rows, key_rows, value_rows, grad_mixed, doc_row, doc_col, tables
     )
@@ -424,8 +426,8 @@
         [grad_query_rows, grad_keys.astype(jnp.bfloat16), grad_value_rows], axis=1
     )
     grad_one_part = contract_cols(grad_qkv_rows, qkv_full).astype(jnp.bfloat16)
-    grad_one_part, grad_qkv_rows, mixed_all = lax.optimization_barrier(
-        (grad_one_part, grad_qkv_rows, mixed_all)
+    grad_one_part, grad_qkv_rows, mixed_all, grad_residual_bf = lax.optimization_barrier(
+        (grad_one_part, grad_qkv_rows, mixed_all, grad_residual_bf)
     )
     pair_small = jnp.concatenate(
         [

time: 755 us -> 736 us (0.975)
  waiting for transfers between devices: 333 us -> 312 us
    ppermute x42 -> x41, waiting for transfers between devices: 186 us -> 171 us  [swap(): return lax.ppermute(array, axis, [(i, i ^ bit) for i in range(size)])]
    concatenate x2 -> x1, other arithmetic: 11.2 us -> 3.16 us  [per_device(): gate_up_full = gather(jnp.concatenate([w_gate, w_up], axis=1))]
    dot_general x5 -> x4, matrix products: 52.8 us -> 48.9 us  [contract_cols(): lax.dot_general(left_side, right_side, (((1,), (1,)), ((), ())), preferre...]
    ppermute x42 -> x41, starting transfers between devices: 44.7 us -> 45.5 us  [swap(): return lax.ppermute(array, axis, [(i, i ^ bit) for i in range(size)])]
    dot_general x10 -> x8, matrix products: 48.9 us -> 48.5 us  [contract_rows(): lax.dot_general(left_side, right_side, (((0,), (0,)), ((), ())), preferre...]
  transfers between devices with their start and end apart: 48 -> 47, of which waited for: 29 -> 30; matrix products, arithmetic and copies ran while one was open for 32% -> 33% of each run, Pallas kernels for 6% -> 6%
where the time goes in v5:
time: 736 us; the launch traced here: 725 us
  waiting for transfers between devices  312 us (42%)
  matrix products  161 us (22%)
  local copies, waits for them, and re-layouts  103 us (14%)
  starting transfers between devices  46.2 us (6%)
  other arithmetic  46 us (6%)
  Pallas kernels  41.5 us (6%)
  between operations  15.5 us (2%)
    ppermute x41, waiting for transfers between devices, swap(): return lax.ppermute(array, axis, [(i, i ^ bit) for i in range(size)])  171 us
    reduce_scatter x3, waiting for transfers between devices, sum_pairs(): lax.psum_scatter(pair_sum, 'dp', scatter_dimension=0, tiled=True, axis_in...  97.9 us
    dot_general x5, matrix products, matmul(): return jnp.dot(left_side, right_side, preferred_element_type=jnp.float32)  64.1 us
    dot_general x4, matrix products, contract_cols(): lax.dot_general(left_side, right_side, (((1,), (1,)), ((), ())), preferre...  48.9 us
    dot_general x8, matrix products, contract_rows(): lax.dot_general(left_side, right_side, (((0,), (0,)), ((), ())), preferre...  48.5 us
    ppermute x41, starting transfers between devices, swap(): return lax.ppermute(array, axis, [(i, i ^ bit) for i in range(size)])  45.5 us
    all_gather x3, waiting for transfers between devices, gather(): return lax.all_gather(weight, 'dp', axis=0, tiled=True)  42.6 us
    pallas_call x1, Pallas kernels, attend_back(): pl.pallas_call(functools.partial(attend_back_kernel, groups), name='atten...  23.2 us
  transfers between devices with their start and end apart: 47, of which 30 were waited for; matrix products, arithmetic and copies ran while one was open for 33% of the time, Pallas kernels for 6%

profile of v5, /device:TPU:0, one launch (start us, length us, event | category | flops | bytes accessed | tf_op | source)
XLA Modules:
  0.0 725.5 jit_solution(6032326529726077811)
XLA Ops:
  23.9 16.1 %collective-permute-done = bf16[256,2048]{1,0:T(8,128)(2,1)} collective-permute-done((bf16[256,2048]{1,0:T(8,128)(2,1)S(1)}, bf16[256,2048]{1,0:T(8,128)(2,1)}, u32[]{:S(2)}, u32[]{:S(2)}) %collective-permute-start) | collective-permute-done | bytes 1048608 | tf_op jit(solution)/shard_map/ppermute | solution.py:233
  61.5 7.4 %all-gather.4.cloned.1.call-done = bf16[2048,1280]{1,0:T(8,128)(2,1)} async-done(((bf16[256,1280]{1,0:T(8,128)(2,1)}), bf16[2048,1280]{1,0:T(8,128)(2,1)}) %all-gather.4.cloned.1.call-update) | async-done | bytes 5242896 | tf_op jit(solution)/shard_map/all_gather | solution.py:353
  68.9 6.2 fusion.6
  77.8 18.3 %attend.1 = (bf16[1024,512]{1,0:T(8,128)(2,1)}, bf16[1024,128]{1,0:T(8,128)(2,1)}, bf16[1024,128]{1,0:T(8,128)(2,1)}, bf16[1024,512]{1,0:T(8,128)(2,1)}) custom-call(f32[1024,512]{1,0:T(8,128)} %split.44.q_ref, f32[1024,128]{1,0:T(8,128)} %get-tuple-element.143.k_ref, f32[1024,128]{1,0:T(8,128)} %get-tuple-element.142.v_ref, s32[2,1,512]{2,1,0:T(1,128)} %bitcast.60, ...), custom_call_target="tpu_custom_call" | custom-call | flops 1073741824 | bytes 8388608 | tf_op jit(solution)/shard_map/attend/pallas_call | solution.py:195
  96.1 4.4 convolution_convert_fusion.3
  107.2 9.7 %collective-permute-done.4 = bf16[128,2048]{1,0:T(8,128)(2,1)} collective-permute-done((bf16[128,2048]{1,0:T(8,128)(2,1)}, bf16[128,2048]{1,0:T(8,128)(2,1)}, u32[]{:S(2)}, u32[]{:S(2)}) %collective-permute-start.4) | collective-permute-done | bytes 524320 | tf_op jit(solution)/shard_map/ppermute | solution.py:233
  126.3 14.5 %collective-permute-done.8 = bf16[256,2048]{0,1:T(8,128)(2,1)} collective-permute-done((bf16[256,2048]{0,1:T(8,128)(2,1)S(1)}, bf16[256,2048]{0,1:T(8,128)(2,1)}, u32[]{:S(2)}, u32[]{:S(2)}) %collective-permute-start.8) | collective-permute-done | bytes 1048608 | tf_op jit(solution)/shard_map/ppermute | solution.py:233
  146.3 17.0 %collective-permute-done.5 = bf16[256,2048]{1,0:T(8,128)(2,1)} collective-permute-done((bf16[256,2048]{1,0:T(8,128)(2,1)}, bf16[256,2048]{1,0:T(8,128)(2,1)}, u32[]{:S(2)}, u32[]{:S(2)}) %collective-permute-start.5) | collective-permute-done | bytes 1048608 | tf_op jit(solution)/shard_map/ppermute | solution.py:233
  176.6 5.8 constant_dynamic-slice_fusion.17
  182.9 13.2 %collective-permute-done.12 = bf16[256,2048]{1,0:T(8,128)(2,1)} collective-permute-done((bf16[256,2048]{1,0:T(8,128)(2,1)S(1)}, bf16[256,2048]{1,0:T(8,128)(2,1)}, u32[]{:S(2)}, u32[]{:S(2)}) %collective-permute-start.12) | collective-permute-done | bytes 1048608 | tf_op jit(solution)/shard_map/ppermute | solution.py:233
  216.9 4.1 all-gather.6.cloned.1.call-done
  221.0 13.1 %fusion.2 = f32[1024,2048]{1,0:T(8,128)S(1)} fusion(bf16[1024,2048]{0,1:T(8,128)(2,1)} %constant_dynamic-update-slice_fusion.5, bf16[2048,4096]{1,0:T(8,128)(2,1)} %all-gather.6.cloned.1.call-done), kind=kOutput, calls=%fused_computation.3 | convolution fusion | flops 8589934592 | bytes 20971520 | tf_op jit(solution)/shard_map/dot_general | solution.py:51
  234.1 19.0 %multiply_convert_fusion.2 = (bf16[1024,2048]{1,0:T(8,128)(2,1)S(1)}, f32[1024,2048]{1,0:T(8,128)}) fusion(f32[1024,2048]{1,0:T(8,128)S(1)} %fusion.2, bf16[1024,2048]{0,1:T(8,128)(2,1)} %constant_dynamic-update-slice_fusion.5, bf16[2048,4096]{1,0:T(8,128)(2,1)} %all-gather.6.cloned.1.call-done), kind=kOutput, calls=%fused_computation.8 | convolution fusion | flops 8602517504 | bytes 33554432 | tf_op jit(solution)/shard_map/dot_general | solution.py:51
  253.1 4.9 convolution_convert_fusion.5
  258.5 4.3 constant_dynamic-slice_fusion.15
  265.7 6.1 add_convert_fusion.1
  271.7 31.1 %all-gather.8.cloned.1.call-done = bf16[2048,2048]{1,0:T(8,128)(2,1)} async-done(((bf16[256,2048]{1,0:T(8,128)(2,1)}), bf16[2048,2048]{1,0:T(8,128)(2,1)}) %all-gather.8.cloned.1.call-update) | async-done | bytes 8388624 | tf_op jit(solution)/shard_map/all_gather | solution.py:353
  302.9 19.5 %multiply_convert_fusion = (bf16[1024,2048]{1,0:T(8,128)(2,1)S(1)}, bf16[1024,2048]{1,0:T(8,128)(2,1)S(1)}) fusion(f32[1024,2048]{1,0:T(8,128)} %copy-done.40, f32[1024,2048]{1,0:T(8,128)} %get-tuple-element.159, bf16[1024,2048]{0,1:T(8,128)(2,1)} %copy-done.4, bf16[2048,2048]{1,0:T(8,128)(2,1)} %all-gather.8.cloned.1.call-done), kind=kOutput, calls=%fused_computation.5 | convolution fusion | flops 8617197568 | bytes 37748736 | tf_op jit(solution)/shard_map/dot_general | solution.py:51
  327.7 23.4 %convolution_convert_fusion.1 = bf16[1024,2048]{1,0:T(8,128)(2,1)S(1)} fusion(bf16[1024,4096]{1,0:T(8,128)(2,1)} %constant_dynamic-update-slice_fusion.20, bf16[2048,4096]{1,0:T(8,128)(2,1)} %all-gather.6.cloned.1.call-done), kind=kOutput, calls=%fused_computation.18 | convolution fusion | flops 17181966336 | bytes 29360128 | tf_op jit(solution)/shard_map/dot_general | solution.py:45
  351.1 15.8 %convolution_convert_fusion = bf16[1024,4096]{1,0:T(8,128)(2,1)} fusion(bf16[1024,1024]{0,1:T(8,128)(2,1)S(1)} %bitcast.51, bf16[1024,4096]{1,0:T(8,128)(2,1)} %constant_dynamic-update-slice_fusion.20), kind=kOutput, calls=%fused_computation.11 | convolution fusion | flops 8594128896 | bytes 18874368 | tf_op jit(solution)/shard_map/dot_general | solution.py:39
  372.9 10.0 %collective-permute-done.18 = bf16[128,2048]{1,0:T(8,128)(2,1)} collective-permute-done((bf16[128,2048]{1,0:T(8,128)(2,1)}, bf16[128,2048]{1,0:T(8,128)(2,1)}, u32[]{:S(2)}, u32[]{:S(2)}) %collective-permute-start.18) | collective-permute-done | bytes 524320 | tf_op jit(solution)/shard_map/ppermute | solution.py:233
  390.3 15.3 %add_convert_fusion = bf16[1024,4096]{1,0:T(8,128)(2,1)} fusion(bf16[1024,4096]{1,0:T(8,128)(2,1)} %collective-permute-done.17, bf16[1024,1024]{0,1:T(8,128)(2,1)S(1)} %bitcast.48, bf16[1024,4096]{1,0:T(8,128)(2,1)} %constant_dynamic-update-slice_fusion.20), kind=kOutput, calls=%fused_computation | convolution fusion | flops 8602517504 | bytes 27262976 | tf_op jit(solution)/shard_map/dot_general | solution.py:39
  405.6 6.1 collective-permute-done.19
  422.4 13.9 %convolution_convert_fusion.2 = bf16[1024,2048]{1,0:T(8,128)(2,1)} fusion(bf16[1024,2048]{1,0:T(8,128)(2,1)} %copy-done.41, bf16[2048,2048]{1,0:T(8,128)(2,1)} %all-gather.8.cloned.1.call-done), kind=kOutput, calls=%fused_computation.19 | convolution fusion | flops 8592031744 | bytes 16777216 | tf_op jit(solution)/shard_map/dot_general | solution.py:45
  436.3 8.1 %collective-permute-done.22 = bf16[256,2048]{1,0:T(8,128)(2,1)S(1)} collective-permute-done((bf16[256,2048]{1,0:T(8,128)(2,1)}, bf16[256,2048]{1,0:T(8,128)(2,1)S(1)}, u32[]{:S(2)}, u32[]{:S(2)}) %collective-permute-start.22) | collective-permute-done | bytes 1048608 | tf_op jit(solution)/shard_map/ppermute | solution.py:233
  462.7 6.2 multiply_convert_fusion.3.grad_ref
  468.8 23.2 %attend_back.1 = (bf16[1024,512]{1,0:T(8,128)(2,1)}, f32[1024,128]{1,0:T(8,128)}, bf16[1024,128]{1,0:T(8,128)(2,1)}) custom-call(bf16[1024,512]{1,0:T(8,128)(2,1)} %get-tuple-element.52.q_ref, bf16[1024,128]{1,0:T(8,128)(2,1)} %get-tuple-element.53.k_ref, bf16[1024,128]{1,0:T(8,128)(2,1)} %get-tuple-element.54.v_ref, ...), custom_call_target="tpu_custom_call" | custom-call | flops 2684354560 | bytes 8388608 | tf_op jit(solution)/shard_map/attend_back/pallas_call | solution.py:216
  494.7 7.3 %convolution_convert_fusion.4 = bf16[1024,2048]{1,0:T(8,128)(2,1)} fusion(bf16[2048,1280]{1,0:T(8,128)(2,1)} %all-gather.4.cloned.1.call-done, bf16[1024,128]{1,0:T(8,128)(2,1)S(1)} %copy-done.26, bf16[1024,128]{1,0:T(8,128)(2,1)S(1)} %convert_element_type.251, bf16[1024,512]{1,0:T(8,128)(2,1)S(1)} %copy-done.25), kind=kOutput, calls=%fused_computation.21 | convolution fusion | flops 3228041216 | bytes 8912896 | tf_op jit(solution)/shard_map/dot_general | solution.py:45
  521.4 11.4 %collective-permute-done.30 = bf16[128,2048]{1,0:T(8,128)(2,1)S(1)} collective-permute-done((bf16[128,2048]{1,0:T(8,128)(2,1)S(1)}, bf16[128,2048]{1,0:T(8,128)(2,1)S(1)}, u32[]{:S(2)}, u32[]{:S(2)}) %collective-permute-start.30) | collective-permute-done | bytes 524320 | tf_op jit(solution)/shard_map/ppermute | solution.py:233
  545.9 28.8 %collective-permute-done.26 = bf16[128,2048]{1,0:T(8,128)(2,1)} collective-permute-done((bf16[128,2048]{1,0:T(8,128)(2,1)}, bf16[128,2048]{1,0:T(8,128)(2,1)}, u32[]{:S(2)}, u32[]{:S(2)}) %collective-permute-start.26) | collective-permute-done | bytes 524320 | tf_op jit(solution)/shard_map/ppermute | solution.py:233
  594.8 9.2 %collective-permute-done.27 = bf16[256,2048]{1,0:T(8,128)(2,1)S(1)} collective-permute-done((bf16[256,2048]{1,0:T(8,128)(2,1)S(1)}, bf16[256,2048]{1,0:T(8,128)(2,1)S(1)}, u32[]{:S(2)}, u32[]{:S(2)}) %collective-permute-start.27) | collective-permute-done | bytes 1048608 | tf_op jit(solution)/shard_map/ppermute | solution.py:233
  616.2 97.9 %reduce-scatter.6.cloned.1.call-done = bf16[256,4096]{1,0:T(8,128)(2,1)} async-done(((bf16[1024,4096]{1,0:T(8,128)(2,1)}), bf16[256,4096]{1,0:T(8,128)(2,1)}) %reduce-scatter.6.cloned.1.call-update) | async-done | bytes 2097168 | tf_op jit(solution)/shard_map/reduce_scatter | solution.py:324
  (285 shorter events, 218.8 us)
Async XLA Ops:
  7.2 61.8 %all-gather.4.cloned.1.call-start = ((), (), s32[]{:S(2)}) async-start(), calls=%async_computation.3 | async-start | bytes 5898240 | tf_op jit(solution)/shard_map/all_gather | solution.py:353
  9.3 211.7 %all-gather.6.cloned.1.call-start = ((), (), s32[]{:S(2)}) async-start(), calls=%async_computation.4 | async-start | bytes 18874368 | tf_op jit(solution)/shard_map/all_gather | solution.py:353
  12.5 290.4 %all-gather.8.cloned.1.call-start = ((), (), s32[]{:S(2)}) async-start(), calls=%async_computation.5 | async-start | bytes 9437184 | tf_op jit(solution)/shard_map/all_gather | solution.py:353
  13.7 26.3 %collective-permute-start = (bf16[256,2048]{1,0:T(8,128)(2,1)S(1)}, bf16[256,2048]{1,0:T(8,128)(2,1)}, u32[]{:S(2)}, u32[]{:S(2)}) collective-permute-start(bf16[256,2048]{1,0:T(8,128)(2,1)S(1)} %fusion.10), channel_id=1, source_target_pairs={{0,1},{1,0},{2,3},{3,2},{4,5},{5,4},{6,7},{7,6},{8,9},{9,8},{10,11... | collective-permute-start | bytes 3145736 | tf_op jit(solution)/shard_map/ppermute | solution.py:233
  16.8 26.9 %collective-permute-start.1 = (bf16[256,2048]{1,0:T(8,128)(2,1)S(1)}, bf16[256,2048]{1,0:T(8,128)(2,1)}, u32[]{:S(2)}, u32[]{:S(2)}) collective-permute-start(bf16[256,2048]{1,0:T(8,128)(2,1)S(1)} %fusion.10), channel_id=1, source_target_pairs={{0,2},{1,3},{2,0},{3,1},{4,6},{5,7},{6,4},{7,5},{8,10},{9,11},{10,... | collective-permute-start | bytes 3145736 | tf_op jit(solution)/shard_map/ppermute | solution.py:233
  41.9 15.0 %collective-permute-start.2 = (bf16[128,2048]{1,0:T(8,128)(2,1)}, bf16[128,2048]{1,0:T(8,128)(2,1)}, u32[]{:S(2)}, u32[]{:S(2)}) collective-permute-start(bf16[128,2048]{1,0:T(8,128)(2,1)} %slice.48), channel_id=1, source_target_pairs={{0,2},{1,3},{2,0},{3,1},{4,6},{5,7},{6,4},{7,5},{8,10},{9,11},{10,... | collective-permute-start | bytes 1572872 | tf_op jit(solution)/shard_map/ppermute | solution.py:233
  101.8 15.1 %collective-permute-start.4 = (bf16[128,2048]{1,0:T(8,128)(2,1)}, bf16[128,2048]{1,0:T(8,128)(2,1)}, u32[]{:S(2)}, u32[]{:S(2)}) collective-permute-start(bf16[128,2048]{1,0:T(8,128)(2,1)} %get-tuple-element.139), channel_id=1, source_target_pairs={{0,2},{1,3},{2,0},{3,1},{4,6},{5,7},{6,4},{7,5},{8,10},{9,11},{10,... | collective-permute-start | bytes 1572872 | tf_op jit(solution)/shard_map/ppermute | solution.py:233
  103.2 15.1 %collective-permute-start.6 = (bf16[128,2048]{1,0:T(8,128)(2,1)}, bf16[128,2048]{1,0:T(8,128)(2,1)}, u32[]{:S(2)}, u32[]{:S(2)}) collective-permute-start(bf16[128,2048]{1,0:T(8,128)(2,1)} %get-tuple-element.138), channel_id=1, source_target_pairs={{0,1},{1,0},{2,3},{3,2},{4,5},{5,4},{6,7},{7,6},{8,9},{9,8},{10,11... | collective-permute-start | bytes 1572872 | tf_op jit(solution)/shard_map/ppermute | solution.py:233
  105.2 35.6 %collective-permute-start.8 = (bf16[256,2048]{0,1:T(8,128)(2,1)S(1)}, bf16[256,2048]{0,1:T(8,128)(2,1)}, u32[]{:S(2)}, u32[]{:S(2)}) collective-permute-start(bf16[256,2048]{0,1:T(8,128)(2,1)S(1)} %copy.43), channel_id=1, source_target_pairs={{0,1},{1,0},{2,3},{3,2},{4,5},{5,4},{6,7},{7,6},{8,9},{9,8},{10,11... | collective-permute-start | bytes 3145736 | tf_op jit(solution)/shard_map/ppermute | solution.py:233
  105.8 37.5 %collective-permute-start.9 = (bf16[256,2048]{0,1:T(8,128)(2,1)S(1)}, bf16[256,2048]{0,1:T(8,128)(2,1)S(1)}, u32[]{:S(2)}, u32[]{:S(2)}) collective-permute-start(bf16[256,2048]{0,1:T(8,128)(2,1)S(1)} %copy.43), channel_id=1, source_target_pairs={{0,2},{1,3},{2,0},{3,1},{4,6},{5,7},{6,4},{7,5},{8,10},{9,11},{10,... | collective-permute-start | bytes 3145736 | tf_op jit(solution)/shard_map/ppermute | solution.py:233
  121.5 41.8 %collective-permute-start.5 = (bf16[256,2048]{1,0:T(8,128)(2,1)}, bf16[256,2048]{1,0:T(8,128)(2,1)}, u32[]{:S(2)}, u32[]{:S(2)}) collective-permute-start(bf16[256,2048]{1,0:T(8,128)(2,1)} %pad_maximum_fusion.3), channel_id=1, source_target_pairs={{0,1},{1,0},{2,3},{3,2},{4,5},{5,4},{6,7},{7,6},{8,9},{9,8},{10,11... | collective-permute-start | bytes 3145736 | tf_op jit(solution)/shard_map/ppermute | solution.py:233
  124.0 39.3 %collective-permute-start.7 = (bf16[256,2048]{1,0:T(8,128)(2,1)}, bf16[256,2048]{1,0:T(8,128)(2,1)}, u32[]{:S(2)}, u32[]{:S(2)}) collective-permute-start(bf16[256,2048]{1,0:T(8,128)(2,1)} %pad_maximum_fusion.4), channel_id=1, source_target_pairs={{0,2},{1,3},{2,0},{3,1},{4,6},{5,7},{6,4},{7,5},{8,10},{9,11},{10,... | collective-permute-start | bytes 3145736 | tf_op jit(solution)/shard_map/ppermute | solution.py:233
  125.4 417.6 %reduce-scatter.8.cloned.1.call-start = ((), (), s32[]{:S(2)}) async-start(), calls=%async_computation.8 | async-start | bytes 5242880 | tf_op jit(solution)/shard_map/reduce_scatter | solution.py:324
  141.9 31.1 %collective-permute-start.10 = (bf16[128,2048]{0,1:T(8,128)(2,1)S(1)}, bf16[128,2048]{0,1:T(8,128)(2,1)S(1)}, u32[]{:S(2)}, u32[]{:S(2)}) collective-permute-start(bf16[128,2048]{0,1:T(8,128)(2,1)S(1)} %slice.52), channel_id=1, source_target_pairs={{0,2},{1,3},{2,0},{3,1},{4,6},{5,7},{6,4},{7,5},{8,10},{9,11},{10,... | collective-permute-start | bytes 1572872 | tf_op jit(solution)/shard_map/ppermute | solution.py:233
  143.4 31.1 %collective-permute-start.11 = (bf16[128,2048]{0,1:T(8,128)(2,1)S(1)}, bf16[128,2048]{0,1:T(8,128)(2,1)S(1)}, u32[]{:S(2)}, u32[]{:S(2)}) collective-permute-start(bf16[128,2048]{0,1:T(8,128)(2,1)S(1)} %slice.53), channel_id=1, source_target_pairs={{0,1},{1,0},{2,3},{3,2},{4,5},{5,4},{6,7},{7,6},{8,9},{9,8},{10,11... | collective-permute-start | bytes 1572872 | tf_op jit(solution)/shard_map/ppermute | solution.py:233
  166.8 29.3 %collective-permute-start.12 = (bf16[256,2048]{1,0:T(8,128)(2,1)S(1)}, bf16[256,2048]{1,0:T(8,128)(2,1)}, u32[]{:S(2)}, u32[]{:S(2)}) collective-permute-start(bf16[256,2048]{1,0:T(8,128)(2,1)S(1)} %multiply_convert_fusion.4), channel_id=1, source_target_pairs={{0,1},{1,0},{2,3},{3,2},{4,5},{5,4},{6,7},{7,6},{8,9},{9,8},{10,11... | collective-permute-start | bytes 3145736 | tf_op jit(solution)/shard_map/ppermute | solution.py:233
  168.4 30.4 %collective-permute-start.13 = (bf16[256,2048]{1,0:T(8,128)(2,1)S(1)}, bf16[256,2048]{1,0:T(8,128)(2,1)}, u32[]{:S(2)}, u32[]{:S(2)}) collective-permute-start(bf16[256,2048]{1,0:T(8,128)(2,1)S(1)} %multiply_convert_fusion.4), channel_id=1, source_target_pairs={{0,2},{1,3},{2,0},{3,1},{4,6},{5,7},{6,4},{7,5},{8,10},{9,11},{10,... | collective-permute-start | bytes 3145736 | tf_op jit(solution)/shard_map/ppermute | solution.py:233
  366.9 23.4 %collective-permute-start.17 = (bf16[1024,4096]{1,0:T(8,128)(2,1)}, bf16[1024,4096]{1,0:T(8,128)(2,1)}, u32[]{:S(2)}, u32[]{:S(2)}) collective-permute-start(bf16[1024,4096]{1,0:T(8,128)(2,1)} %convolution_convert_fusion), channel_id=1, source_target_pairs={{0,4},{4,0},{8,12},{12,8},{16,20},{20,16},{24,28},{28,24},{1,5},{5... | collective-permute-start | bytes 25165832 | tf_op jit(solution)/shard_map/ppermute | solution.py:233
  368.5 14.4 %collective-permute-start.18 = (bf16[128,2048]{1,0:T(8,128)(2,1)}, bf16[128,2048]{1,0:T(8,128)(2,1)}, u32[]{:S(2)}, u32[]{:S(2)}) collective-permute-start(bf16[128,2048]{1,0:T(8,128)(2,1)} %get-tuple-element.127), channel_id=1, source_target_pairs={{0,2},{1,3},{2,0},{3,1},{4,6},{5,7},{6,4},{7,5},{8,10},{9,11},{10,... | collective-permute-start | bytes 1572872 | tf_op jit(solution)/shard_map/ppermute | solution.py:233
  371.4 239.3 %reduce-scatter.4.cloned.1.call-start = ((), (), s32[]{:S(2)}) async-start(), calls=%async_computation.6 | async-start | bytes 3276800 | tf_op jit(solution)/shard_map/reduce_scatter | solution.py:324
  387.2 24.5 %collective-permute-start.19 = (bf16[256,2048]{1,0:T(8,128)(2,1)}, bf16[256,2048]{1,0:T(8,128)(2,1)}, u32[]{:S(2)}, u32[]{:S(2)}) collective-permute-start(bf16[256,2048]{1,0:T(8,128)(2,1)} %pad_maximum_fusion.5), channel_id=1, source_target_pairs={{0,1},{1,0},{2,3},{3,2},{4,5},{5,4},{6,7},{7,6},{8,9},{9,8},{10,11... | collective-permute-start | bytes 3145736 | tf_op jit(solution)/shard_map/ppermute | solution.py:233
  389.7 24.2 %collective-permute-start.21 = (bf16[256,2048]{1,0:T(8,128)(2,1)}, bf16[256,2048]{1,0:T(8,128)(2,1)}, u32[]{:S(2)}, u32[]{:S(2)}) collective-permute-start(bf16[256,2048]{1,0:T(8,128)(2,1)} %pad_maximum_fusion.6), channel_id=1, source_target_pairs={{0,2},{1,3},{2,0},{3,1},{4,6},{5,7},{6,4},{7,5},{8,10},{9,11},{10,... | collective-permute-start | bytes 3145736 | tf_op jit(solution)/shard_map/ppermute | solution.py:233
  421.2 23.3 %collective-permute-start.22 = (bf16[256,2048]{1,0:T(8,128)(2,1)}, bf16[256,2048]{1,0:T(8,128)(2,1)S(1)}, u32[]{:S(2)}, u32[]{:S(2)}) collective-permute-start(bf16[256,2048]{1,0:T(8,128)(2,1)} %get-tuple-element.49), channel_id=1, source_target_pairs={{0,1},{1,0},{2,3},{3,2},{4,5},{5,4},{6,7},{7,6},{8,9},{9,8},{10,11... | collective-permute-start | bytes 3145736 | tf_op jit(solution)/shard_map/ppermute | solution.py:233
  421.7 24.2 %collective-permute-start.23 = (bf16[256,2048]{1,0:T(8,128)(2,1)}, bf16[256,2048]{1,0:T(8,128)(2,1)S(1)}, u32[]{:S(2)}, u32[]{:S(2)}) collective-permute-start(bf16[256,2048]{1,0:T(8,128)(2,1)} %get-tuple-element.49), channel_id=1, source_target_pairs={{0,2},{1,3},{2,0},{3,1},{4,6},{5,7},{6,4},{7,5},{8,10},{9,11},{10,... | collective-permute-start | bytes 3145736 | tf_op jit(solution)/shard_map/ppermute | solution.py:233
  516.2 197.9 %reduce-scatter.6.cloned.1.call-start = ((), (), s32[]{:S(2)}) async-start(), calls=%async_computation.7 | async-start | bytes 10485760 | tf_op jit(solution)/shard_map/reduce_scatter | solution.py:324
  536.5 40.4 %collective-permute-start.31 = (bf16[256,2048]{1,0:T(8,128)(2,1)}, bf16[256,2048]{1,0:T(8,128)(2,1)}, u32[]{:S(2)}, u32[]{:S(2)}) collective-permute-start(bf16[256,2048]{1,0:T(8,128)(2,1)} %pad_maximum_fusion.9), channel_id=1, source_target_pairs={{0,1},{1,0},{2,3},{3,2},{4,5},{5,4},{6,7},{7,6},{8,9},{9,8},{10,11... | collective-permute-start | bytes 3145736 | tf_op jit(solution)/shard_map/ppermute | solution.py:233
  539.0 37.9 %collective-permute-start.33 = (bf16[256,2048]{1,0:T(8,128)(2,1)}, bf16[256,2048]{1,0:T(8,128)(2,1)}, u32[]{:S(2)}, u32[]{:S(2)}) collective-permute-start(bf16[256,2048]{1,0:T(8,128)(2,1)} %pad_maximum_fusion.10), channel_id=1, source_target_pairs={{0,2},{1,3},{2,0},{3,1},{4,6},{5,7},{6,4},{7,5},{8,10},{9,11},{10,... | collective-permute-start | bytes 3145736 | tf_op jit(solution)/shard_map/ppermute | solution.py:233
  541.0 33.6 %collective-permute-start.26 = (bf16[128,2048]{1,0:T(8,128)(2,1)}, bf16[128,2048]{1,0:T(8,128)(2,1)}, u32[]{:S(2)}, u32[]{:S(2)}) collective-permute-start(bf16[128,2048]{1,0:T(8,128)(2,1)} %get-tuple-element.121), channel_id=1, source_target_pairs={{0,2},{1,3},{2,0},{3,1},{4,6},{5,7},{6,4},{7,5},{8,10},{9,11},{10,... | collective-permute-start | bytes 1572872 | tf_op jit(solution)/shard_map/ppermute | solution.py:233
  542.4 32.3 %collective-permute-start.28 = (bf16[128,2048]{1,0:T(8,128)(2,1)}, bf16[128,2048]{1,0:T(8,128)(2,1)}, u32[]{:S(2)}, u32[]{:S(2)}) collective-permute-start(bf16[128,2048]{1,0:T(8,128)(2,1)} %get-tuple-element.120), channel_id=1, source_target_pairs={{0,1},{1,0},{2,3},{3,2},{4,5},{5,4},{6,7},{7,6},{8,9},{9,8},{10,11... | collective-permute-start | bytes 1572872 | tf_op jit(solution)/shard_map/ppermute | solution.py:233
  580.7 23.3 %collective-permute-start.27 = (bf16[256,2048]{1,0:T(8,128)(2,1)S(1)}, bf16[256,2048]{1,0:T(8,128)(2,1)S(1)}, u32[]{:S(2)}, u32[]{:S(2)}) collective-permute-start(bf16[256,2048]{1,0:T(8,128)(2,1)S(1)} %pad_maximum_fusion.7), channel_id=1, source_target_pairs={{0,1},{1,0},{2,3},{3,2},{4,5},{5,4},{6,7},{7,6},{8,9},{9,8},{10,11... | collective-permute-start | bytes 3145736 | tf_op jit(solution)/shard_map/ppermute | solution.py:233
  584.9 22.4 %collective-permute-start.29 = (bf16[256,2048]{1,0:T(8,128)(2,1)S(1)}, bf16[256,2048]{1,0:T(8,128)(2,1)S(1)}, u32[]{:S(2)}, u32[]{:S(2)}) collective-permute-start(bf16[256,2048]{1,0:T(8,128)(2,1)S(1)} %pad_maximum_fusion.8), channel_id=1, source_target_pairs={{0,2},{1,3},{2,0},{3,1},{4,6},{5,7},{6,4},{7,5},{8,10},{9,11},{10,... | collective-permute-start | bytes 3145736 | tf_op jit(solution)/shard_map/ppermute | solution.py:233
  593.7 16.4 %collective-permute-start.40 = (f32[2,2048]{1,0:T(2,128)S(1)}, f32[2,2048]{1,0:T(2,128)S(1)}, u32[]{:S(2)}, u32[]{:S(2)}) collective-permute-start(f32[2,2048]{1,0:T(2,128)S(1)} %add.276), channel_id=1, source_target_pairs={{0,16},{4,20},{8,24},{12,28},{16,0},{20,4},{24,8},{28,12},{1,17},{... | collective-permute-start | bytes 49160 | tf_op jit(solution)/shard_map/ppermute | solution.py:233
  (58 other events, 640.5 us)
Sparse Core Ops, SparseCore 0:
  10.2 58.6 all-gather.3
  71.1 149.8 all-gather.5
  222.6 80.2 all-gather.7
  371.6 73.4 reduce-scatter.7
  516.3 50.5 reduce-scatter.3
  569.2 144.8 reduce-scatter.5

commit v6 on v5

--- a/solution.py
+++ b/solution.py
@@ -272,24 +272,16 @@
     from_x = swap(part(me ^ 3, 0, half), "tensor", size, 1)
     from_y = swap(part(me ^ 3, half, half), "tensor", size, 2)
     wide = jnp.float32
-    to_y = jnp.concatenate(
-        [
-            (part(me ^ 2, 0, half).astype(wide) + from_x.astype(wide)).astype(jnp.bfloat16),
-            part(me ^ 2, half, half),
-        ]
-    )
-    to_x = jnp.concatenate(
-        [
-            part(me ^ 1, 0, half),
-            (part(me ^ 1, half, half).astype(wide) + from_y.astype(wide)).astype(jnp.bfloat16),
-        ]
-    )
+    near_low, near_high = part(me ^ 2, 0, half), part(me ^ 1, half, half)
+    if beside is not None:
+        near_low, near_high, _ = lax.optimization_barrier((near_low, near_high, beside))
+    near_low = (near_low.astype(wide) + from_x.astype(wide)).astype(jnp.bfloat16)
+    near_high = (near_high.astype(wide) + from_y.astype(wide)).astype(jnp.bfloat16)
+    to_y = jnp.concatenate([near_low, part(me ^ 2, half, half)])
+    to_x = jnp.concatenate([part(me ^ 1, 0, half), near_high])
     last_y = swap(to_y, "tensor", size, 2)
     last_x = swap(to_x, "tensor", size, 1)
-    own = part(me)
-    if beside is not None:
-        own, _ = lax.optimization_barrier((own, beside))
-    return own.astype(wide) + last_x.astype(wide) + last_y.astype(wide)
+    return part(me).astype(wide) + last_x.astype(wide) + last_y.astype(wide)
 
 
 def sum_all(array, axis, size):
@@ -302,31 +294,74 @@
     return array
 
 
-def parity_columns(rows, size):
-    mine = lax.axis_index("dp") % 2
+def odd_device():
+    return lax.axis_index("dp") % 2 == 1
+
+
+def to_pairs(rows, size):
     cut = rows.reshape(rows.shape[0], size // 2, 2, rows.shape[1] // size)
-
-    def pick(which):
-        return lax.dynamic_index_in_dim(cut, which, 2, keepdims=False).reshape(rows.shape[0], -1)
-
-    return pick(mine), pick(1 - mine)
-
-
-def pair_grad(parities, right_side, size):
-    mine, other = parities
-    from_pair = swap(contract_rows(other, right_side).astype(jnp.bfloat16), "dp", size, 1)
-    pair_sum = contract_rows(mine, right_side) + from_pair.astype(jnp.float32)
+    even = cut[:, :, 0].reshape(rows.shape[0], -1)
+    odd = cut[:, :, 1].reshape(rows.shape[0], -1)
+    flip = odd_device()
+    return jnp.concatenate([jnp.where(flip, odd, even), jnp.where(flip, even, odd)], axis=1)
+
+
+def from_pairs(rows, size):
+    mine, other = jnp.split(rows, 2, axis=1)
+    flip = odd_device()
+    shape = (rows.shape[0], size // 2, rows.shape[1] // size)
+    even = jnp.where(flip, other, mine).reshape(shape)
+    odd = jnp.where(flip, mine, other).reshape(shape)
+    return jnp.stack([even, odd], axis=2).reshape(rows.shape)
+
+
+def parity_groups(size):
+    return [list(range(0, size, 2)), list(range(1, size, 2))]
+
+
+def gather_parity(weight, size):
+    return lax.all_gather(
+        weight, "dp", axis=0, tiled=True, axis_index_groups=parity_groups(size)
+    )
+
+
+def with_partner(mine, size):
+    return mine, swap(mine, "dp", size, 1)
+
+
+def columns(pair, start, stop):
+    return tuple(part[:, start:stop] for part in pair)
+
+
+def matmul_pair(left_side, pair):
+    mine, other = jnp.split(left_side, 2, axis=1)
+    return matmul(other, pair[1]) + matmul(mine, pair[0])
+
+
+def contract_pair(left_side, pair):
+    return jnp.concatenate(
+        [contract_cols(left_side, part).astype(jnp.bfloat16) for part in pair], axis=1
+    )
+
+
+def other_grad(left_side, right_side):
+    return contract_rows(jnp.split(left_side, 2, axis=1)[1], right_side).astype(jnp.bfloat16)
+
+
+def pair_grad(left_side, right_side, size, other=None):
+    other = other_grad(left_side, right_side) if other is None else other
+    from_pair = swap(other, "dp", size, 1)
+    pair_sum = contract_rows(jnp.split(left_side, 2, axis=1)[0], right_side) + from_pair.astype(jnp.float32)
     return pair_sum.astype(jnp.bfloat16)
 
 
 def sum_pairs(pair_sum, size):
-    groups = [list(range(0, size, 2)), list(range(1, size, 2))]
     return lax.psum_scatter(
         pair_sum,
         "dp",
         scatter_dimension=0,
         tiled=True,
-        axis_index_groups=groups,
+        axis_index_groups=parity_groups(size),
     ).astype(jnp.float32)
 
 
@@ -349,51 +384,55 @@
     heads_width, keys_width = w_query.shape[1], w_key.shape[1]
     splits = (heads_width, heads_width + keys_width)
 
-    def gather(weight):
-        return lax.all_gather(weight, "dp", axis=0, tiled=True)
-
     narrow = splits[1] + keys_width
-    small_full = gather(jnp.concatenate([w_query, w_key, w_value, w_out], axis=1))
-    qkv_full, out_full = small_full[:, :narrow], small_full[:, narrow:]
-    gate_up_full = gather(jnp.concatenate([w_gate, w_up], axis=1))
-    gate_full, up_full = jnp.split(gate_up_full, 2, axis=1)
-    down_full = gather(w_down)
+    small_full = with_partner(
+        gather_parity(jnp.concatenate([w_query, w_key, w_value, w_out], axis=1), dp), dp
+    )
+    qkv_full = columns(small_full, 0, narrow)
+    out_full = columns(small_full, narrow, narrow + heads_width)
+    gate_up_mine = gather_parity(jnp.concatenate([w_gate, w_up], axis=1), dp)
+    down_mine = gather_parity(w_down, dp)
+    attn_gain = to_pairs(attn_gain[None, :], dp)[0]
+    mlp_gain = to_pairs(mlp_gain[None, :], dp)[0]
+    cotangent = to_pairs(cotangent, dp)
 
     live_all = (doc_ids >= 0).astype(jnp.float32)
     doc_row = doc_ids.reshape(-1, 1, SEQ)
     doc_col = doc_ids.reshape(-1, 1)
     tables = rotary_tables(SEQ, HD, heads_width // keys_width)
 
-    input_own = block_input.astype(jnp.float32)
+    input_own = to_pairs(block_input, dp).astype(jnp.float32)
     scale_one = norm_scale(input_own)
     normed_one = gather_rows(
         (input_own * scale_one * attn_gain[None, :]).astype(jnp.bfloat16), tp
     )
     grad_full = gather_rows(cotangent, tp)
 
-    qkv_pre = matmul(normed_one, qkv_full)
+    qkv_pre = matmul_pair(normed_one, qkv_full)
     query_rows, key_rows, value_rows, mixed_all = attend(
         *jnp.split(qkv_pre, splits, axis=1), doc_row, doc_col, tables
     )
-    residual_own = input_own + sum_rows(contract_cols(mixed_all, out_full), tp)
+    residual_own = input_own + sum_rows(contract_pair(mixed_all, out_full), tp)
     scale_two_own = norm_scale(residual_own)
     normed_two = gather_rows(
         (residual_own * scale_two_own * mlp_gain[None, :]).astype(jnp.bfloat16), tp
     )
-    gate_pre = matmul(normed_two, gate_full)
-    up_pre = matmul(normed_two, up_full)
+    normed_two, gate_up_mine = lax.optimization_barrier((normed_two, gate_up_mine))
+    gate_up_full = with_partner(gate_up_mine, dp)
+    units = w_gate.shape[1]
+    gate_full = columns(gate_up_full, 0, units)
+    up_full = columns(gate_up_full, units, 2 * units)
+    gate_pre = matmul_pair(normed_two, gate_full)
+    up_pre = matmul_pair(normed_two, up_full)
     sigmoid_gate = jax.nn.sigmoid(gate_pre)
     silu_gate = gate_pre * sigmoid_gate
     hidden = (silu_gate * up_pre).astype(jnp.bfloat16)
-    pair_down = pair_grad(parity_columns(grad_full, dp), hidden, dp)
-    one_parities = parity_columns(normed_one, dp)
-    two_parities = parity_columns(normed_two, dp)
-    pair_down, down_full, one_parities, two_parities = lax.optimization_barrier(
-        (pair_down, down_full, one_parities, two_parities)
-    )
+    pair_down = pair_grad(grad_full, hidden, dp)
+    pair_down, down_mine = lax.optimization_barrier((pair_down, down_mine))
+    down_full = with_partner(down_mine, dp)
     grad_down = sum_pairs(pair_down, dp)
 
-    grad_hidden = matmul(grad_full, down_full)
+    grad_hidden = matmul_pair(grad_full, down_full)
     grad_gate_pre = (
         grad_hidden * up_pre * sigmoid_gate * (1.0 + gate_pre * (1.0 - sigmoid_gate))
     ).astype(jnp.bfloat16)
@@ -401,11 +440,12 @@
     grad_gate_up = jnp.concatenate(
         lax.optimization_barrier((grad_gate_pre, grad_up_pre)), axis=1
     )
-    grad_normed_part = contract_cols(grad_gate_up, gate_up_full).astype(jnp.bfloat16)
+    other_gate_up = other_grad(normed_two, grad_gate_up)
+    other_gate_up, grad_gate_up = lax.optimization_barrier((other_gate_up, grad_gate_up))
+    grad_normed_part = contract_pair(grad_gate_up, gate_up_full)
     grad_normed_part, grad_gate_up = lax.optimization_barrier((grad_normed_part, grad_gate_up))
-    pair_gate_up = pair_grad(two_parities, grad_gate_up, dp)
+    pair_gate_up = pair_grad(normed_two, grad_gate_up, dp, other_gate_up)
     grad_normed_own = sum_rows(grad_normed_part, tp, beside=pair_gate_up)
-    grad_normed_own, pair_gate_up = lax.optimization_barrier((grad_normed_own, pair_gate_up))
     grad_gate, grad_up = jnp.split(sum_pairs(pair_gate_up, dp), 2, axis=1)
     grad_mlp_gain = jnp.sum(grad_normed_own * residual_own * scale_two_own, axis=0)
     grad_residual_own = cotangent.astype(jnp.float32) + norm_back(
@@ -415,24 +455,26 @@
         (grad_residual_own.astype(jnp.bfloat16), hidden)
     )
     grad_residual_bf = gather_rows(to_gather, tp)
-    block_part = contract_cols(hidden, down_full).astype(jnp.bfloat16)
+    block_part = contract_pair(hidden, down_full)
     grad_residual_bf, block_part = lax.optimization_barrier((grad_residual_bf, block_part))
-    grad_mixed = (matmul(grad_residual_bf, out_full) * live_all[:, None]).astype(jnp.bfloat16)
-    block_output = (residual_own + sum_rows(block_part, tp)).astype(jnp.bfloat16)
+    grad_mixed = (matmul_pair(grad_residual_bf, out_full) * live_all[:, None]).astype(jnp.bfloat16)
+    block_output = from_pairs(
+        (residual_own + sum_rows(block_part, tp)).astype(jnp.bfloat16), dp
+    )
     grad_query_rows, grad_keys, grad_value_rows = attend_back(
         query_rows, key_rows, value_rows, grad_mixed, doc_row, doc_col, tables
     )
     grad_qkv_rows = jnp.concatenate(
         [grad_query_rows, grad_keys.astype(jnp.bfloat16), grad_value_rows], axis=1
     )
-    grad_one_part = contract_cols(grad_qkv_rows, qkv_full).astype(jnp.bfloat16)
+    grad_one_part = contract_pair(grad_qkv_rows, qkv_full)
     grad_one_part, grad_qkv_rows, mixed_all, grad_residual_bf = lax.optimization_barrier(
         (grad_one_part, grad_qkv_rows, mixed_all, grad_residual_bf)
     )
     pair_small = jnp.concatenate(
         [
-            pair_grad(one_parities, grad_qkv_rows, dp),
-            pair_grad(parity_columns(grad_residual_bf, dp), mixed_all, dp),
+            pair_grad(normed_one, grad_qkv_rows, dp),
+            pair_grad(grad_residual_bf, mixed_all, dp),
         ],
         axis=1,
     )
@@ -441,10 +483,13 @@
     )
     grad_normed_one = sum_rows(grad_one_part, tp)
     grad_attn_gain = jnp.sum(grad_normed_one * input_own * scale_one, axis=0)
-    input_grad = (
-        grad_residual_own + norm_back(grad_normed_one, input_own, scale_one, attn_gain)
-    ).astype(jnp.bfloat16)
-    gains = jnp.stack([grad_attn_gain, grad_mlp_gain])
+    input_grad = from_pairs(
+        (
+            grad_residual_own + norm_back(grad_normed_one, input_own, scale_one, attn_gain)
+        ).astype(jnp.bfloat16),
+        dp,
+    )
+    gains = from_pairs(jnp.stack([grad_attn_gain, grad_mlp_gain]), dp)
     gains = sum_all(sum_all(gains, "tensor", tp), "dp", dp)
     return (
         block_output,

time: 736 us -> 769 us (1.045)
  waiting for transfers between devices: 312 us -> 356 us
  local copies, waits for them, and re-layouts: 103 us -> 70.7 us
  matrix products: 161 us -> 176 us
  other arithmetic: 46 us -> 60 us
    ppermute x41 -> x44, waiting for transfers between devices: 171 us -> 225 us  [swap(): return lax.ppermute(array, axis, [(i, i ^ bit) for i in range(size)])]
    dot_general x5 -> x10, matrix products: 64.1 us -> 81.3 us  [matmul(): return jnp.dot(left_side, right_side, preferred_element_type=jnp.float32)]
    ppermute x12 -> x0, local copies, waits for them, and re-layouts: 16.5 us -> none  [swap(): return lax.ppermute(array, axis, [(i, i ^ bit) for i in range(size)])]
    dynamic_slice x3 -> x0, local copies, waits for them, and re-layouts: 12.9 us -> none  [pick(): lax.dynamic_index_in_dim(cut, which, 2, keepdims=False)]
    all_gather x3, waiting for transfers between devices: 42.6 us -> 33.6 us  [gather_parity(): lax.all_gather(weight, 'dp', axis=0, tiled=True, axis_index_groups=parity...]
    concatenate x10 -> x17, other arithmetic: 11.5 us -> 20.2 us  [the longest x4 7.34 us: contract_pair(): jnp.concatenate([contract_cols(left_side, part).astype(jnp.bfloat16) for...]
    unnamed x92 -> x113, local copies, waits for them, and re-layouts: 9.68 us -> 16.7 us
    dot_general x4 -> x8, matrix products: 48.9 us -> 42.5 us  [contract_cols(): lax.dot_general(left_side, right_side, (((1,), (1,)), ((), ())), preferre...]
  transfers between devices with their start and end apart: 47 -> 50, of which waited for: 30 -> 32; matrix products, arithmetic and copies ran while one was open for 33% -> 35% of each run, Pallas kernels for 6% -> 5%
where the time goes in v6:
time: 769 us; the launch traced here: 760 us
  waiting for transfers between devices  356 us (46%)
  matrix products  176 us (23%)
  local copies, waits for them, and re-layouts  70.7 us (9%)
  other arithmetic  60 us (8%)
  Pallas kernels  41.5 us (5%)
  starting transfers between devices  41.3 us (5%)
  between operations  15.5 us (2%)
    ppermute x44, waiting for transfers between devices, swap(): return lax.ppermute(array, axis, [(i, i ^ bit) for i in range(size)])  225 us
    reduce_scatter x3, waiting for transfers between devices, sum_pairs(): lax.psum_scatter(pair_sum, 'dp', scatter_dimension=0, tiled=True, axis_in...  96.6 us
    dot_general x10, matrix products, matmul(): return jnp.dot(left_side, right_side, preferred_element_type=jnp.float32)  81.3 us
    dot_general x8, matrix products, contract_rows(): lax.dot_general(left_side, right_side, (((0,), (0,)), ((), ())), preferre...  52.1 us
    dot_general x8, matrix products, contract_cols(): lax.dot_general(left_side, right_side, (((1,), (1,)), ((), ())), preferre...  42.5 us
    ppermute x44, starting transfers between devices, swap(): return lax.ppermute(array, axis, [(i, i ^ bit) for i in range(size)])  40.6 us
    all_gather x3, waiting for transfers between devices, gather_parity(): lax.all_gather(weight, 'dp', axis=0, tiled=True, axis_index_groups=parity...  33.6 us
    pallas_call x1, Pallas kernels, attend_back(): pl.pallas_call(functools.partial(attend_back_kernel, groups), name='atten...  23.2 us
  transfers between devices with their start and end apart: 50, of which 32 were waited for; matrix products, arithmetic and copies ran while one was open for 35% of the time, Pallas kernels for 5%

profile of v6, /device:TPU:0, one launch (start us, length us, event | category | flops | bytes accessed | tf_op | source)
XLA Modules:
  0.0 760.4 jit_solution(8353585200672408082)
XLA Ops:
  36.0 31.6 %all-gather.4.cloned.1.call-done = bf16[1024,1280]{1,0:T(8,128)(2,1)} async-done(((bf16[256,1280]{1,0:T(8,128)(2,1)}), bf16[1024,1280]{1,0:T(8,128)(2,1)}) %all-gather.4.cloned.1.call-update) | async-done | bytes 2621456 | tf_op jit(solution)/shard_map/all_gather | solution.py:323
  76.7 17.2 %collective-permute-done.1 = bf16[256,2048]{0,1:T(8,128)(2,1)S(1)} collective-permute-done((bf16[256,2048]{0,1:T(8,128)(2,1)}, bf16[256,2048]{0,1:T(8,128)(2,1)S(1)}, u32[]{:S(2)}, u32[]{:S(2)}) %collective-permute-start.1) | collective-permute-done | bytes 1048608 | tf_op jit(solution)/shard_map/ppermute | solution.py:233
  97.7 7.0 collective-permute-done.2
  118.2 18.4 %attend.1 = (bf16[1024,512]{1,0:T(8,128)(2,1)}, bf16[1024,128]{1,0:T(8,128)(2,1)}, bf16[1024,128]{1,0:T(8,128)(2,1)}, bf16[1024,512]{1,0:T(8,128)(2,1)}) custom-call(f32[1024,512]{1,0:T(8,128)} %split.110.q_ref, f32[1024,128]{1,0:T(8,128)} %get-tuple-element.126.k_ref, f32[1024,128]{1,0:T(8,128)} %get-tuple-element.125.v_ref, s32[2,1,512]{2,1,0:T(1,128)} %bitcast.66, ...), custom_call_target="tpu_custom_call" | custom-call | flops 1073741824 | bytes 8388608 | tf_op jit(solution)/shard_map/attend/pallas_call | solution.py:195
  147.0 10.4 %collective-permute-done.5 = bf16[128,2048]{0,1:T(8,128)(2,1)} collective-permute-done((bf16[128,2048]{0,1:T(8,128)(2,1)}, bf16[128,2048]{0,1:T(8,128)(2,1)}, u32[]{:S(2)}, u32[]{:S(2)}) %collective-permute-start.5) | collective-permute-done | bytes 524320 | tf_op jit(solution)/shard_map/ppermute | solution.py:233
  162.7 21.0 %collective-permute-done.6 = bf16[256,2048]{0,1:T(8,128)(2,1)S(1)} collective-permute-done((bf16[256,2048]{0,1:T(8,128)(2,1)S(1)}, bf16[256,2048]{0,1:T(8,128)(2,1)S(1)}, u32[]{:S(2)}, u32[]{:S(2)}) %collective-permute-start.6) | collective-permute-done | bytes 1048608 | tf_op jit(solution)/shard_map/ppermute | solution.py:233
  191.5 21.3 %collective-permute-done.9 = bf16[256,2048]{0,1:T(8,128)(2,1)S(1)} collective-permute-done((bf16[256,2048]{0,1:T(8,128)(2,1)S(1)}, bf16[256,2048]{0,1:T(8,128)(2,1)S(1)}, u32[]{:S(2)}, u32[]{:S(2)}) %collective-permute-start.9) | collective-permute-done | bytes 1048608 | tf_op jit(solution)/shard_map/ppermute | solution.py:233
  218.7 5.3 collective-permute-done.11
  230.8 23.3 %collective-permute-done.13 = bf16[256,2048]{0,1:T(8,128)(2,1)S(1)} collective-permute-done((bf16[256,2048]{0,1:T(8,128)(2,1)S(1)}, bf16[256,2048]{0,1:T(8,128)(2,1)S(1)}, u32[]{:S(2)}, u32[]{:S(2)}) %collective-permute-start.13) | collective-permute-done | bytes 1048608 | tf_op jit(solution)/shard_map/ppermute | solution.py:233
  259.7 9.1 %collective-permute-done.15 = bf16[128,2048]{0,1:T(8,128)(2,1)} collective-permute-done((bf16[128,2048]{0,1:T(8,128)(2,1)}, bf16[128,2048]{0,1:T(8,128)(2,1)}, u32[]{:S(2)}, u32[]{:S(2)}) %collective-permute-start.15) | collective-permute-done | bytes 524320 | tf_op jit(solution)/shard_map/ppermute | solution.py:233
  271.6 11.3 %fusion.5 = f32[1024,2048]{1,0:T(8,128)} fusion(bf16[1024,4096]{1,0:T(8,128)(2,1)} %all-gather.6.cloned.1.call-done, bf16[1024,2048]{0,1:T(8,128)(2,1)} %constant_dynamic-update-slice_fusion.10), kind=kOutput, calls=%fused_computation.35 | convolution fusion | flops 4294967296 | bytes 14680064 | tf_op jit(solution)/shard_map/dot_general | solution.py:51
  282.8 6.2 fusion.7
  289.1 7.6 %fusion.9 = f32[1024,2048]{1,0:T(8,128)S(1)} fusion(f32[1024,2048]{1,0:T(8,128)S(1)} %fusion.7, bf16[1024,4096]{1,0:T(8,128)(2,1)} %collective-permute-done.17, bf16[1024,2048]{0,1:T(8,128)(2,1)} %constant_dynamic-update-slice_fusion.10), kind=kOutput, calls=%fused_computation.39 | convolution fusion | flops 4297064448 | bytes 23068672 | tf_op jit(solution)/shard_map/dot_general | solution.py:51
  296.8 15.7 %multiply_convert_fusion.2 = (bf16[1024,2048]{1,0:T(8,128)(2,1)}, f32[1024,2048]{1,0:T(8,128)}) fusion(f32[1024,2048]{1,0:T(8,128)S(1)} %fusion.9, f32[1024,2048]{1,0:T(8,128)} %fusion.5, bf16[1024,4096]{1,0:T(8,128)(2,1)} %collective-permute-done.17, bf16[1024,2048]{0,1:T(8,128)(2,1)} %constant_dynamic-update-slice_fusion.10), kind=kOutput, calls=%fused_computation.4 | convolution fusion | flops 4309647360 | bytes 35651584 | tf_op jit(solution)/shard_map/dot_general | solution.py:51
  312.5 7.1 convolution_convert_fusion.1
  319.7 7.1 collective-permute-done.18
  326.9 6.5 add_convert_fusion.1
  335.3 10.6 %fusion.33 = f32[1024,2048]{1,0:T(8,128)} fusion(bf16[1024,2048]{1,0:T(8,128)(2,1)} %all-gather.8.cloned.1.call-done, bf16[1024,2048]{0,1:T(8,128)(2,1)} %constant_dynamic-update-slice_fusion.5), kind=kOutput, calls=%fused_computation.82 | convolution fusion | flops 4294967296 | bytes 14680064 | tf_op jit(solution)/shard_map/dot_general | solution.py:51
  347.9 15.5 %multiply_convert_fusion = (bf16[1024,2048]{1,0:T(8,128)(2,1)S(1)}, bf16[1024,2048]{1,0:T(8,128)(2,1)S(1)}) fusion(f32[1024,2048]{1,0:T(8,128)} %copy-done.47, f32[1024,2048]{1,0:T(8,128)} %get-tuple-element.162, f32[1024,2048]{1,0:T(8,128)} %fusion.33, bf16[1024,2048]{1,0:T(8,128)(2,1)} %copy-done.41, bf16[1024,2048]{0,1:T(8,128)(2,1)} %constant_dynamic-update-slice_fusion.5), kind=kOutput, calls=%fused_computation.1 | convolution fusion | flops 4324327424 | bytes 39845888 | tf_op jit(solution)/shard_map/dot_general | solution.py:51
  364.0 14.4 %convolution_convert_fusion = bf16[1024,4096]{1,0:T(8,128)(2,1)} fusion(bf16[1024,4096]{1,0:T(8,128)(2,1)S(1)} %constant_dynamic-update-slice_fusion.20, bf16[1024,2048]{0,1:T(8,128)(2,1)} %constant_dynamic-update-slice_fusion.10), kind=kOutput, calls=%fused_computation.7 | convolution fusion | flops 8594128896 | bytes 18874368 | tf_op jit(solution)/shard_map/dot_general | solution.py:39
  379.0 11.3 %convolution_convert_fusion.3 = bf16[1024,1024]{0,1:T(8,128)(2,1)S(1)} fusion(bf16[1024,4096]{1,0:T(8,128)(2,1)S(1)} %constant_dynamic-update-slice_fusion.20, bf16[1024,4096]{1,0:T(8,128)(2,1)} %all-gather.6.cloned.1.call-done), kind=kOutput, calls=%fused_computation.75 | convolution fusion | flops 8590983168 | bytes 18874368 | tf_op jit(solution)/shard_map/dot_general | solution.py:45
  390.2 11.3 %convolution_convert_fusion.2 = bf16[1024,1024]{0,1:T(8,128)(2,1)S(1)} fusion(bf16[1024,4096]{1,0:T(8,128)(2,1)S(1)} %constant_dynamic-update-slice_fusion.20, bf16[1024,4096]{1,0:T(8,128)(2,1)} %collective-permute-done.17), kind=kOutput, calls=%fused_computation.74 | convolution fusion | flops 8590983168 | bytes 18874368 | tf_op jit(solution)/shard_map/dot_general | solution.py:45
  407.1 14.5 %add_convert_fusion = bf16[1024,4096]{1,0:T(8,128)(2,1)} fusion(bf16[1024,4096]{1,0:T(8,128)(2,1)} %collective-permute-done.20, bf16[1024,4096]{1,0:T(8,128)(2,1)S(1)} %copy-done.19, bf16[1024,2048]{0,1:T(8,128)(2,1)} %constant_dynamic-update-slice_fusion.10), kind=kOutput, calls=%fused_computation | convolution fusion | flops 8602517504 | bytes 27262976 | tf_op jit(solution)/shard_map/dot_general | solution.py:39
  428.5 20.1 %collective-permute-done.22 = bf16[256,2048]{0,1:T(8,128)(2,1)} collective-permute-done((bf16[256,2048]{0,1:T(8,128)(2,1)}, bf16[256,2048]{0,1:T(8,128)(2,1)}, u32[]{:S(2)}, u32[]{:S(2)}) %collective-permute-start.22) | collective-permute-done | bytes 1048608 | tf_op jit(solution)/shard_map/ppermute | solution.py:233
  473.5 9.9 %collective-permute-done.25 = bf16[256,2048]{0,1:T(8,128)(2,1)S(1)} collective-permute-done((bf16[256,2048]{0,1:T(8,128)(2,1)S(1)}, bf16[256,2048]{0,1:T(8,128)(2,1)S(1)}, u32[]{:S(2)}, u32[]{:S(2)}) %collective-permute-start.25) | collective-permute-done | bytes 1048608 | tf_op jit(solution)/shard_map/ppermute | solution.py:233
  486.6 9.0 %collective-permute-done.27 = bf16[128,2048]{0,1:T(8,128)(2,1)S(1)} collective-permute-done((bf16[128,2048]{0,1:T(8,128)(2,1)S(1)}, bf16[128,2048]{0,1:T(8,128)(2,1)S(1)}, u32[]{:S(2)}, u32[]{:S(2)}) %collective-permute-start.27) | collective-permute-done | bytes 524320 | tf_op jit(solution)/shard_map/ppermute | solution.py:233
  504.5 23.2 %attend_back.1 = (bf16[1024,512]{1,0:T(8,128)(2,1)}, f32[1024,128]{1,0:T(8,128)}, bf16[1024,128]{1,0:T(8,128)(2,1)}) custom-call(bf16[1024,512]{1,0:T(8,128)(2,1)} %get-tuple-element.53.q_ref, bf16[1024,128]{1,0:T(8,128)(2,1)} %get-tuple-element.54.k_ref, bf16[1024,128]{1,0:T(8,128)(2,1)} %get-tuple-element.55.v_ref, ...), custom_call_target="tpu_custom_call" | custom-call | flops 2684354560 | bytes 8388608 | tf_op jit(solution)/shard_map/attend_back/pallas_call | solution.py:216
  561.3 9.1 %collective-permute-done.33 = bf16[128,2048]{0,1:T(8,128)(2,1)S(1)} collective-permute-done((bf16[128,2048]{0,1:T(8,128)(2,1)S(1)}, bf16[128,2048]{0,1:T(8,128)(2,1)S(1)}, u32[]{:S(2)}, u32[]{:S(2)}) %collective-permute-start.33) | collective-permute-done | bytes 524320 | tf_op jit(solution)/shard_map/ppermute | solution.py:233
  589.2 15.5 %collective-permute-done.34 = bf16[256,2048]{0,1:T(8,128)(2,1)} collective-permute-done((bf16[256,2048]{0,1:T(8,128)(2,1)}, bf16[256,2048]{0,1:T(8,128)(2,1)}, u32[]{:S(2)}, u32[]{:S(2)}) %collective-permute-start.34) | collective-permute-done | bytes 1048608 | tf_op jit(solution)/shard_map/ppermute | solution.py:233
  612.3 13.9 %collective-permute-done.30 = bf16[256,2048]{0,1:T(8,128)(2,1)} collective-permute-done((bf16[256,2048]{0,1:T(8,128)(2,1)}, bf16[256,2048]{0,1:T(8,128)(2,1)}, u32[]{:S(2)}, u32[]{:S(2)}) %collective-permute-start.30) | collective-permute-done | bytes 1048608 | tf_op jit(solution)/shard_map/ppermute | solution.py:233
  633.9 6.1 collective-permute-done.42
  652.6 96.6 %reduce-scatter.6.cloned.1.call-done = bf16[256,4096]{1,0:T(8,128)(2,1)} async-done(((bf16[1024,4096]{1,0:T(8,128)(2,1)}), bf16[256,4096]{1,0:T(8,128)(2,1)}) %reduce-scatter.6.cloned.1.call-update) | async-done | bytes 2097168 | tf_op jit(solution)/shard_map/reduce_scatter | solution.py:359
  (326 shorter events, 237.9 us)
Async XLA Ops:
  7.2 60.5 %all-gather.4.cloned.1.call-start = ((), (), s32[]{:S(2)}) async-start(), calls=%async_computation.3 | async-start | bytes 3276800 | tf_op jit(solution)/shard_map/all_gather | solution.py:323
  9.2 216.5 %all-gather.6.cloned.1.call-start = ((), (), s32[]{:S(2)}) async-start(), calls=%async_computation.4 | async-start | bytes 10485760 | tf_op jit(solution)/shard_map/all_gather | solution.py:323
  12.5 322.8 %all-gather.8.cloned.1.call-start = ((), (), s32[]{:S(2)}) async-start(), calls=%async_computation.5 | async-start | bytes 5242880 | tf_op jit(solution)/shard_map/all_gather | solution.py:323
  32.9 37.7 %collective-permute-start = (bf16[256,2048]{0,1:T(8,128)(2,1)}, bf16[256,2048]{0,1:T(8,128)(2,1)S(1)}, u32[]{:S(2)}, u32[]{:S(2)}) collective-permute-start(bf16[256,2048]{0,1:T(8,128)(2,1)} %get-tuple-element.98), channel_id=1, source_target_pairs={{0,1},{1,0},{2,3},{3,2},{4,5},{5,4},{6,7},{7,6},{8,9},{9,8},{10,11... | collective-permute-start | bytes 3145736 | tf_op jit(solution)/shard_map/ppermute | solution.py:233
  67.6 43.9 %collective-permute-start.4 = (bf16[1024,1280]{1,0:T(8,128)(2,1)}, bf16[1024,1280]{1,0:T(8,128)(2,1)}, u32[]{:S(2)}, u32[]{:S(2)}) collective-permute-start(bf16[1024,1280]{1,0:T(8,128)(2,1)} %all-gather.4.cloned.1.call-done), channel_id=1, source_target_pairs={{0,4},{4,0},{8,12},{12,8},{16,20},{20,16},{24,28},{28,24},{1,5},{5... | collective-permute-start | bytes 7864328 | tf_op jit(solution)/shard_map/ppermute | solution.py:233
  67.6 26.2 %collective-permute-start.1 = (bf16[256,2048]{0,1:T(8,128)(2,1)}, bf16[256,2048]{0,1:T(8,128)(2,1)S(1)}, u32[]{:S(2)}, u32[]{:S(2)}) collective-permute-start(bf16[256,2048]{0,1:T(8,128)(2,1)} %get-tuple-element.98), channel_id=1, source_target_pairs={{0,2},{1,3},{2,0},{3,1},{4,6},{5,7},{6,4},{7,5},{8,10},{9,11},{10,... | collective-permute-start | bytes 3145736 | tf_op jit(solution)/shard_map/ppermute | solution.py:233
  71.5 33.3 %collective-permute-start.2 = (bf16[128,2048]{0,1:T(8,128)(2,1)}, bf16[128,2048]{0,1:T(8,128)(2,1)}, u32[]{:S(2)}, u32[]{:S(2)}) collective-permute-start(bf16[128,2048]{0,1:T(8,128)(2,1)} %slice.108), channel_id=1, source_target_pairs={{0,2},{1,3},{2,0},{3,1},{4,6},{5,7},{6,4},{7,5},{8,10},{9,11},{10,... | collective-permute-start | bytes 1572872 | tf_op jit(solution)/shard_map/ppermute | solution.py:233
  160.5 23.2 %collective-permute-start.6 = (bf16[256,2048]{0,1:T(8,128)(2,1)S(1)}, bf16[256,2048]{0,1:T(8,128)(2,1)S(1)}, u32[]{:S(2)}, u32[]{:S(2)}) collective-permute-start(bf16[256,2048]{0,1:T(8,128)(2,1)S(1)} %pad_maximum_fusion.7), channel_id=1, source_target_pairs={{0,1},{1,0},{2,3},{3,2},{4,5},{5,4},{6,7},{7,6},{8,9},{9,8},{10,11... | collective-permute-start | bytes 3145736 | tf_op jit(solution)/shard_map/ppermute | solution.py:233
  162.1 23.0 %collective-permute-start.8 = (bf16[256,2048]{0,1:T(8,128)(2,1)S(1)}, bf16[256,2048]{0,1:T(8,128)(2,1)S(1)}, u32[]{:S(2)}, u32[]{:S(2)}) collective-permute-start(bf16[256,2048]{0,1:T(8,128)(2,1)S(1)} %pad_maximum_fusion.8), channel_id=1, source_target_pairs={{0,2},{1,3},{2,0},{3,1},{4,6},{5,7},{6,4},{7,5},{8,10},{9,11},{10,... | collective-permute-start | bytes 3145736 | tf_op jit(solution)/shard_map/ppermute | solution.py:233
  190.4 22.5 %collective-permute-start.9 = (bf16[256,2048]{0,1:T(8,128)(2,1)S(1)}, bf16[256,2048]{0,1:T(8,128)(2,1)S(1)}, u32[]{:S(2)}, u32[]{:S(2)}) collective-permute-start(bf16[256,2048]{0,1:T(8,128)(2,1)S(1)} %get-tuple-element.94), channel_id=1, source_target_pairs={{0,1},{1,0},{2,3},{3,2},{4,5},{5,4},{6,7},{7,6},{8,9},{9,8},{10,11... | collective-permute-start | bytes 3145736 | tf_op jit(solution)/shard_map/ppermute | solution.py:233
  190.9 23.1 %collective-permute-start.10 = (bf16[256,2048]{0,1:T(8,128)(2,1)S(1)}, bf16[256,2048]{0,1:T(8,128)(2,1)S(1)}, u32[]{:S(2)}, u32[]{:S(2)}) collective-permute-start(bf16[256,2048]{0,1:T(8,128)(2,1)S(1)} %get-tuple-element.94), channel_id=1, source_target_pairs={{0,2},{1,3},{2,0},{3,1},{4,6},{5,7},{6,4},{7,5},{8,10},{9,11},{10,... | collective-permute-start | bytes 3145736 | tf_op jit(solution)/shard_map/ppermute | solution.py:233
  225.8 63.3 %collective-permute-start.17 = (bf16[1024,4096]{1,0:T(8,128)(2,1)}, bf16[1024,4096]{1,0:T(8,128)(2,1)}, u32[]{:S(2)}, u32[]{:S(2)}) collective-permute-start(bf16[1024,4096]{1,0:T(8,128)(2,1)} %all-gather.6.cloned.1.call-done), channel_id=1, source_target_pairs={{0,4},{4,0},{8,12},{12,8},{16,20},{20,16},{24,28},{28,24},{1,5},{5... | collective-permute-start | bytes 25165832 | tf_op jit(solution)/shard_map/ppermute | solution.py:233
  228.6 25.6 %collective-permute-start.13 = (bf16[256,2048]{0,1:T(8,128)(2,1)S(1)}, bf16[256,2048]{0,1:T(8,128)(2,1)S(1)}, u32[]{:S(2)}, u32[]{:S(2)}) collective-permute-start(bf16[256,2048]{0,1:T(8,128)(2,1)S(1)} %get-tuple-element.133), channel_id=1, source_target_pairs={{0,1},{1,0},{2,3},{3,2},{4,5},{5,4},{6,7},{7,6},{8,9},{9,8},{10,11... | collective-permute-start | bytes 3145736 | tf_op jit(solution)/shard_map/ppermute | solution.py:233
  230.0 25.9 %collective-permute-start.14 = (bf16[256,2048]{0,1:T(8,128)(2,1)S(1)}, bf16[256,2048]{0,1:T(8,128)(2,1)S(1)}, u32[]{:S(2)}, u32[]{:S(2)}) collective-permute-start(bf16[256,2048]{0,1:T(8,128)(2,1)S(1)} %get-tuple-element.133), channel_id=1, source_target_pairs={{0,2},{1,3},{2,0},{3,1},{4,6},{5,7},{6,4},{7,5},{8,10},{9,11},{10,... | collective-permute-start | bytes 3145736 | tf_op jit(solution)/shard_map/ppermute | solution.py:233
  255.7 320.7 %reduce-scatter.8.cloned.1.call-start = ((), (), s32[]{:S(2)}) async-start(), calls=%async_computation.8 | async-start | bytes 5242880 | tf_op jit(solution)/shard_map/reduce_scatter | solution.py:359
  378.4 28.6 %collective-permute-start.20 = (bf16[1024,4096]{1,0:T(8,128)(2,1)}, bf16[1024,4096]{1,0:T(8,128)(2,1)}, u32[]{:S(2)}, u32[]{:S(2)}) collective-permute-start(bf16[1024,4096]{1,0:T(8,128)(2,1)} %convolution_convert_fusion), channel_id=1, source_target_pairs={{0,4},{4,0},{8,12},{12,8},{16,20},{20,16},{24,28},{28,24},{1,5},{5... | collective-permute-start | bytes 25165832 | tf_op jit(solution)/shard_map/ppermute | solution.py:233
  404.1 17.5 %collective-permute-start.21 = (bf16[128,2048]{0,1:T(8,128)(2,1)S(1)}, bf16[128,2048]{0,1:T(8,128)(2,1)}, u32[]{:S(2)}, u32[]{:S(2)}) collective-permute-start(bf16[128,2048]{0,1:T(8,128)(2,1)S(1)} %get-tuple-element.116), channel_id=1, source_target_pairs={{0,2},{1,3},{2,0},{3,1},{4,6},{5,7},{6,4},{7,5},{8,10},{9,11},{10,... | collective-permute-start | bytes 1572872 | tf_op jit(solution)/shard_map/ppermute | solution.py:233
  405.6 19.1 %collective-permute-start.23 = (bf16[128,2048]{0,1:T(8,128)(2,1)S(1)}, bf16[128,2048]{0,1:T(8,128)(2,1)}, u32[]{:S(2)}, u32[]{:S(2)}) collective-permute-start(bf16[128,2048]{0,1:T(8,128)(2,1)S(1)} %get-tuple-element.115), channel_id=1, source_target_pairs={{0,1},{1,0},{2,3},{3,2},{4,5},{5,4},{6,7},{7,6},{8,9},{9,8},{10,11... | collective-permute-start | bytes 1572872 | tf_op jit(solution)/shard_map/ppermute | solution.py:233
  423.8 24.8 %collective-permute-start.22 = (bf16[256,2048]{0,1:T(8,128)(2,1)}, bf16[256,2048]{0,1:T(8,128)(2,1)}, u32[]{:S(2)}, u32[]{:S(2)}) collective-permute-start(bf16[256,2048]{0,1:T(8,128)(2,1)} %pad_maximum_fusion.10), channel_id=1, source_target_pairs={{0,1},{1,0},{2,3},{3,2},{4,5},{5,4},{6,7},{7,6},{8,9},{9,8},{10,11... | collective-permute-start | bytes 3145736 | tf_op jit(solution)/shard_map/ppermute | solution.py:233
  427.0 25.1 %collective-permute-start.24 = (bf16[256,2048]{0,1:T(8,128)(2,1)}, bf16[256,2048]{0,1:T(8,128)(2,1)}, u32[]{:S(2)}, u32[]{:S(2)}) collective-permute-start(bf16[256,2048]{0,1:T(8,128)(2,1)} %pad_maximum_fusion.11), channel_id=1, source_target_pairs={{0,2},{1,3},{2,0},{3,1},{4,6},{5,7},{6,4},{7,5},{8,10},{9,11},{10,... | collective-permute-start | bytes 3145736 | tf_op jit(solution)/shard_map/ppermute | solution.py:233
  428.5 218.6 %reduce-scatter.4.cloned.1.call-start = ((), (), s32[]{:S(2)}) async-start(), calls=%async_computation.6 | async-start | bytes 3276800 | tf_op jit(solution)/shard_map/reduce_scatter | solution.py:359
  459.5 24.0 %collective-permute-start.25 = (bf16[256,2048]{0,1:T(8,128)(2,1)S(1)}, bf16[256,2048]{0,1:T(8,128)(2,1)S(1)}, u32[]{:S(2)}, u32[]{:S(2)}) collective-permute-start(bf16[256,2048]{0,1:T(8,128)(2,1)S(1)} %get-tuple-element.50), channel_id=1, source_target_pairs={{0,1},{1,0},{2,3},{3,2},{4,5},{5,4},{6,7},{7,6},{8,9},{9,8},{10,11... | collective-permute-start | bytes 3145736 | tf_op jit(solution)/shard_map/ppermute | solution.py:233
  460.1 25.6 %collective-permute-start.26 = (bf16[256,2048]{0,1:T(8,128)(2,1)S(1)}, bf16[256,2048]{0,1:T(8,128)(2,1)S(1)}, u32[]{:S(2)}, u32[]{:S(2)}) collective-permute-start(bf16[256,2048]{0,1:T(8,128)(2,1)S(1)} %get-tuple-element.50), channel_id=1, source_target_pairs={{0,2},{1,3},{2,0},{3,1},{4,6},{5,7},{6,4},{7,5},{8,10},{9,11},{10,... | collective-permute-start | bytes 3145736 | tf_op jit(solution)/shard_map/ppermute | solution.py:233
  553.0 196.2 %reduce-scatter.6.cloned.1.call-start = ((), (), s32[]{:S(2)}) async-start(), calls=%async_computation.7 | async-start | bytes 10485760 | tf_op jit(solution)/shard_map/reduce_scatter | solution.py:359
  555.5 14.9 %collective-permute-start.33 = (bf16[128,2048]{0,1:T(8,128)(2,1)S(1)}, bf16[128,2048]{0,1:T(8,128)(2,1)S(1)}, u32[]{:S(2)}, u32[]{:S(2)}) collective-permute-start(bf16[128,2048]{0,1:T(8,128)(2,1)S(1)} %get-tuple-element.104), channel_id=1, source_target_pairs={{0,2},{1,3},{2,0},{3,1},{4,6},{5,7},{6,4},{7,5},{8,10},{9,11},{10,... | collective-permute-start | bytes 1572872 | tf_op jit(solution)/shard_map/ppermute | solution.py:233
  558.6 23.1 %collective-permute-start.29 = (bf16[128,2048]{0,1:T(8,128)(2,1)}, bf16[128,2048]{0,1:T(8,128)(2,1)}, u32[]{:S(2)}, u32[]{:S(2)}) collective-permute-start(bf16[128,2048]{0,1:T(8,128)(2,1)} %get-tuple-element.110), channel_id=1, source_target_pairs={{0,2},{1,3},{2,0},{3,1},{4,6},{5,7},{6,4},{7,5},{8,10},{9,11},{10,... | collective-permute-start | bytes 1572872 | tf_op jit(solution)/shard_map/ppermute | solution.py:233
  559.7 22.6 %collective-permute-start.31 = (bf16[128,2048]{0,1:T(8,128)(2,1)}, bf16[128,2048]{0,1:T(8,128)(2,1)}, u32[]{:S(2)}, u32[]{:S(2)}) collective-permute-start(bf16[128,2048]{0,1:T(8,128)(2,1)} %get-tuple-element.109), channel_id=1, source_target_pairs={{0,1},{1,0},{2,3},{3,2},{4,5},{5,4},{6,7},{7,6},{8,9},{9,8},{10,11... | collective-permute-start | bytes 1572872 | tf_op jit(solution)/shard_map/ppermute | solution.py:233
  573.5 31.2 %collective-permute-start.34 = (bf16[256,2048]{0,1:T(8,128)(2,1)}, bf16[256,2048]{0,1:T(8,128)(2,1)}, u32[]{:S(2)}, u32[]{:S(2)}) collective-permute-start(bf16[256,2048]{0,1:T(8,128)(2,1)} %pad_maximum_fusion.15), channel_id=1, source_target_pairs={{0,1},{1,0},{2,3},{3,2},{4,5},{5,4},{6,7},{7,6},{8,9},{9,8},{10,11... | collective-permute-start | bytes 3145736 | tf_op jit(solution)/shard_map/ppermute | solution.py:233
  575.0 29.8 %collective-permute-start.36 = (bf16[256,2048]{0,1:T(8,128)(2,1)}, bf16[256,2048]{0,1:T(8,128)(2,1)}, u32[]{:S(2)}, u32[]{:S(2)}) collective-permute-start(bf16[256,2048]{0,1:T(8,128)(2,1)} %pad_maximum_fusion.16), channel_id=1, source_target_pairs={{0,2},{1,3},{2,0},{3,1},{4,6},{5,7},{6,4},{7,5},{8,10},{9,11},{10,... | collective-permute-start | bytes 3145736 | tf_op jit(solution)/shard_map/ppermute | solution.py:233
  586.2 40.1 %collective-permute-start.30 = (bf16[256,2048]{0,1:T(8,128)(2,1)}, bf16[256,2048]{0,1:T(8,128)(2,1)}, u32[]{:S(2)}, u32[]{:S(2)}) collective-permute-start(bf16[256,2048]{0,1:T(8,128)(2,1)} %pad_maximum_fusion.12), channel_id=1, source_target_pairs={{0,1},{1,0},{2,3},{3,2},{4,5},{5,4},{6,7},{7,6},{8,9},{9,8},{10,11... | collective-permute-start | bytes 3145736 | tf_op jit(solution)/shard_map/ppermute | solution.py:233
  587.7 38.6 %collective-permute-start.32 = (bf16[256,2048]{0,1:T(8,128)(2,1)}, bf16[256,2048]{0,1:T(8,128)(2,1)}, u32[]{:S(2)}, u32[]{:S(2)}) collective-permute-start(bf16[256,2048]{0,1:T(8,128)(2,1)} %pad_maximum_fusion.13), channel_id=1, source_target_pairs={{0,2},{1,3},{2,0},{3,1},{4,6},{5,7},{6,4},{7,5},{8,10},{9,11},{10,... | collective-permute-start | bytes 3145736 | tf_op jit(solution)/shard_map/ppermute | solution.py:233
  607.8 20.8 %collective-permute-start.39 = (f32[2,2048]{1,0:T(2,128)S(1)}, f32[2,2048]{1,0:T(2,128)S(1)}, u32[]{:S(2)}, u32[]{:S(2)}) collective-permute-start(f32[2,2048]{1,0:T(2,128)S(1)} %reshape.188), channel_id=1, source_target_pairs={{0,1},{1,0},{2,3},{3,2},{4,5},{5,4},{6,7},{7,6},{8,9},{9,8},{10,11... | collective-permute-start | bytes 49160 | tf_op jit(solution)/shard_map/ppermute | solution.py:233
  (70 other events, 1117.3 us)
Sparse Core Ops, SparseCore 0:
  10.1 57.4 all-gather.3
  69.8 148.3 all-gather.5
  255.9 79.3 all-gather.7
  428.6 74.1 reduce-scatter.7
  553.1 48.9 reduce-scatter.3
  604.3 144.8 reduce-scatter.5

commit v7 on v5

--- a/solution.py
+++ b/solution.py
@@ -5,6 +5,7 @@
 from jax import lax
 from jax.experimental import pallas as pl
 from jax.experimental.pallas import tpu as pltpu
+from jax.experimental.layout import Layout, with_layout_constraint
 from jax.sharding import PartitionSpec as P
 
 
@@ -272,24 +273,16 @@
     from_x = swap(part(me ^ 3, 0, half), "tensor", size, 1)
     from_y = swap(part(me ^ 3, half, half), "tensor", size, 2)
     wide = jnp.float32
-    to_y = jnp.concatenate(
-        [
-            (part(me ^ 2, 0, half).astype(wide) + from_x.astype(wide)).astype(jnp.bfloat16),
-            part(me ^ 2, half, half),
-        ]
-    )
-    to_x = jnp.concatenate(
-        [
-            part(me ^ 1, 0, half),
-            (part(me ^ 1, half, half).astype(wide) + from_y.astype(wide)).astype(jnp.bfloat16),
-        ]
-    )
+    near_low, near_high = part(me ^ 2, 0, half), part(me ^ 1, half, half)
+    if beside is not None:
+        near_low, near_high, _ = lax.optimization_barrier((near_low, near_high, beside))
+    near_low = (near_low.astype(wide) + from_x.astype(wide)).astype(jnp.bfloat16)
+    near_high = (near_high.astype(wide) + from_y.astype(wide)).astype(jnp.bfloat16)
+    to_y = jnp.concatenate([near_low, part(me ^ 2, half, half)])
+    to_x = jnp.concatenate([part(me ^ 1, 0, half), near_high])
     last_y = swap(to_y, "tensor", size, 2)
     last_x = swap(to_x, "tensor", size, 1)
-    own = part(me)
-    if beside is not None:
-        own, _ = lax.optimization_barrier((own, beside))
-    return own.astype(wide) + last_x.astype(wide) + last_y.astype(wide)
+    return part(me).astype(wide) + last_x.astype(wide) + last_y.astype(wide)
 
 
 def sum_all(array, axis, size):
@@ -312,10 +305,14 @@
     return pick(mine), pick(1 - mine)
 
 
-def pair_grad(parities, right_side, size):
-    mine, other = parities
-    from_pair = swap(contract_rows(other, right_side).astype(jnp.bfloat16), "dp", size, 1)
-    pair_sum = contract_rows(mine, right_side) + from_pair.astype(jnp.float32)
+def other_grad(parities, right_side):
+    return contract_rows(parities[1], right_side).astype(jnp.bfloat16)
+
+
+def pair_grad(parities, right_side, size, other=None):
+    other = other_grad(parities, right_side) if other is None else other
+    from_pair = swap(other, "dp", size, 1)
+    pair_sum = contract_rows(parities[0], right_side) + from_pair.astype(jnp.float32)
     return pair_sum.astype(jnp.bfloat16)
 
 
@@ -401,11 +398,12 @@
     grad_gate_up = jnp.concatenate(
         lax.optimization_barrier((grad_gate_pre, grad_up_pre)), axis=1
     )
+    other_gate_up = other_grad(two_parities, grad_gate_up)
+    other_gate_up, grad_gate_up = lax.optimization_barrier((other_gate_up, grad_gate_up))
     grad_normed_part = contract_cols(grad_gate_up, gate_up_full).astype(jnp.bfloat16)
     grad_normed_part, grad_gate_up = lax.optimization_barrier((grad_normed_part, grad_gate_up))
-    pair_gate_up = pair_grad(two_parities, grad_gate_up, dp)
+    pair_gate_up = pair_grad(two_parities, grad_gate_up, dp, other_gate_up)
     grad_normed_own = sum_rows(grad_normed_part, tp, beside=pair_gate_up)
-    grad_normed_own, pair_gate_up = lax.optimization_barrier((grad_normed_own, pair_gate_up))
     grad_gate, grad_up = jnp.split(sum_pairs(pair_gate_up, dp), 2, axis=1)
     grad_mlp_gain = jnp.sum(grad_normed_own * residual_own * scale_two_own, axis=0)
     grad_residual_own = cotangent.astype(jnp.float32) + norm_back(
@@ -436,6 +434,7 @@
         ],
         axis=1,
     )
+    pair_small = with_layout_constraint(pair_small, Layout(major_to_minor=(0, 1)))
     grad_query, grad_key, grad_value, grad_out = jnp.split(
         sum_pairs(pair_small, dp), splits + (narrow,), axis=1
     )

time: 736 us -> 730 us (level)
  matrix products: 161 us -> 152 us
  transfers between devices with their start and end apart: 47 -> 47, of which waited for: 30 -> 29; matrix products, arithmetic and copies ran while one was open for 33% -> 36% of each run, Pallas kernels for 6% -> 6%
where the time goes in v7:
time: 730 us; the launch traced here: 720 us
  waiting for transfers between devices  319 us (44%)
  matrix products  152 us (21%)
  local copies, waits for them, and re-layouts  97.2 us (13%)
  other arithmetic  49.2 us (7%)
  starting transfers between devices  45.9 us (6%)
  Pallas kernels  41.7 us (6%)
  between operations  15.2 us (2%)
    ppermute x41, waiting for transfers between devices, swap(): return lax.ppermute(array, axis, [(i, i ^ bit) for i in range(size)])  175 us
    reduce_scatter x3, waiting for transfers between devices, sum_pairs(): lax.psum_scatter(pair_sum, 'dp', scatter_dimension=0, tiled=True, axis_in...  100 us
    dot_general x5, matrix products, matmul(): return jnp.dot(left_side, right_side, preferred_element_type=jnp.float32)  63.8 us
    dot_general x4, matrix products, contract_cols(): lax.dot_general(left_side, right_side, (((1,), (1,)), ((), ())), preferre...  45.6 us
    ppermute x41, starting transfers between devices, swap(): return lax.ppermute(array, axis, [(i, i ^ bit) for i in range(size)])  45.3 us
    all_gather x3, waiting for transfers between devices, gather(): return lax.all_gather(weight, 'dp', axis=0, tiled=True)  42.8 us
    dot_general x8, matrix products, contract_rows(): lax.dot_general(left_side, right_side, (((0,), (0,)), ((), ())), preferre...  42.5 us
    pallas_call x1, Pallas kernels, attend_back(): pl.pallas_call(functools.partial(attend_back_kernel, groups), name='atten...  23.4 us
  transfers between devices with their start and end apart: 47, of which 29 were waited for; matrix products, arithmetic and copies ran while one was open for 36% of the time, Pallas kernels for 6%

profile of v7, /device:TPU:0, one launch (start us, length us, event | category | flops | bytes accessed | tf_op | source)
XLA Modules:
  0.0 719.6 jit_solution(11502703434084258183)
XLA Ops:
  23.9 16.1 %collective-permute-done = bf16[256,2048]{1,0:T(8,128)(2,1)} collective-permute-done((bf16[256,2048]{1,0:T(8,128)(2,1)S(1)}, bf16[256,2048]{1,0:T(8,128)(2,1)}, u32[]{:S(2)}, u32[]{:S(2)}) %collective-permute-start) | collective-permute-done | bytes 1048608 | tf_op jit(solution)/shard_map/ppermute | solution.py:234
  61.5 7.4 %all-gather.4.cloned.1.call-done = bf16[2048,1280]{1,0:T(8,128)(2,1)} async-done(((bf16[256,1280]{1,0:T(8,128)(2,1)}), bf16[2048,1280]{1,0:T(8,128)(2,1)}) %all-gather.4.cloned.1.call-update) | async-done | bytes 5242896 | tf_op jit(solution)/shard_map/all_gather | solution.py:350
  68.9 6.2 fusion.6
  77.8 18.3 %attend.1 = (bf16[1024,512]{1,0:T(8,128)(2,1)}, bf16[1024,128]{1,0:T(8,128)(2,1)}, bf16[1024,128]{1,0:T(8,128)(2,1)}, bf16[1024,512]{1,0:T(8,128)(2,1)}) custom-call(f32[1024,512]{1,0:T(8,128)} %split.44.q_ref, f32[1024,128]{1,0:T(8,128)} %get-tuple-element.112.k_ref, f32[1024,128]{1,0:T(8,128)} %get-tuple-element.111.v_ref, s32[2,1,512]{2,1,0:T(1,128)} %bitcast.60, ...), custom_call_target="tpu_custom_call" | custom-call | flops 1073741824 | bytes 8388608 | tf_op jit(solution)/shard_map/attend/pallas_call | solution.py:196
  96.1 4.4 convolution_convert_fusion.3
  107.2 9.7 %collective-permute-done.4 = bf16[128,2048]{1,0:T(8,128)(2,1)} collective-permute-done((bf16[128,2048]{1,0:T(8,128)(2,1)}, bf16[128,2048]{1,0:T(8,128)(2,1)}, u32[]{:S(2)}, u32[]{:S(2)}) %collective-permute-start.4) | collective-permute-done | bytes 524320 | tf_op jit(solution)/shard_map/ppermute | solution.py:234
  126.3 14.5 %collective-permute-done.8 = bf16[256,2048]{0,1:T(8,128)(2,1)} collective-permute-done((bf16[256,2048]{0,1:T(8,128)(2,1)S(1)}, bf16[256,2048]{0,1:T(8,128)(2,1)}, u32[]{:S(2)}, u32[]{:S(2)}) %collective-permute-start.8) | collective-permute-done | bytes 1048608 | tf_op jit(solution)/shard_map/ppermute | solution.py:234
  146.3 17.0 %collective-permute-done.5 = bf16[256,2048]{1,0:T(8,128)(2,1)} collective-permute-done((bf16[256,2048]{1,0:T(8,128)(2,1)}, bf16[256,2048]{1,0:T(8,128)(2,1)}, u32[]{:S(2)}, u32[]{:S(2)}) %collective-permute-start.5) | collective-permute-done | bytes 1048608 | tf_op jit(solution)/shard_map/ppermute | solution.py:234
  176.6 5.8 constant_dynamic-slice_fusion.18
  182.9 13.1 %collective-permute-done.12 = bf16[256,2048]{1,0:T(8,128)(2,1)S(1)} collective-permute-done((bf16[256,2048]{1,0:T(8,128)(2,1)S(1)}, bf16[256,2048]{1,0:T(8,128)(2,1)S(1)}, u32[]{:S(2)}, u32[]{:S(2)}) %collective-permute-start.12) | collective-permute-done | bytes 1048608 | tf_op jit(solution)/shard_map/ppermute | solution.py:234
  216.6 4.4 all-gather.6.cloned.1.call-done
  221.0 13.1 %fusion.2 = f32[1024,2048]{1,0:T(8,128)S(1)} fusion(bf16[1024,2048]{0,1:T(8,128)(2,1)} %constant_dynamic-update-slice_fusion.5, bf16[2048,4096]{1,0:T(8,128)(2,1)} %all-gather.6.cloned.1.call-done), kind=kOutput, calls=%fused_computation.3 | convolution fusion | flops 8589934592 | bytes 20971520 | tf_op jit(solution)/shard_map/dot_general | solution.py:52
  234.1 18.9 %multiply_convert_fusion.2 = (bf16[1024,2048]{1,0:T(8,128)(2,1)S(1)}, f32[1024,2048]{1,0:T(8,128)}) fusion(f32[1024,2048]{1,0:T(8,128)S(1)} %fusion.2, bf16[1024,2048]{0,1:T(8,128)(2,1)} %constant_dynamic-update-slice_fusion.5, bf16[2048,4096]{1,0:T(8,128)(2,1)} %all-gather.6.cloned.1.call-done), kind=kOutput, calls=%fused_computation.8 | convolution fusion | flops 8602517504 | bytes 33554432 | tf_op jit(solution)/shard_map/dot_general | solution.py:52
  253.0 5.1 convolution_convert_fusion.5
  258.6 4.3 constant_dynamic-slice_fusion.16
  265.8 6.0 add_convert_fusion.1
  271.8 31.0 %all-gather.8.cloned.1.call-done = bf16[2048,2048]{1,0:T(8,128)(2,1)} async-done(((bf16[256,2048]{1,0:T(8,128)(2,1)}), bf16[2048,2048]{1,0:T(8,128)(2,1)}) %all-gather.8.cloned.1.call-update) | async-done | bytes 8388624 | tf_op jit(solution)/shard_map/all_gather | solution.py:350
  302.9 19.3 %multiply_convert_fusion = (bf16[1024,2048]{1,0:T(8,128)(2,1)S(1)}, bf16[1024,2048]{1,0:T(8,128)(2,1)S(1)}) fusion(f32[1024,2048]{1,0:T(8,128)} %copy-done.42, f32[1024,2048]{1,0:T(8,128)} %get-tuple-element.128, bf16[1024,2048]{0,1:T(8,128)(2,1)} %copy-done.4, bf16[2048,2048]{1,0:T(8,128)(2,1)} %all-gather.8.cloned.1.call-done), kind=kOutput, calls=%fused_computation.5 | convolution fusion | flops 8617197568 | bytes 37748736 | tf_op jit(solution)/shard_map/dot_general | solution.py:52
  324.1 11.0 %convolution_convert_fusion = bf16[1024,4096]{1,0:T(8,128)(2,1)} fusion(bf16[1024,1024]{0,1:T(8,128)(2,1)S(1)} %bitcast.51, bf16[1024,4096]{1,0:T(8,128)(2,1)S(1)} %constant_dynamic-update-slice_fusion.20), kind=kOutput, calls=%fused_computation.11 | convolution fusion | flops 8594128896 | bytes 18874368 | tf_op jit(solution)/shard_map/dot_general | solution.py:40
  335.3 20.3 %convolution_convert_fusion.1 = bf16[1024,2048]{1,0:T(8,128)(2,1)S(1)} fusion(bf16[1024,4096]{1,0:T(8,128)(2,1)S(1)} %constant_dynamic-update-slice_fusion.20, bf16[2048,4096]{1,0:T(8,128)(2,1)} %all-gather.6.cloned.1.call-done), kind=kOutput, calls=%fused_computation.18 | convolution fusion | flops 17181966336 | bytes 29360128 | tf_op jit(solution)/shard_map/dot_general | solution.py:46
  361.3 14.2 %add_convert_fusion = bf16[1024,4096]{1,0:T(8,128)(2,1)} fusion(bf16[1024,4096]{1,0:T(8,128)(2,1)S(1)} %collective-permute-done.17, bf16[1024,1024]{0,1:T(8,128)(2,1)S(1)} %bitcast.50, bf16[1024,4096]{1,0:T(8,128)(2,1)} %copy-done.22), kind=kOutput, calls=%fused_computation | convolution fusion | flops 8602517504 | bytes 27262976 | tf_op jit(solution)/shard_map/dot_general | solution.py:40
  382.6 20.3 %collective-permute-done.19 = bf16[256,2048]{1,0:T(8,128)(2,1)S(1)} collective-permute-done((bf16[256,2048]{1,0:T(8,128)(2,1)}, bf16[256,2048]{1,0:T(8,128)(2,1)S(1)}, u32[]{:S(2)}, u32[]{:S(2)}) %collective-permute-start.19) | collective-permute-done | bytes 1048608 | tf_op jit(solution)/shard_map/ppermute | solution.py:234
  409.3 4.2 fusion.24
  417.2 13.9 %convolution_convert_fusion.2 = bf16[1024,2048]{1,0:T(8,128)(2,1)} fusion(bf16[1024,2048]{1,0:T(8,128)(2,1)} %copy-done.43, bf16[2048,2048]{1,0:T(8,128)(2,1)} %all-gather.8.cloned.1.call-done), kind=kOutput, calls=%fused_computation.19 | convolution fusion | flops 8592031744 | bytes 16777216 | tf_op jit(solution)/shard_map/dot_general | solution.py:46
  431.1 7.9 %collective-permute-done.22 = bf16[256,2048]{1,0:T(8,128)(2,1)S(1)} collective-permute-done((bf16[256,2048]{1,0:T(8,128)(2,1)}, bf16[256,2048]{1,0:T(8,128)(2,1)S(1)}, u32[]{:S(2)}, u32[]{:S(2)}) %collective-permute-start.22) | collective-permute-done | bytes 1048608 | tf_op jit(solution)/shard_map/ppermute | solution.py:234
  458.0 6.2 multiply_convert_fusion.3.grad_ref
  464.2 23.4 %attend_back.1 = (bf16[1024,512]{1,0:T(8,128)(2,1)}, f32[1024,128]{1,0:T(8,128)}, bf16[1024,128]{1,0:T(8,128)(2,1)}) custom-call(bf16[1024,512]{1,0:T(8,128)(2,1)} %get-tuple-element.55.q_ref, bf16[1024,128]{1,0:T(8,128)(2,1)} %get-tuple-element.56.k_ref, bf16[1024,128]{1,0:T(8,128)(2,1)} %get-tuple-element.57.v_ref, ...), custom_call_target="tpu_custom_call" | custom-call | flops 2684354560 | bytes 8388608 | tf_op jit(solution)/shard_map/attend_back/pallas_call | solution.py:217
  490.3 7.0 convolution_convert_fusion.4
  515.5 12.1 %collective-permute-done.30 = bf16[128,2048]{1,0:T(8,128)(2,1)S(1)} collective-permute-done((bf16[128,2048]{1,0:T(8,128)(2,1)S(1)}, bf16[128,2048]{1,0:T(8,128)(2,1)S(1)}, u32[]{:S(2)}, u32[]{:S(2)}) %collective-permute-start.30) | collective-permute-done | bytes 524320 | tf_op jit(solution)/shard_map/ppermute | solution.py:234
  540.9 27.9 %collective-permute-done.26 = bf16[128,2048]{1,0:T(8,128)(2,1)} collective-permute-done((bf16[128,2048]{1,0:T(8,128)(2,1)}, bf16[128,2048]{1,0:T(8,128)(2,1)}, u32[]{:S(2)}, u32[]{:S(2)}) %collective-permute-start.26) | collective-permute-done | bytes 524320 | tf_op jit(solution)/shard_map/ppermute | solution.py:234
  589.1 10.2 %collective-permute-done.27 = bf16[256,2048]{1,0:T(8,128)(2,1)S(1)} collective-permute-done((bf16[256,2048]{1,0:T(8,128)(2,1)S(1)}, bf16[256,2048]{1,0:T(8,128)(2,1)S(1)}, u32[]{:S(2)}, u32[]{:S(2)}) %collective-permute-start.27) | collective-permute-done | bytes 1048608 | tf_op jit(solution)/shard_map/ppermute | solution.py:234
  608.3 100.1 %reduce-scatter.6.cloned.1.call-done = bf16[256,4096]{1,0:T(8,128)(2,1)} async-done(((bf16[1024,4096]{1,0:T(8,128)(2,1)}), bf16[256,4096]{1,0:T(8,128)(2,1)}) %reduce-scatter.6.cloned.1.call-update) | async-done | bytes 2097168 | tf_op jit(solution)/shard_map/reduce_scatter | solution.py:321
  (284 shorter events, 210.9 us)
Async XLA Ops:
  7.2 61.8 %all-gather.4.cloned.1.call-start = ((), (), s32[]{:S(2)}) async-start(), calls=%async_computation.3 | async-start | bytes 5898240 | tf_op jit(solution)/shard_map/all_gather | solution.py:350
  9.3 211.7 %all-gather.6.cloned.1.call-start = ((), (), s32[]{:S(2)}) async-start(), calls=%async_computation.4 | async-start | bytes 18874368 | tf_op jit(solution)/shard_map/all_gather | solution.py:350
  12.5 290.4 %all-gather.8.cloned.1.call-start = ((), (), s32[]{:S(2)}) async-start(), calls=%async_computation.5 | async-start | bytes 9437184 | tf_op jit(solution)/shard_map/all_gather | solution.py:350
  13.7 26.3 %collective-permute-start = (bf16[256,2048]{1,0:T(8,128)(2,1)S(1)}, bf16[256,2048]{1,0:T(8,128)(2,1)}, u32[]{:S(2)}, u32[]{:S(2)}) collective-permute-start(bf16[256,2048]{1,0:T(8,128)(2,1)S(1)} %fusion.10), channel_id=1, source_target_pairs={{0,1},{1,0},{2,3},{3,2},{4,5},{5,4},{6,7},{7,6},{8,9},{9,8},{10,11... | collective-permute-start | bytes 3145736 | tf_op jit(solution)/shard_map/ppermute | solution.py:234
  16.8 26.9 %collective-permute-start.1 = (bf16[256,2048]{1,0:T(8,128)(2,1)S(1)}, bf16[256,2048]{1,0:T(8,128)(2,1)}, u32[]{:S(2)}, u32[]{:S(2)}) collective-permute-start(bf16[256,2048]{1,0:T(8,128)(2,1)S(1)} %fusion.10), channel_id=1, source_target_pairs={{0,2},{1,3},{2,0},{3,1},{4,6},{5,7},{6,4},{7,5},{8,10},{9,11},{10,... | collective-permute-start | bytes 3145736 | tf_op jit(solution)/shard_map/ppermute | solution.py:234
  101.8 15.1 %collective-permute-start.4 = (bf16[128,2048]{1,0:T(8,128)(2,1)}, bf16[128,2048]{1,0:T(8,128)(2,1)}, u32[]{:S(2)}, u32[]{:S(2)}) collective-permute-start(bf16[128,2048]{1,0:T(8,128)(2,1)} %get-tuple-element.108), channel_id=1, source_target_pairs={{0,2},{1,3},{2,0},{3,1},{4,6},{5,7},{6,4},{7,5},{8,10},{9,11},{10,... | collective-permute-start | bytes 1572872 | tf_op jit(solution)/shard_map/ppermute | solution.py:234
  103.2 15.1 %collective-permute-start.6 = (bf16[128,2048]{1,0:T(8,128)(2,1)}, bf16[128,2048]{1,0:T(8,128)(2,1)}, u32[]{:S(2)}, u32[]{:S(2)}) collective-permute-start(bf16[128,2048]{1,0:T(8,128)(2,1)} %get-tuple-element.107), channel_id=1, source_target_pairs={{0,1},{1,0},{2,3},{3,2},{4,5},{5,4},{6,7},{7,6},{8,9},{9,8},{10,11... | collective-permute-start | bytes 1572872 | tf_op jit(solution)/shard_map/ppermute | solution.py:234
  105.2 35.6 %collective-permute-start.8 = (bf16[256,2048]{0,1:T(8,128)(2,1)S(1)}, bf16[256,2048]{0,1:T(8,128)(2,1)}, u32[]{:S(2)}, u32[]{:S(2)}) collective-permute-start(bf16[256,2048]{0,1:T(8,128)(2,1)S(1)} %copy.35), channel_id=1, source_target_pairs={{0,1},{1,0},{2,3},{3,2},{4,5},{5,4},{6,7},{7,6},{8,9},{9,8},{10,11... | collective-permute-start | bytes 3145736 | tf_op jit(solution)/shard_map/ppermute | solution.py:234
  105.8 37.5 %collective-permute-start.9 = (bf16[256,2048]{0,1:T(8,128)(2,1)S(1)}, bf16[256,2048]{0,1:T(8,128)(2,1)S(1)}, u32[]{:S(2)}, u32[]{:S(2)}) collective-permute-start(bf16[256,2048]{0,1:T(8,128)(2,1)S(1)} %copy.35), channel_id=1, source_target_pairs={{0,2},{1,3},{2,0},{3,1},{4,6},{5,7},{6,4},{7,5},{8,10},{9,11},{10,... | collective-permute-start | bytes 3145736 | tf_op jit(solution)/shard_map/ppermute | solution.py:234
  121.5 41.8 %collective-permute-start.5 = (bf16[256,2048]{1,0:T(8,128)(2,1)}, bf16[256,2048]{1,0:T(8,128)(2,1)}, u32[]{:S(2)}, u32[]{:S(2)}) collective-permute-start(bf16[256,2048]{1,0:T(8,128)(2,1)} %pad_maximum_fusion.3), channel_id=1, source_target_pairs={{0,1},{1,0},{2,3},{3,2},{4,5},{5,4},{6,7},{7,6},{8,9},{9,8},{10,11... | collective-permute-start | bytes 3145736 | tf_op jit(solution)/shard_map/ppermute | solution.py:234
  124.0 39.3 %collective-permute-start.7 = (bf16[256,2048]{1,0:T(8,128)(2,1)}, bf16[256,2048]{1,0:T(8,128)(2,1)}, u32[]{:S(2)}, u32[]{:S(2)}) collective-permute-start(bf16[256,2048]{1,0:T(8,128)(2,1)} %pad_maximum_fusion.4), channel_id=1, source_target_pairs={{0,2},{1,3},{2,0},{3,1},{4,6},{5,7},{6,4},{7,5},{8,10},{9,11},{10,... | collective-permute-start | bytes 3145736 | tf_op jit(solution)/shard_map/ppermute | solution.py:234
  125.4 412.6 %reduce-scatter.8.cloned.1.call-start = ((), (), s32[]{:S(2)}) async-start(), calls=%async_computation.8 | async-start | bytes 5242880 | tf_op jit(solution)/shard_map/reduce_scatter | solution.py:321
  141.9 31.1 %collective-permute-start.10 = (bf16[128,2048]{0,1:T(8,128)(2,1)S(1)}, bf16[128,2048]{0,1:T(8,128)(2,1)S(1)}, u32[]{:S(2)}, u32[]{:S(2)}) collective-permute-start(bf16[128,2048]{0,1:T(8,128)(2,1)S(1)} %slice.52), channel_id=1, source_target_pairs={{0,2},{1,3},{2,0},{3,1},{4,6},{5,7},{6,4},{7,5},{8,10},{9,11},{10,... | collective-permute-start | bytes 1572872 | tf_op jit(solution)/shard_map/ppermute | solution.py:234
  143.4 31.1 %collective-permute-start.11 = (bf16[128,2048]{0,1:T(8,128)(2,1)S(1)}, bf16[128,2048]{0,1:T(8,128)(2,1)S(1)}, u32[]{:S(2)}, u32[]{:S(2)}) collective-permute-start(bf16[128,2048]{0,1:T(8,128)(2,1)S(1)} %slice.53), channel_id=1, source_target_pairs={{0,1},{1,0},{2,3},{3,2},{4,5},{5,4},{6,7},{7,6},{8,9},{9,8},{10,11... | collective-permute-start | bytes 1572872 | tf_op jit(solution)/shard_map/ppermute | solution.py:234
  166.8 29.2 %collective-permute-start.12 = (bf16[256,2048]{1,0:T(8,128)(2,1)S(1)}, bf16[256,2048]{1,0:T(8,128)(2,1)S(1)}, u32[]{:S(2)}, u32[]{:S(2)}) collective-permute-start(bf16[256,2048]{1,0:T(8,128)(2,1)S(1)} %multiply_convert_fusion.4), channel_id=1, source_target_pairs={{0,1},{1,0},{2,3},{3,2},{4,5},{5,4},{6,7},{7,6},{8,9},{9,8},{10,11... | collective-permute-start | bytes 3145736 | tf_op jit(solution)/shard_map/ppermute | solution.py:234
  168.3 30.0 %collective-permute-start.13 = (bf16[256,2048]{1,0:T(8,128)(2,1)S(1)}, bf16[256,2048]{1,0:T(8,128)(2,1)}, u32[]{:S(2)}, u32[]{:S(2)}) collective-permute-start(bf16[256,2048]{1,0:T(8,128)(2,1)S(1)} %multiply_convert_fusion.4), channel_id=1, source_target_pairs={{0,2},{1,3},{2,0},{3,1},{4,6},{5,7},{6,4},{7,5},{8,10},{9,11},{10,... | collective-permute-start | bytes 3145736 | tf_op jit(solution)/shard_map/ppermute | solution.py:234
  335.1 26.2 %collective-permute-start.17 = (bf16[1024,4096]{1,0:T(8,128)(2,1)}, bf16[1024,4096]{1,0:T(8,128)(2,1)S(1)}, u32[]{:S(2)}, u32[]{:S(2)}) collective-permute-start(bf16[1024,4096]{1,0:T(8,128)(2,1)} %convolution_convert_fusion), channel_id=1, source_target_pairs={{0,4},{4,0},{8,12},{12,8},{16,20},{20,16},{24,28},{28,24},{1,5},{5... | collective-permute-start | bytes 25165832 | tf_op jit(solution)/shard_map/ppermute | solution.py:234
  358.3 17.2 %collective-permute-start.18 = (bf16[128,2048]{1,0:T(8,128)(2,1)}, bf16[128,2048]{1,0:T(8,128)(2,1)}, u32[]{:S(2)}, u32[]{:S(2)}) collective-permute-start(bf16[128,2048]{1,0:T(8,128)(2,1)} %get-tuple-element.96), channel_id=1, source_target_pairs={{0,2},{1,3},{2,0},{3,1},{4,6},{5,7},{6,4},{7,5},{8,10},{9,11},{10,... | collective-permute-start | bytes 1572872 | tf_op jit(solution)/shard_map/ppermute | solution.py:234
  359.8 18.6 %collective-permute-start.20 = (bf16[128,2048]{1,0:T(8,128)(2,1)}, bf16[128,2048]{1,0:T(8,128)(2,1)}, u32[]{:S(2)}, u32[]{:S(2)}) collective-permute-start(bf16[128,2048]{1,0:T(8,128)(2,1)} %get-tuple-element.95), channel_id=1, source_target_pairs={{0,1},{1,0},{2,3},{3,2},{4,5},{5,4},{6,7},{7,6},{8,9},{9,8},{10,11... | collective-permute-start | bytes 1572872 | tf_op jit(solution)/shard_map/ppermute | solution.py:234
  377.9 25.0 %collective-permute-start.19 = (bf16[256,2048]{1,0:T(8,128)(2,1)}, bf16[256,2048]{1,0:T(8,128)(2,1)S(1)}, u32[]{:S(2)}, u32[]{:S(2)}) collective-permute-start(bf16[256,2048]{1,0:T(8,128)(2,1)} %pad_maximum_fusion.5), channel_id=1, source_target_pairs={{0,1},{1,0},{2,3},{3,2},{4,5},{5,4},{6,7},{7,6},{8,9},{9,8},{10,11... | collective-permute-start | bytes 3145736 | tf_op jit(solution)/shard_map/ppermute | solution.py:234
  381.9 24.8 %collective-permute-start.21 = (bf16[256,2048]{1,0:T(8,128)(2,1)}, bf16[256,2048]{1,0:T(8,128)(2,1)}, u32[]{:S(2)}, u32[]{:S(2)}) collective-permute-start(bf16[256,2048]{1,0:T(8,128)(2,1)} %pad_maximum_fusion.6), channel_id=1, source_target_pairs={{0,2},{1,3},{2,0},{3,1},{4,6},{5,7},{6,4},{7,5},{8,10},{9,11},{10,... | collective-permute-start | bytes 3145736 | tf_op jit(solution)/shard_map/ppermute | solution.py:234
  382.5 222.1 %reduce-scatter.4.cloned.1.call-start = ((), (), s32[]{:S(2)}) async-start(), calls=%async_computation.6 | async-start | bytes 3276800 | tf_op jit(solution)/shard_map/reduce_scatter | solution.py:321
  415.1 23.9 %collective-permute-start.22 = (bf16[256,2048]{1,0:T(8,128)(2,1)}, bf16[256,2048]{1,0:T(8,128)(2,1)S(1)}, u32[]{:S(2)}, u32[]{:S(2)}) collective-permute-start(bf16[256,2048]{1,0:T(8,128)(2,1)} %get-tuple-element.52), channel_id=1, source_target_pairs={{0,1},{1,0},{2,3},{3,2},{4,5},{5,4},{6,7},{7,6},{8,9},{9,8},{10,11... | collective-permute-start | bytes 3145736 | tf_op jit(solution)/shard_map/ppermute | solution.py:234
  416.7 23.8 %collective-permute-start.23 = (bf16[256,2048]{1,0:T(8,128)(2,1)}, bf16[256,2048]{1,0:T(8,128)(2,1)S(1)}, u32[]{:S(2)}, u32[]{:S(2)}) collective-permute-start(bf16[256,2048]{1,0:T(8,128)(2,1)} %get-tuple-element.52), channel_id=1, source_target_pairs={{0,2},{1,3},{2,0},{3,1},{4,6},{5,7},{6,4},{7,5},{8,10},{9,11},{10,... | collective-permute-start | bytes 3145736 | tf_op jit(solution)/shard_map/ppermute | solution.py:234
  511.2 197.3 %reduce-scatter.6.cloned.1.call-start = ((), (), s32[]{:S(2)}) async-start(), calls=%async_computation.7 | async-start | bytes 10485760 | tf_op jit(solution)/shard_map/reduce_scatter | solution.py:321
  531.5 39.6 %collective-permute-start.31 = (bf16[256,2048]{1,0:T(8,128)(2,1)}, bf16[256,2048]{1,0:T(8,128)(2,1)}, u32[]{:S(2)}, u32[]{:S(2)}) collective-permute-start(bf16[256,2048]{1,0:T(8,128)(2,1)} %pad_maximum_fusion.9), channel_id=1, source_target_pairs={{0,1},{1,0},{2,3},{3,2},{4,5},{5,4},{6,7},{7,6},{8,9},{9,8},{10,11... | collective-permute-start | bytes 3145736 | tf_op jit(solution)/shard_map/ppermute | solution.py:234
  533.2 38.0 %collective-permute-start.33 = (bf16[256,2048]{1,0:T(8,128)(2,1)}, bf16[256,2048]{1,0:T(8,128)(2,1)}, u32[]{:S(2)}, u32[]{:S(2)}) collective-permute-start(bf16[256,2048]{1,0:T(8,128)(2,1)} %pad_maximum_fusion.10), channel_id=1, source_target_pairs={{0,2},{1,3},{2,0},{3,1},{4,6},{5,7},{6,4},{7,5},{8,10},{9,11},{10,... | collective-permute-start | bytes 3145736 | tf_op jit(solution)/shard_map/ppermute | solution.py:234
  535.1 33.7 %collective-permute-start.26 = (bf16[128,2048]{1,0:T(8,128)(2,1)}, bf16[128,2048]{1,0:T(8,128)(2,1)}, u32[]{:S(2)}, u32[]{:S(2)}) collective-permute-start(bf16[128,2048]{1,0:T(8,128)(2,1)} %get-tuple-element.90), channel_id=1, source_target_pairs={{0,2},{1,3},{2,0},{3,1},{4,6},{5,7},{6,4},{7,5},{8,10},{9,11},{10,... | collective-permute-start | bytes 1572872 | tf_op jit(solution)/shard_map/ppermute | solution.py:234
  536.6 32.3 %collective-permute-start.28 = (bf16[128,2048]{1,0:T(8,128)(2,1)}, bf16[128,2048]{1,0:T(8,128)(2,1)}, u32[]{:S(2)}, u32[]{:S(2)}) collective-permute-start(bf16[128,2048]{1,0:T(8,128)(2,1)} %get-tuple-element.89), channel_id=1, source_target_pairs={{0,1},{1,0},{2,3},{3,2},{4,5},{5,4},{6,7},{7,6},{8,9},{9,8},{10,11... | collective-permute-start | bytes 1572872 | tf_op jit(solution)/shard_map/ppermute | solution.py:234
  576.1 23.3 %collective-permute-start.27 = (bf16[256,2048]{1,0:T(8,128)(2,1)S(1)}, bf16[256,2048]{1,0:T(8,128)(2,1)S(1)}, u32[]{:S(2)}, u32[]{:S(2)}) collective-permute-start(bf16[256,2048]{1,0:T(8,128)(2,1)S(1)} %pad_maximum_fusion.7), channel_id=1, source_target_pairs={{0,1},{1,0},{2,3},{3,2},{4,5},{5,4},{6,7},{7,6},{8,9},{9,8},{10,11... | collective-permute-start | bytes 3145736 | tf_op jit(solution)/shard_map/ppermute | solution.py:234
  578.9 22.3 %collective-permute-start.29 = (bf16[256,2048]{1,0:T(8,128)(2,1)S(1)}, bf16[256,2048]{1,0:T(8,128)(2,1)S(1)}, u32[]{:S(2)}, u32[]{:S(2)}) collective-permute-start(bf16[256,2048]{1,0:T(8,128)(2,1)S(1)} %pad_maximum_fusion.8), channel_id=1, source_target_pairs={{0,2},{1,3},{2,0},{3,1},{4,6},{5,7},{6,4},{7,5},{8,10},{9,11},{10,... | collective-permute-start | bytes 3145736 | tf_op jit(solution)/shard_map/ppermute | solution.py:234
  588.1 15.9 %collective-permute-start.40 = (f32[2,2048]{1,0:T(2,128)S(1)}, f32[2,2048]{1,0:T(2,128)S(1)}, u32[]{:S(2)}, u32[]{:S(2)}) collective-permute-start(f32[2,2048]{1,0:T(2,128)S(1)} %add.276), channel_id=1, source_target_pairs={{0,16},{4,20},{8,24},{12,28},{16,0},{20,4},{24,8},{28,12},{1,17},{... | collective-permute-start | bytes 49160 | tf_op jit(solution)/shard_map/ppermute | solution.py:234
  (60 other events, 720.7 us)
Sparse Core Ops, SparseCore 0:
  10.2 58.6 all-gather.3
  71.1 149.8 all-gather.5
  222.6 80.2 all-gather.7
  382.6 75.2 reduce-scatter.7
  511.3 49.9 reduce-scatter.3
  563.5 144.8 reduce-scatter.5
